TPU v7x, 32 devices: a whole 2x2x4 slice. The times are simulated.
32 devices in a mesh: row: 4 (over y, x), col: 8 (over z, core).
Axes of the slice: x: 2, y: 2, z: 4, core: 2. Of those that a mesh axis runs over, the one named last changes fastest.
Arguments:
- iterates: float32 [11, 1024], P(None, ('col', 'row')), may hold values from -6 to 6
- residuals: float32 [11, 1024], P(None, ('col', 'row')), may hold values from -3 to 3
- operator: float32 [16384, 1024], P('row', 'col'), may hold values from -0.1875 to 0.1875
- target: float32 [16384], replicated, may hold values from -6 to 6
- cone_id: int32 [16384], replicated, may hold values from 0 to 2047, never falling along the last dimension, each value on 1 to 16 neighbouring positions
Outputs:
- next_point: float32 [1024], P(('col', 'row'))
- projected: float32 [16384], P('row')
Inputs may be any that keep to these rules, and one draw needn't show every extreme that they name: cone_id never falls along the rows; each of the 2048 cones holds 1 to 16 consecutive rows.
All inputs are finite; a program needn't handle non-finite values.
Results may differ from a plain program's by a relative error of at most 0.0003.
Values sent between devices are 32-bit elements; how exact they have to be, the bound alone decides.
No kernel may reach another device: no remote copies, remote signals or barrier semaphores. Data moves between devices by JAX's collectives and lax.ppermute only.
A program may use at most 64 MiB of HBM per device.

v0:
```python
import math

import jax
import jax.numpy as jnp
from jax import lax
from jax.sharding import PartitionSpec as P

HIGH = lax.Precision.HIGHEST
RIM = 16


def with_halo(x, sides, width):
    for axis, dim in sides:
        devices, length = (lax.axis_size(axis), x.shape[dim])
        up = [(i, (i + 1) % devices) for i in range(devices - 1)]
        down = [(j, i) for i, j in up]
        last = lax.slice_in_dim(x, length - width, length, axis=dim)
        leading = lax.slice_in_dim(x, 0, width, axis=dim)
        before = lax.ppermute(last, axis, up)
        after = lax.ppermute(leading, axis, down)
        x = jnp.concatenate([before, x, after], axis=dim)
    return x


def solve_weights(gram, right_side):
    count = gram.shape[0]
    shifted = gram + 0.01 * (jnp.trace(gram) / count) * jnp.eye(count, dtype=jnp.float32)
    factor = jnp.linalg.cholesky(shifted)
    return jax.scipy.linalg.cho_solve((factor, True), right_side)


def window_cones(slack_ext, ids_ext, head_ext, length):
    shifts = range(1 - RIM, RIM)
    slack_win = jnp.stack([slack_ext[RIM + s : RIM + s + length] for s in shifts])
    ids_win = jnp.stack([ids_ext[RIM + s : RIM + s + length] for s in shifts])
    head_win = jnp.stack([head_ext[RIM + s : RIM + s + length] for s in shifts])
    own_ids = ids_ext[RIM : RIM + length]
    slack = slack_ext[RIM : RIM + length]
    head_own = head_ext[RIM : RIM + length]
    same = (ids_win == own_ids[None, :]).astype(jnp.float32)
    head_row = jnp.sum(same * head_win * slack_win, axis=0)
    tail_tot = jnp.sum(same * (1.0 - head_win) * slack_win * slack_win, axis=0)
    norm_row = jnp.sqrt(tail_tot)
    inside = norm_row <= head_row
    killed = norm_row <= -head_row
    safe_norm = jnp.where(norm_row > 0, norm_row, 1.0)
    middle = 0.5 * (head_row + norm_row)
    outside = jnp.where(head_own > 0, middle, middle * slack / safe_norm)
    return jnp.where(inside, slack, jnp.where(killed, 0.0, outside))


def body(iterates, residuals, operator, target, cone_id):
    row_count = lax.axis_size("row")
    col_count = lax.axis_size("col")
    row_block = operator.shape[0]
    local_len = iterates.shape[1]
    all_rows = row_block * row_count
    scale_back = math.sqrt(local_len * row_count * col_count / all_rows)
    row_index = lax.axis_index("row")
    row_offset = row_index * row_block
    delta_x = iterates[1:] - iterates[:-1]
    delta_f = residuals[1:] - residuals[:-1]
    last_f = residuals[-1]
    gram_local = jnp.dot(delta_f, delta_f.T, precision=HIGH)
    side_local = jnp.dot(delta_f, last_f, precision=HIGH)
    anchor = iterates[-1] + last_f
    step_dirs = delta_x + delta_f
    gram, right_side = lax.psum((gram_local, side_local), ("row", "col"))
    weights = solve_weights(gram, right_side)
    blended = anchor - jnp.dot(weights, step_dirs, precision=HIGH)
    columns = operator
    partial_value = jnp.zeros((row_block,), jnp.float32) + jnp.dot(
        columns, lax.all_gather(blended, "row", axis=0, tiled=True), precision=HIGH
    )
    image_own = lax.psum(partial_value, "col")
    head_all = jnp.concatenate(
        [jnp.ones((1,), jnp.float32), (cone_id[1:] != cone_id[:-1]).astype(jnp.float32)]
    )
    ids_pad = jnp.concatenate(
        [jnp.full((RIM,), -1, jnp.int32), cone_id, jnp.full((RIM,), -1, jnp.int32)]
    )
    head_pad = jnp.concatenate(
        [jnp.zeros((RIM,), jnp.float32), head_all, jnp.zeros((RIM,), jnp.float32)]
    )
    ids_ext = lax.dynamic_slice_in_dim(ids_pad, row_offset, row_block + 2 * RIM, 0)
    head_ext = lax.dynamic_slice_in_dim(head_pad, row_offset, row_block + 2 * RIM, 0)
    slack_own = lax.dynamic_slice_in_dim(target, row_offset, row_block, 0) - image_own
    slack_ext = with_halo(slack_own, (("row", 0),), RIM)
    slack_own = slack_ext[RIM : RIM + row_block]
    proj_own = window_cones(slack_ext, ids_ext, head_ext, row_block)
    correction = proj_own - slack_own
    columns = operator
    back = lax.psum_scatter(
        jnp.dot(correction, columns, precision=HIGH), "row", scatter_dimension=0, tiled=True
    )
    next_point = blended - scale_back * back
    return (next_point, proj_own)


def solution(mesh):
    return jax.shard_map(
        body,
        mesh=mesh,
        in_specs=(P(None, ("col", "row")), P(None, ("col", "row")), P("row", "col"), P(), P()),
        out_specs=(P(("col", "row")), P("row")),
        check_vma=False,
    )
```

profile of v0, /device:TPU:0, one launch (start us, length us, event | category | flops | bytes accessed | tf_op | source)
XLA Modules:
  0.0 124.1 jit_solution(8513609570144858646)
XLA Ops:
  0.6 0.0 copy-start
  0.7 1.0 convolution_bitcast_fusion.3
  1.7 1.0 fusion.48
  2.7 42.1 %all-reduce.2 = (f32[10,10]{0,1:T(8,128)S(1)}, f32[10]{0:T(128)S(1)}) all-reduce(f32[10,10]{0,1:T(8,128)S(1)} %fusion.48, f32[10]{0:T(128)S(1)} %convolution_bitcast_fusion.3), channel_id=1, replica_groups=mesh['row'=4,'col'=8] {'row','col'}, use_global_device_ids=true, to_apply=%region_0.0 | all-reduce | flops 110 | bytes 880 | tf_op jit(solution)/shard_map/psum | solution.py:68
  44.7 0.6 select_reduce_fusion.1
  46.0 0.1 copy.20
  46.1 0.9 cholesky.17
  47.0 0.1 copy.21
  47.1 0.1 select_reduce_fusion
  47.2 0.6 compare_reduce_fusion
  47.9 0.6 select_select_fusion
  48.5 0.1 copy.23
  48.6 0.8 custom-call.10
  49.4 0.1 convolution_bitcast_fusion.2
  49.5 0.1 convolution_bitcast_fusion.1
  49.7 1.4 %fusion.56 = (u32[1]{0:T(128)}, u32[1]{0:T(128)}) fusion(u32[32]{0:T(128)} %constant.89, u32[]{:T(128)S(6)} %add.52, u32[]{:T(128)S(6)} %add.49), kind=kLoop, calls=%fused_computation.136 | loop fusion | bytes 24
  51.7 0.9 fusion
  52.6 0.2 dynamic-update-slice.3
  52.9 0.3 copy-done.2
  53.1 9.7 %all-reduce = f32[128]{0:T(128)S(1)} all-reduce(f32[128]{0:T(128)S(1)} %dynamic-update-slice.3), channel_id=1, replica_groups=mesh['row'=4,'col'=8] {'row'}, use_global_device_ids=true, to_apply=%add | all-reduce | flops 128 | bytes 1024
  62.9 0.0 copy-done
  62.9 1.8 %fusion.43 = f32[1,4096]{1,0:T(1,128)S(1)} fusion(f32[4096,128]{1,0:T(8,128)S(1)} %copy-done, f32[128]{0:T(128)S(1)} %all-reduce), kind=kOutput, calls=%fused_computation.123 | convolution fusion | flops 6291456 | bytes 2114048 | tf_op jit(solution)/shard_map/dot_general | solution.py:72
  64.7 25.9 %psum.23 = f32[4096]{0:T(1024)S(1)} all-reduce(f32[4096]{0:T(1024)S(1)} %bitcast.210), channel_id=1, replica_groups=mesh['row'=4,'col'=8] {'col'}, use_global_device_ids=true, to_apply=%region_5.6 | all-reduce | flops 4096 | bytes 32768 | tf_op jit(solution)/shard_map/psum | solution.py:75
  90.6 0.7 dynamic-slice_subtract_fusion
  91.3 0.6 fusion.55
  91.9 1.3 %collective-permute-start.1 = (f32[16]{0:T(128)}, f32[16]{0:T(128)}, u32[]{:S(2)}, u32[]{:S(2)}) collective-permute-start(f32[16]{0:T(128)} %get-tuple-element.100), channel_id=1, source_target_pairs={{8,0},{16,8},{24,16},{9,1},{17,9},{25,17},{10,2},{18,10},{26,18},{... | collective-permute-start | bytes 200 | tf_op jit(solution)/shard_map/ppermute | solution.py:20
  93.2 5.1 %collective-permute-start = (f32[16]{0:T(128)}, f32[16]{0:T(128)}, u32[]{:S(2)}, u32[]{:S(2)}) collective-permute-start(f32[16]{0:T(128)} %get-tuple-element.101), channel_id=1, source_target_pairs={{0,8},{8,16},{16,24},{1,9},{9,17},{17,25},{2,10},{10,18},{18,26},{... | collective-permute-start | bytes 200 | tf_op jit(solution)/shard_map/ppermute | solution.py:19
  98.3 0.1 fusion.2
  98.4 0.1 concatenate.41
  98.5 0.1 concatenate.42
  98.6 0.8 fusion.54
  99.4 0.2 fusion.52
  99.6 0.3 fusion.51
  99.9 0.3 fusion.53
  100.8 0.8 stack.351
  101.5 1.6 %stack.319 = s32[31,4096]{1,0:T(8,128)S(1)} concatenate(s32[1,4096]{1,0:T(1,128)} %bitcast.224, s32[1,4096]{1,0:T(1,128)} %bitcast.223, s32[1,4096]{1,0:T(1,128)} %bitcast.222, s32[1,4096]{1,0:T(1,128)} %bitcast.221, s32[1,4096]{1,0:T(1,128)} %bitcast.220, s32[1,4096]{1,0:T(1,128)} %bitcast.219, s32[1,4096]{1,0:T(1,128)} %bitcast.218, s32[1,4096]{1,0:T(1,128)} %bitcast.217, ...), dimensions={0} | concatenate | bytes 1015808 | tf_op jit(solution)/shard_map/stack | solution.py:35
  103.1 0.0 collective-permute-done.1
  103.1 1.1 pad_maximum_fusion
  104.2 1.0 fusion.3
  105.2 0.0 collective-permute-done
  105.2 1.0 fusion.17
  106.2 1.7 %pad_maximum_fusion.1 = (f32[4096]{0:T(1024)S(1)}, f32[4096]{0:T(1024)}, f32[4096]{0:T(1024)}, f32[4096]{0:T(1024)}, f32[4096]{0:T(1024)}, /*index=5*/f32[4096]{...) fusion(f32[4096]{0:T(1024)S(1)} %dynamic-slice_subtract_fusion, f32[16]{0:T(128)} %collective-permute-done), kind=kLoop, calls=%fused_computation.102 | loop fusion | flops 36864 | bytes 163904 | tf_op jit(solution)/shard_map/concatenate | solution.py:21
  108.0 4.1 %stack.383 = f32[31,4096]{1,0:T(8,128)} concatenate(f32[1,4096]{1,0:T(1,128)} %bitcast.202, f32[1,4096]{1,0:T(1,128)} %bitcast.203, f32[1,4096]{1,0:T(1,128)} %bitcast.204, f32[1,4096]{1,0:T(1,128)} %bitcast.205, f32[1,4096]{1,0:T(1,128)} %bitcast.206, f32[1,4096]{1,0:T(1,128)} %bitcast.207, f32[1,4096]{1,0:T(1,128)} %bitcast.208, f32[1,4096]{1,0:T(1,128)} %bitcast.209, ...), dimensions={0} | concatenate | bytes 1015808 | tf_op jit(solution)/shard_map/stack | solution.py:34
  112.1 1.3 %fusion.1 = (f32[4096]{0:T(1024)S(1)}, f32[4096]{0:T(1024)S(1)}) fusion(f32[31,4096]{1,0:T(8,128)} %stack.383, f32[31,4096]{1,0:T(8,128)S(1)} %stack.351, s32[31,4096]{1,0:T(8,128)S(1)} %stack.319, s32[4096]{0:T(1024)S(1)} %get-tuple-element.54), kind=kLoop, calls=%fused_computation.7 | loop fusion | flops 1134592 | bytes 1572864 | tf_op jit(solution)/shard_map/reduce_sum | solution.py:42
  113.4 0.6 fusion.49
  114.0 1.1 convolution_bitcast_fusion.4
  115.1 8.4 %all-reduce.1 = f32[128]{0:T(128)S(1)} all-reduce(f32[128]{0:T(128)S(1)} %convolution_bitcast_fusion.4), channel_id=2, replica_groups=mesh['row'=4,'col'=8] {'row'}, use_global_device_ids=true, to_apply=%region_8.9.clone | all-reduce | flops 128 | bytes 1024
  123.5 0.6 fusion.42
  (10 shorter events, 0.0 us)
Async XLA Ops:
  0.6 62.2 %copy-start = (f32[4096,128]{1,0:T(8,128)S(1)}, f32[4096,128]{1,0:T(8,128)}, u32[]{:S(2)}) copy-start(f32[4096,128]{1,0:T(8,128)} %param.7) | copy-start | bytes 6291460
  0.6 97.7 %copy-start.1 = (s32[16384]{0:T(1024)S(1)}, s32[16384]{0:T(1024)}, u32[]{:S(2)}) copy-start(s32[16384]{0:T(1024)} %param.9) | copy-start | bytes 196612
  52.6 0.5 copy-start.2
  91.9 11.2 %collective-permute-start.1 = (f32[16]{0:T(128)}, f32[16]{0:T(128)}, u32[]{:S(2)}, u32[]{:S(2)}) collective-permute-start(f32[16]{0:T(128)} %get-tuple-element.100), channel_id=1, source_target_pairs={{8,0},{16,8},{24,16},{9,1},{17,9},{25,17},{10,2},{18,10},{26,18},{... | collective-permute-start | bytes 200 | tf_op jit(solution)/shard_map/ppermute | solution.py:20
  93.2 12.0 %collective-permute-start = (f32[16]{0:T(128)}, f32[16]{0:T(128)}, u32[]{:S(2)}, u32[]{:S(2)}) collective-permute-start(f32[16]{0:T(128)} %get-tuple-element.101), channel_id=1, source_target_pairs={{0,8},{8,16},{16,24},{1,9},{9,17},{17,25},{2,10},{10,18},{18,26},{... | collective-permute-start | bytes 200 | tf_op jit(solution)/shard_map/ppermute | solution.py:19
  112.1 11.4 %copy-start.3 = (f32[32]{0:T(128)S(1)}, f32[32]{0:T(128)}, u32[]{:S(2)}) copy-start(f32[32]{0:T(128)} %copy-done.2) | copy-start | bytes 388
where the time goes:
time: 125 us; the launch traced here: 124 us
  blocking collectives  86.1 us (69%)
  other arithmetic  11.8 us (9%)
  local copies, waits for them, and re-layouts  10.9 us (9%)
  starting transfers between devices  6.42 us (5%)
  matrix products  6.11 us (5%)
  between operations  2.75 us (2%)
    psum x1, blocking collectives, body(): gram, right_side = lax.psum((gram_local, side_local), ('row', 'col'))  42.1 us
    psum x1, blocking collectives, body(): image_own = lax.psum(partial_value, 'col')  25.9 us
    unnamed x2, blocking collectives  18.1 us
    ppermute x1, starting transfers between devices, with_halo(): before = lax.ppermute(last, axis, up)  5.14 us
    concatenate x4, other arithmetic, with_halo(): x = jnp.concatenate([before, x, after], axis=dim)  4.81 us
    another operation x1, local copies, waits for them, and re-layouts, window_cones(): slack_win = jnp.stack([slack_ext[RIM + s:RIM + s + length] for s in shifts])  4.14 us
  transfers between devices with their start and end apart: 2, of which 0 were waited for; matrix products, arithmetic and copies ran while one was open for 5% of the time, Pallas kernels for 0%

commit v1 on v0

v1 whole, which is shorter than its diff:
```python
import functools
import math

import jax
import jax.numpy as jnp
from jax import lax
from jax.experimental import pallas as pl
from jax.experimental.pallas import tpu as pltpu
from jax.sharding import PartitionSpec as P

RIM = 16
LANES = 128
TILE = 8
BF16 = jnp.bfloat16
F32 = jnp.float32
LIMIT = 24 * 1024 * 1024
SHIFTS = (1, 2, 4, 8)
NT = (((1,), (1,)), ((), ()))


def params(limit=LIMIT):
    return pltpu.CompilerParams(vmem_limit_bytes=limit)


def vmem():
    return pl.BlockSpec(memory_space=pltpu.VMEM)


def smem():
    return pl.BlockSpec(memory_space=pltpu.SMEM)


def tree(terms):
    terms = list(terms)
    while len(terms) > 1:
        terms = [a + b for a, b in zip(terms[::2], terms[1::2])]
    return terms[0]


def up(length):
    return -(-length // TILE) * TILE


def split(x):
    high = x.astype(BF16)
    return high, (x - high.astype(F32)).astype(BF16)


def shifted(x, step):
    rows, lanes = x.shape
    lane = lax.broadcasted_iota(jnp.int32, x.shape, 1)
    turned = pltpu.roll(x, step % lanes, 1)
    carried = pltpu.roll(turned, (1 if step > 0 else -1) % rows, 0)
    return jnp.where(lane < step if step > 0 else lane >= lanes + step, carried, turned)


def pack_kernel(hist, local, x_ref, f_ref, top_ref, low_ref, out_ref, dirs_ref, diff_ref):
    out_ref[...] = jnp.zeros_like(out_ref)
    dirs_ref[...] = jnp.zeros_like(dirs_ref)
    diff_ref[...] = jnp.zeros_like(diff_ref)
    delta_f = f_ref[1 : hist + 1, :] - f_ref[0:hist, :]
    delta_x = x_ref[1 : hist + 1, :] - x_ref[0:hist, :]
    last_f = f_ref[hist : hist + 1, :]
    diff_ref[0:hist, :] = delta_f
    diff_ref[hist : hist + 1, :] = last_f
    dirs_ref[0:hist, :] = delta_x + delta_f
    dirs_ref[hist : hist + 1, :] = x_ref[hist : hist + 1, :] + last_f
    diff = diff_ref[...]
    gram = lax.dot_general(diff, diff, NT, precision=lax.Precision.HIGHEST, preferred_element_type=F32)
    wide = gram.shape[0]
    out_ref[0:wide, 0:local] = dirs_ref[...]
    out_ref[0:wide, local : local + wide] = gram
    out_ref[wide : wide + RIM, 0 : top_ref.shape[1]] = top_ref[...]
    out_ref[wide + RIM : wide + 2 * RIM, 0 : low_ref.shape[1]] = low_ref[...]


def image_kernel(hist, local, row_count, chunk, row_ref, *refs):
    parts = refs[:row_count]
    oper_ref, target_ref, ids_ref, cat_ref, img_ref, dirs_ref, aux_ref = refs[row_count:]
    row = row_ref[0]
    row_block, width = oper_ref.shape
    wide = up(hist + 1)
    wide = -(-wide // 16) * 16
    own_rows = row_block // LANES
    ext_rows = own_rows + TILE

    lane = lax.broadcasted_iota(jnp.int32, (wide, width), 1)
    dirs = jnp.zeros((wide, width), F32)
    for turn in range(row_count):
        place = lax.bitwise_xor(row, turn)
        block = parts[turn][0:wide, 0:LANES]
        if width > LANES:
            block = jnp.concatenate([block] * (width // LANES), axis=1)
        for slot in range(row_count):
            moved = pltpu.roll(block, slot * local, 1) if slot else block
            dirs = jnp.where((lane // local == slot) & (place == slot), moved, dirs)
    dirs_ref[...] = dirs
    high, low = split(dirs)
    left = jnp.concatenate(
        [jnp.concatenate([high, high], axis=1), jnp.concatenate([low, jnp.zeros_like(low)], axis=1)], axis=0
    )

    def multiply(tile):
        both = lax.dot_general(left, tile, NT, preferred_element_type=F32)
        return both[0:wide, :] + both[wide : 2 * wide, :]

    for start in range(0, row_block, chunk):
        high, low = split(oper_ref[start : start + chunk, :])
        cat_ref[start : start + chunk, 0:width] = high
        cat_ref[start : start + chunk, width : 2 * width] = low
        image = multiply(jnp.concatenate([high, low], axis=1))
        for piece in range(chunk // LANES):
            tile = image[:, piece * LANES : (piece + 1) * LANES]
            img_ref[pl.ds(start // LANES + piece, hist + 1, stride=ext_rows), :] = tile[0 : hist + 1, :]

    after = jnp.zeros((RIM, width), F32)
    before = jnp.zeros((RIM, width), F32)
    for turn in range(row_count):
        place = lax.bitwise_xor(row, turn)
        after = jnp.where(place == row + 1, parts[turn][wide : wide + RIM, 0:width], after)
        before = jnp.where(place == row - 1, parts[turn][wide + RIM : wide + 2 * RIM, 0:width], before)
    edge = jnp.concatenate([after, jnp.zeros((LANES - 2 * RIM, width), F32), before], axis=0)
    high, low = split(edge)
    tile = multiply(jnp.concatenate([high, low], axis=1))
    for place in range(own_rows, ext_rows):
        img_ref[pl.ds(place, hist + 1, stride=ext_rows), :] = tile[0 : hist + 1, :]

    last = ids_ref.shape[0] - 1
    first = row * own_rows
    follow = jnp.minimum(first + own_rows, last)
    ahead = jnp.maximum(first - 1, 0)
    lane1 = lax.broadcasted_iota(jnp.int32, (1, LANES), 1)
    has_next = (first + own_rows) <= last
    ids_next = jnp.where((lane1 < RIM) & has_next, ids_ref[pl.ds(follow, 1), :], -1)
    ids_prev = jnp.where((lane1 >= LANES - RIM) & (first > 0), ids_ref[pl.ds(ahead, 1), :], -1)
    ids = jnp.concatenate(
        [ids_ref[pl.ds(first, own_rows), :], ids_next, jnp.full((TILE - 2, LANES), -1, jnp.int32), ids_prev], axis=0
    )
    aux_ref[0] = jnp.concatenate(
        [
            target_ref[pl.ds(first, own_rows), :],
            target_ref[pl.ds(follow, 1), :],
            jnp.zeros((TILE - 2, LANES), F32),
            target_ref[pl.ds(ahead, 1), :],
        ],
        axis=0,
    )
    for index, step in enumerate(SHIFTS):
        same = (shifted(ids, step) == ids).astype(F32)
        aux_ref[2 + index] = same
        aux_ref[2 + len(SHIFTS) + index] = (shifted(ids, -step) == ids).astype(F32)
        if step == 1:
            aux_ref[1] = 1.0 - same


def solve_kernel(hist, local, count, *refs):
    grams = refs[:count]
    img_ref, dirs_ref, part_ref, blend_ref = refs[count:]
    wide, width = dirs_ref.shape
    gram = tree(g[...] for g in grams)
    index = lax.broadcasted_iota(jnp.int32, (wide, LANES), 0)
    cols = [jnp.broadcast_to(gram[:, local + j : local + j + 1], (wide, LANES)) for j in range(hist + 1)]

    def row_of(x, k):
        return jnp.broadcast_to(x[k : k + 1, :], (wide, LANES))

    trace = row_of(cols[0], 0)
    for k in range(1, hist):
        trace = trace + row_of(cols[k], k)
    ridge = 0.01 * (trace / hist)
    for k in range(hist):
        cols[k] = jnp.where(index == k, cols[k] + ridge, cols[k])
    for k in range(hist):
        inverse = 1.0 / row_of(cols[k], k)
        for j in range(k + 1, hist + 1):
            ratio = row_of(cols[j], k) * inverse
            cols[j] = jnp.where(index == k, ratio, cols[j] - cols[k] * ratio)
    weights = cols[hist]

    ext_rows = part_ref.shape[0]
    total = img_ref[hist * ext_rows : (hist + 1) * ext_rows, :]
    for k in range(hist):
        total = total - jnp.broadcast_to(weights[k : k + 1, :], (ext_rows, LANES)) * img_ref[k * ext_rows : (k + 1) * ext_rows, :]
    part_ref[...] = total
    factors = jnp.where(index < hist, -weights, jnp.where(index == hist, 1.0, 0.0))
    for start in range(0, width, LANES):
        blend_ref[:, start : start + LANES] = jnp.sum(factors * dirs_ref[:, start : start + LANES], axis=0, keepdims=True)


def cone_kernel(count, *refs):
    parts = refs[:count]
    aux_ref, cat_ref, proj_ref, back_ref = refs[count:]
    slack = aux_ref[0] - tree(p[...] for p in parts)
    head = aux_ref[1]
    square = (1.0 - head) * slack * slack
    lead, ahead, behind = head * slack, square, square
    for index, step in enumerate(SHIFTS):
        same = aux_ref[2 + index]
        lead = lead + same * shifted(lead, step)
        ahead = ahead + same * shifted(ahead, step)
        behind = behind + aux_ref[2 + len(SHIFTS) + index] * shifted(behind, -step)
    norm = jnp.sqrt(jnp.maximum(ahead + behind - square, 0.0))
    inside = norm <= lead
    killed = norm <= -lead
    safe = jnp.where(norm > 0, norm, 1.0)
    middle = 0.5 * (lead + norm)
    outside = jnp.where(head > 0, middle, middle * slack / safe)
    projected = jnp.where(inside, slack, jnp.where(killed, 0.0, outside))
    own_rows = proj_ref.shape[0]
    proj_ref[...] = projected[0:own_rows, :]
    correction = projected[0:own_rows, :] - slack[0:own_rows, :]
    high, low = split(correction)
    high, low = high.astype(F32), low.astype(F32)
    sub = lax.broadcasted_iota(jnp.int32, (TILE, LANES), 0)
    pieces = []
    for piece in range(own_rows):
        base = piece // TILE * TILE
        mine = sub == piece % TILE
        pieces.append(
            jnp.concatenate(
                [jnp.where(mine, high[base : base + TILE, :], 0.0), jnp.where(mine, low[base : base + TILE, :], 0.0)], axis=0
            ).astype(BF16)
        )
    left = jnp.concatenate(pieces, axis=1)
    both = jnp.dot(left, cat_ref[...], preferred_element_type=F32)
    width = back_ref.shape[1]
    sums = both[0:TILE, 0:width] + both[0:TILE, width : 2 * width] + both[TILE : 2 * TILE, 0:width]
    back_ref[...] = jnp.sum(sums, axis=0, keepdims=True)


def xor_pairs(count, turn):
    return [(i, i ^ turn) for i in range(count)]


def exchange(x, axis, turns):
    count = lax.axis_size(axis)
    return [lax.ppermute(x, axis, xor_pairs(count, turn)) for turn in turns]


def col_stages(count):
    stages, bit = [[1]], 2
    while bit < count:
        stages.append([bit, 2 * bit, 3 * bit] if 2 * bit < count else [bit])
        bit *= 4
    return stages


def reduce_col(x, count):
    stages = col_stages(count)
    for turns in stages[:-1]:
        x = tree([x, *exchange(x, "col", turns)])
    return [x, *exchange(x, "col", stages[-1])]


def body(iterates, residuals, operator, target, cone_id):
    row_count = lax.axis_size("row")
    col_count = lax.axis_size("col")
    row_block, width = operator.shape
    hist, local = iterates.shape[0] - 1, iterates.shape[1]
    all_rows = row_block * row_count
    scale_back = math.sqrt(local * row_count * col_count / all_rows)
    wide = -(-(hist + 1) // 16) * 16
    own_rows = row_block // LANES
    ext_rows = own_rows + TILE
    row = lax.axis_index("row")
    row_arg = row.astype(jnp.int32).reshape(1)

    message = pl.pallas_call(
        functools.partial(pack_kernel, hist, local),
        name="pack",
        grid=(1,),
        in_specs=[
            pl.BlockSpec((hist + 1, local), lambda i: (0, 0)),
            pl.BlockSpec((hist + 1, local), lambda i: (0, 0)),
            pl.BlockSpec((RIM, width), lambda i: (0, 0)),
            pl.BlockSpec((RIM, width), lambda i: (row_block // RIM - 1, 0)),
        ],
        out_specs=pl.BlockSpec((wide + 2 * RIM, width), lambda i: (0, 0)),
        out_shape=jax.ShapeDtypeStruct((wide + 2 * RIM, width), F32),
        scratch_shapes=[pltpu.VMEM((wide, local), F32), pltpu.VMEM((wide, local), F32)],
        compiler_params=params(),
    )(iterates, residuals, operator, operator)
    messages = [message, *exchange(message, "row", range(1, row_count))]

    gram = tree(m[0:wide, 0:LANES] for m in messages)
    grams = reduce_col(gram, col_count)

    cat, img, dirs, aux = pl.pallas_call(
        functools.partial(image_kernel, hist, local, row_count, min(512, row_block)),
        name="image",
        in_specs=[smem()] + [vmem()] * (row_count + 3),
        out_specs=[vmem()] * 4,
        out_shape=[
            jax.ShapeDtypeStruct((row_block, 2 * width), BF16),
            jax.ShapeDtypeStruct(((hist + 1) * ext_rows, LANES), F32),
            jax.ShapeDtypeStruct((wide, width), F32),
            jax.ShapeDtypeStruct((2 + 2 * len(SHIFTS), ext_rows, LANES), F32),
        ],
        compiler_params=params(),
    )(row_arg, *messages, operator, target.reshape(-1, LANES), cone_id.reshape(-1, LANES))

    part, blended = pl.pallas_call(
        functools.partial(solve_kernel, hist, local, len(grams)),
        name="solve",
        in_specs=[vmem()] * (len(grams) + 2),
        out_specs=[vmem()] * 2,
        out_shape=[jax.ShapeDtypeStruct((ext_rows, LANES), F32), jax.ShapeDtypeStruct((1, width), F32)],
        compiler_params=params(),
    )(*grams, img, dirs)

    parts = reduce_col(part, col_count)
    projected, back = pl.pallas_call(
        functools.partial(cone_kernel, len(parts)),
        name="cones",
        in_specs=[vmem()] * (len(parts) + 2),
        out_specs=[vmem()] * 2,
        out_shape=[jax.ShapeDtypeStruct((own_rows, LANES), F32), jax.ShapeDtypeStruct((1, width), F32)],
        compiler_params=params(),
    )(*parts, aux, cat)

    back = tree([back, *exchange(back, "row", range(1, row_count))])
    moved = blended - scale_back * back
    next_point = lax.dynamic_slice_in_dim(moved, row * local, local, 1)
    return (next_point.reshape(local), projected.reshape(row_block))


def solution(mesh):
    return jax.shard_map(
        body,
        mesh=mesh,
        in_specs=(P(None, ("col", "row")), P(None, ("col", "row")), P("row", "col"), P(), P()),
        out_specs=(P(("col", "row")), P("row")),
        check_vma=False,
    )
```

time: 125 us -> 39.3 us (0.31)
  blocking collectives: 86.1 us -> 0 us
  waiting for transfers between devices: 0.01 us -> 15.5 us
  other arithmetic: 11.8 us -> 0.02 us
  starting transfers between devices: 6.42 us -> 16.8 us
  local copies, waits for them, and re-layouts: 10.9 us -> 3.57 us
  matrix products: 6.11 us -> 0 us
  Pallas kernels: 0 us -> 2.42 us
  between operations: 2.75 us -> 0.68 us
    psum x2 -> x0, blocking collectives: 68 us -> none  [the longest x1 42.1 us: body(): gram, right_side = lax.psum((gram_local, side_local), ('row', 'col'))]
    unnamed x2 -> x0, blocking collectives: 18.1 us -> none
    ppermute x2 -> x14, waiting for transfers between devices: 0.01 us -> 15.5 us  [exchange(): return [lax.ppermute(x, axis, xor_pairs(count, turn)) for turn in turns]]
    ppermute x2 -> x14, starting transfers between devices: 6.42 us -> 16.8 us  [exchange(): return [lax.ppermute(x, axis, xor_pairs(count, turn)) for turn in turns]]
    another operation x7 -> x0, local copies, waits for them, and re-layouts: 6.7 us -> none  [the longest x1 4.14 us: window_cones(): slack_win = jnp.stack([slack_ext[RIM + s:RIM + s + length] for s in shifts])]
    dot_general x5 -> x0, matrix products: 5.83 us -> none  [the longest x1 1.8 us: body(): jnp.dot(columns, lax.all_gather(blended, 'row', axis=0, tiled=True), prec...]
    concatenate x4 -> x0, other arithmetic: 4.81 us -> none  [with_halo(): x = jnp.concatenate([before, x, after], axis=dim)]
    another operation x5 -> x0, other arithmetic: 3.07 us -> none  [the longest x3 1.64 us: solve_weights(): factor = jnp.linalg.cholesky(shifted)]
  transfers between devices with their start and end apart: 2 -> 14, of which waited for: 0 -> 12; matrix products, arithmetic and copies ran while one was open for 5% -> 0% of each run, Pallas kernels for 0% -> 2%
where the time goes in v1:
time: 39.3 us; the launch traced here: 39 us
  starting transfers between devices  16.8 us (43%)
  waiting for transfers between devices  15.5 us (39%)
  local copies, waits for them, and re-layouts  3.57 us (9%)
  Pallas kernels  2.42 us (6%)
  between operations  0.68 us (2%)
    ppermute x14, starting transfers between devices, exchange(): return [lax.ppermute(x, axis, xor_pairs(count, turn)) for turn in turns]  16.8 us
    ppermute x14, waiting for transfers between devices, exchange(): return [lax.ppermute(x, axis, xor_pairs(count, turn)) for turn in turns]  15.5 us
    unnamed x12, local copies, waits for them, and re-layouts  2.99 us
    pallas_call x1, Pallas kernels, body(): pl.pallas_call(functools.partial(cone_kernel, len(parts)), name='cones',...  1.16 us
    pallas_call x1, Pallas kernels, body(): pl.pallas_call(functools.partial(image_kernel, hist, local, row_count, mi...  0.8 us
  transfers between devices with their start and end apart: 14, of which 12 were waited for; matrix products, arithmetic and copies ran while one was open for 0% of the time, Pallas kernels for 2%

profile of v1, /device:TPU:0, one launch (start us, length us, event | category | flops | bytes accessed | tf_op | source)
XLA Modules:
  0.0 39.0 jit_solution(2799161482520782746)
XLA Ops:
  0.6 0.0 copy-start
  0.6 1.6 %copy-done = f32[4096,128]{1,0:T(8,128)S(1)} copy-done((f32[4096,128]{1,0:T(8,128)S(1)}, f32[4096,128]{1,0:T(8,128)}, u32[]{:S(2)}) %copy-start) | copy-done | bytes 2097176
  2.2 0.0 copy-start.4
  2.2 0.7 %copy-done.4 = f32[11,32]{1,0:T(8,128)S(1)} copy-done((f32[11,32]{1,0:T(8,128)S(1)}, f32[11,32]{1,0:T(8,128)}, u32[]{:S(2)}) %copy-start.4) | copy-done | bytes 1432
  2.9 0.0 copy-start.5
  2.9 0.7 %copy-done.5 = f32[11,32]{1,0:T(8,128)S(1)} copy-done((f32[11,32]{1,0:T(8,128)S(1)}, f32[11,32]{1,0:T(8,128)}, u32[]{:S(2)}) %copy-start.5) | copy-done | bytes 1432
  3.6 0.0 copy-start.1
  3.6 0.0 copy-start.2
  3.6 0.0 copy-start.3
  3.6 0.2 pack.1.refs_0_
  3.8 3.0 %collective-permute-start = (f32[48,128]{1,0:T(8,128)S(1)}, f32[48,128]{1,0:T(8,128)S(1)}, u32[]{:S(2)}, u32[]{:S(2)}) collective-permute-start(f32[48,128]{1,0:T(8,128)S(1)} %pack.1.refs_0_), channel_id=1, source_target_pairs={{0,8},{8,0},{16,24},{24,16},{1,9},{9,1},{17,25},{25,17},{2,10},{10... | collective-permute-start | bytes 73736 | tf_op jit(solution)/shard_map/ppermute | solution.py:237
  6.8 1.5 %collective-permute-start.1 = (f32[48,128]{1,0:T(8,128)S(1)}, f32[48,128]{1,0:T(8,128)S(1)}, u32[]{:S(2)}, u32[]{:S(2)}) collective-permute-start(f32[48,128]{1,0:T(8,128)S(1)} %pack.1.refs_0_), channel_id=1, source_target_pairs={{0,16},{8,24},{16,0},{24,8},{1,17},{9,25},{17,1},{25,9},{2,18},{10... | collective-permute-start | bytes 73736 | tf_op jit(solution)/shard_map/ppermute | solution.py:237
  8.3 0.0 collective-permute-start.2
  8.3 0.3 collective-permute-done.refs_1_
  8.6 2.0 %collective-permute-done.1.refs_2_ = f32[48,128]{1,0:T(8,128)S(1)} collective-permute-done((f32[48,128]{1,0:T(8,128)S(1)}, f32[48,128]{1,0:T(8,128)S(1)}, u32[]{:S(2)}, u32[]{:S(2)}) %collective-permute-start.1) | collective-permute-done | bytes 24608 | tf_op jit(solution)/shard_map/ppermute | solution.py:237
  10.6 2.4 %collective-permute-done.2.refs_3_ = f32[48,128]{1,0:T(8,128)S(1)} collective-permute-done((f32[48,128]{1,0:T(8,128)S(1)}, f32[48,128]{1,0:T(8,128)S(1)}, u32[]{:S(2)}, u32[]{:S(2)}) %collective-permute-start.2) | collective-permute-done | bytes 24608 | tf_op jit(solution)/shard_map/ppermute | solution.py:237
  13.1 0.0 collective-permute-start.3
  13.1 1.2 %collective-permute-done.3 = f32[16,128]{1,0:T(8,128)S(1)} collective-permute-done((f32[16,128]{1,0:T(8,128)S(1)}, f32[16,128]{1,0:T(8,128)S(1)}, u32[]{:S(2)}, u32[]{:S(2)}) %collective-permute-start.3) | collective-permute-done | bytes 8224 | tf_op jit(solution)/shard_map/ppermute | solution.py:237
  14.2 1.6 %collective-permute-start.4 = (f32[16,128]{1,0:T(8,128)S(1)}, f32[16,128]{1,0:T(8,128)S(1)}, u32[]{:S(2)}, u32[]{:S(2)}) collective-permute-start(f32[16,128]{1,0:T(8,128)S(1)} %add.30.refs_0_), channel_id=1, source_target_pairs={{0,2},{1,3},{2,0},{3,1},{4,6},{5,7},{6,4},{7,5},{8,10},{9,11},{10,... | collective-permute-start | bytes 24584 | tf_op jit(solution)/shard_map/ppermute | solution.py:237
  15.8 2.6 %collective-permute-start.5 = (f32[16,128]{1,0:T(8,128)S(1)}, f32[16,128]{1,0:T(8,128)S(1)}, u32[]{:S(2)}, u32[]{:S(2)}) collective-permute-start(f32[16,128]{1,0:T(8,128)S(1)} %add.30.refs_0_), channel_id=1, source_target_pairs={{0,4},{1,5},{2,6},{3,7},{4,0},{5,1},{6,2},{7,3},{8,12},{9,13},{10,... | collective-permute-start | bytes 24584 | tf_op jit(solution)/shard_map/ppermute | solution.py:237
  18.4 0.2 collective-permute-start.6
  18.6 0.0 copy-done.1
  18.6 0.0 copy-done.2
  18.6 0.0 copy-done.3
  18.6 0.8 %image.1 = (bf16[4096,256]{1,0:T(8,128)(2,1)S(1)}, f32[440,128]{1,0:T(8,128)S(1)}, f32[16,128]{1,0:T(8,128)S(1)}, f32[10,40,128]{2,1,0:T(8,128)S(1)}) custom-call(s32[1]{0:T(128)} %bitcast.row_ref, f32[48,128]{1,0:T(8,128)S(1)} %pack.1.refs_0_, f32[48,128]{1,0:T(8,128)S(1)} %collective-permute-done.refs_1_, f32[48,128]{1,0:T(8,128)S(1)} %collective-permute-done.1.refs_2_, ...), custom_call_target="tpu_custom_call" | custom-call | tf_op jit(solution)/shard_map/image/pallas_call | solution.py:288
  19.4 0.0 collective-permute-done.4.refs_1_
  19.4 0.9 %collective-permute-done.5.refs_2_ = f32[16,128]{1,0:T(8,128)S(1)} collective-permute-done((f32[16,128]{1,0:T(8,128)S(1)}, f32[16,128]{1,0:T(8,128)S(1)}, u32[]{:S(2)}, u32[]{:S(2)}) %collective-permute-start.5) | collective-permute-done | bytes 8224 | tf_op jit(solution)/shard_map/ppermute | solution.py:237
  20.4 3.5 %collective-permute-done.6.refs_3_ = f32[16,128]{1,0:T(8,128)S(1)} collective-permute-done((f32[16,128]{1,0:T(8,128)S(1)}, f32[16,128]{1,0:T(8,128)S(1)}, u32[]{:S(2)}, u32[]{:S(2)}) %collective-permute-start.6) | collective-permute-done | bytes 8224 | tf_op jit(solution)/shard_map/ppermute | solution.py:237
  23.8 0.2 solve.1
  24.1 0.1 collective-permute-start.7
  24.2 1.2 %collective-permute-done.7 = f32[40,128]{1,0:T(8,128)S(1)} collective-permute-done((f32[40,128]{1,0:T(8,128)S(1)}, f32[40,128]{1,0:T(8,128)S(1)}, u32[]{:S(2)}, u32[]{:S(2)}) %collective-permute-start.7) | collective-permute-done | bytes 20512 | tf_op jit(solution)/shard_map/ppermute | solution.py:237
  25.4 0.2 collective-permute-start.10
  25.6 0.0 collective-permute-start.8
  25.6 4.2 %collective-permute-start.9 = (f32[40,128]{1,0:T(8,128)S(1)}, f32[40,128]{1,0:T(8,128)S(1)}, u32[]{:S(2)}, u32[]{:S(2)}) collective-permute-start(f32[40,128]{1,0:T(8,128)S(1)} %add.31.refs_0_), channel_id=1, source_target_pairs={{0,4},{1,5},{2,6},{3,7},{4,0},{5,1},{6,2},{7,3},{8,12},{9,13},{10,... | collective-permute-start | bytes 61448 | tf_op jit(solution)/shard_map/ppermute | solution.py:237
  29.8 1.2 %collective-permute-done.10.refs_3_ = f32[40,128]{1,0:T(8,128)S(1)} collective-permute-done((f32[40,128]{1,0:T(8,128)S(1)}, f32[40,128]{1,0:T(8,128)S(1)}, u32[]{:S(2)}, u32[]{:S(2)}) %collective-permute-start.10) | collective-permute-done | bytes 20512 | tf_op jit(solution)/shard_map/ppermute | solution.py:237
  30.9 0.0 collective-permute-done.8.refs_1_
  30.9 0.6 %collective-permute-done.9.refs_2_ = f32[40,128]{1,0:T(8,128)S(1)} collective-permute-done((f32[40,128]{1,0:T(8,128)S(1)}, f32[40,128]{1,0:T(8,128)S(1)}, u32[]{:S(2)}, u32[]{:S(2)}) %collective-permute-start.9) | collective-permute-done | bytes 20512 | tf_op jit(solution)/shard_map/ppermute | solution.py:237
  31.5 1.2 %cones.1 = (f32[32,128]{1,0:T(8,128)}, f32[1,128]{1,0:T(1,128)S(1)}) custom-call(f32[40,128]{1,0:T(8,128)S(1)} %add.31.refs_0_, f32[40,128]{1,0:T(8,128)S(1)} %collective-permute-done.8.refs_1_, f32[40,128]{1,0:T(8,128)S(1)} %collective-permute-done.9.refs_2_, f32[40,128]{1,0:T(8,128)S(1)} %collective-permute-done.10.refs_3_, ...), custom_call_target="tpu_custom_call" | custom-call | tf_op jit(solution)/shard_map/cones/pallas_call | solution.py:312
  32.7 0.5 %collective-permute-start.11 = (f32[1,128]{1,0:T(1,128)S(1)}, f32[1,128]{1,0:T(1,128)S(1)}, u32[]{:S(2)}, u32[]{:S(2)}) collective-permute-start(f32[1,128]{1,0:T(1,128)S(1)} %get-tuple-element.16), channel_id=1, source_target_pairs={{0,8},{8,0},{16,24},{24,16},{1,9},{9,1},{17,25},{25,17},{2,10},{10... | collective-permute-start | bytes 1544 | tf_op jit(solution)/shard_map/ppermute | solution.py:237
  33.2 0.7 %collective-permute-start.12 = (f32[1,128]{1,0:T(1,128)S(1)}, f32[1,128]{1,0:T(1,128)S(1)}, u32[]{:S(2)}, u32[]{:S(2)}) collective-permute-start(f32[1,128]{1,0:T(1,128)S(1)} %get-tuple-element.16), channel_id=1, source_target_pairs={{0,16},{8,24},{16,0},{24,8},{1,17},{9,25},{17,1},{25,9},{2,18},{10... | collective-permute-start | bytes 1544 | tf_op jit(solution)/shard_map/ppermute | solution.py:237
  33.9 2.2 %collective-permute-start.13 = (f32[1,128]{1,0:T(1,128)S(1)}, f32[1,128]{1,0:T(1,128)S(1)}, u32[]{:S(2)}, u32[]{:S(2)}) collective-permute-start(f32[1,128]{1,0:T(1,128)S(1)} %get-tuple-element.16), channel_id=1, source_target_pairs={{0,24},{8,16},{16,8},{24,0},{1,25},{9,17},{17,9},{25,1},{2,26},{10... | collective-permute-start | bytes 1544 | tf_op jit(solution)/shard_map/ppermute | solution.py:237
  36.2 0.1 collective-permute-done.11
  36.2 0.5 %collective-permute-done.12 = f32[1,128]{1,0:T(1,128)S(1)} collective-permute-done((f32[1,128]{1,0:T(1,128)S(1)}, f32[1,128]{1,0:T(1,128)S(1)}, u32[]{:S(2)}, u32[]{:S(2)}) %collective-permute-start.12) | collective-permute-done | bytes 544 | tf_op jit(solution)/shard_map/ppermute | solution.py:237
  36.8 1.6 %collective-permute-done.13 = f32[1,128]{1,0:T(1,128)S(1)} collective-permute-done((f32[1,128]{1,0:T(1,128)S(1)}, f32[1,128]{1,0:T(1,128)S(1)}, u32[]{:S(2)}, u32[]{:S(2)}) %collective-permute-start.13) | collective-permute-done | bytes 544 | tf_op jit(solution)/shard_map/ppermute | solution.py:237
  38.4 0.6 %dynamic-slice_bitcast_fusion = f32[32]{0:T(128)} fusion(f32[1,128]{1,0:T(1,128)S(1)} %multiply_subtract_fusion, s32[]{:T(128)S(6)} %select_n.3), kind=kLoop, calls=%fused_computation.3 | loop fusion | bytes 260 | tf_op jit(solution)/shard_map/reshape | solution.py:324
  (4 shorter events, 0.0 us)
Async XLA Ops:
  0.6 1.6 %copy-start = (f32[4096,128]{1,0:T(8,128)S(1)}, f32[4096,128]{1,0:T(8,128)}, u32[]{:S(2)}) copy-start(f32[4096,128]{1,0:T(8,128)} %refs_4_.1) | copy-start | bytes 6291460
  2.2 0.7 %copy-start.4 = (f32[11,32]{1,0:T(8,128)S(1)}, f32[11,32]{1,0:T(8,128)}, u32[]{:S(2)}) copy-start(f32[11,32]{1,0:T(8,128)} %x_ref.1) | copy-start | bytes 4228
  2.9 0.7 %copy-start.5 = (f32[11,32]{1,0:T(8,128)S(1)}, f32[11,32]{1,0:T(8,128)}, u32[]{:S(2)}) copy-start(f32[11,32]{1,0:T(8,128)} %f_ref.1) | copy-start | bytes 4228
  3.6 15.0 %copy-start.1 = (f32[4096,128]{1,0:T(8,128)S(1)}, f32[4096,128]{1,0:T(8,128)}, u32[]{:S(2)}) copy-start(f32[4096,128]{1,0:T(8,128)} %refs_4_.1) | copy-start | bytes 6291460
  3.6 15.0 %copy-start.2 = (f32[16384]{0:T(1024)S(1)}, f32[16384]{0:T(1024)}, u32[]{:S(2)}) copy-start(f32[16384]{0:T(1024)} %param.8) | copy-start | bytes 196612
  3.6 15.0 %copy-start.3 = (s32[16384]{0:T(1024)S(1)}, s32[16384]{0:T(1024)}, u32[]{:S(2)}) copy-start(s32[16384]{0:T(1024)} %param.9) | copy-start | bytes 196612
  3.8 4.8 %collective-permute-start = (f32[48,128]{1,0:T(8,128)S(1)}, f32[48,128]{1,0:T(8,128)S(1)}, u32[]{:S(2)}, u32[]{:S(2)}) collective-permute-start(f32[48,128]{1,0:T(8,128)S(1)} %pack.1.refs_0_), channel_id=1, source_target_pairs={{0,8},{8,0},{16,24},{24,16},{1,9},{9,1},{17,25},{25,17},{2,10},{10... | collective-permute-start | bytes 73736 | tf_op jit(solution)/shard_map/ppermute | solution.py:237
  6.8 3.8 %collective-permute-start.1 = (f32[48,128]{1,0:T(8,128)S(1)}, f32[48,128]{1,0:T(8,128)S(1)}, u32[]{:S(2)}, u32[]{:S(2)}) collective-permute-start(f32[48,128]{1,0:T(8,128)S(1)} %pack.1.refs_0_), channel_id=1, source_target_pairs={{0,16},{8,24},{16,0},{24,8},{1,17},{9,25},{17,1},{25,9},{2,18},{10... | collective-permute-start | bytes 73736 | tf_op jit(solution)/shard_map/ppermute | solution.py:237
  8.3 4.7 %collective-permute-start.2 = (f32[48,128]{1,0:T(8,128)S(1)}, f32[48,128]{1,0:T(8,128)S(1)}, u32[]{:S(2)}, u32[]{:S(2)}) collective-permute-start(f32[48,128]{1,0:T(8,128)S(1)} %pack.1.refs_0_), channel_id=1, source_target_pairs={{0,24},{8,16},{16,8},{24,0},{1,25},{9,17},{17,9},{25,1},{2,26},{10... | collective-permute-start | bytes 73736 | tf_op jit(solution)/shard_map/ppermute | solution.py:237
  13.1 1.2 %collective-permute-start.3 = (f32[16,128]{1,0:T(8,128)S(1)}, f32[16,128]{1,0:T(8,128)S(1)}, u32[]{:S(2)}, u32[]{:S(2)}) collective-permute-start(f32[16,128]{1,0:T(8,128)S(1)} %fusion), channel_id=1, source_target_pairs={{0,1},{1,0},{2,3},{3,2},{4,5},{5,4},{6,7},{7,6},{8,9},{9,8},{10,11... | collective-permute-start | bytes 24584 | tf_op jit(solution)/shard_map/ppermute | solution.py:237
  14.2 5.2 %collective-permute-start.4 = (f32[16,128]{1,0:T(8,128)S(1)}, f32[16,128]{1,0:T(8,128)S(1)}, u32[]{:S(2)}, u32[]{:S(2)}) collective-permute-start(f32[16,128]{1,0:T(8,128)S(1)} %add.30.refs_0_), channel_id=1, source_target_pairs={{0,2},{1,3},{2,0},{3,1},{4,6},{5,7},{6,4},{7,5},{8,10},{9,11},{10,... | collective-permute-start | bytes 24584 | tf_op jit(solution)/shard_map/ppermute | solution.py:237
  15.8 4.5 %collective-permute-start.5 = (f32[16,128]{1,0:T(8,128)S(1)}, f32[16,128]{1,0:T(8,128)S(1)}, u32[]{:S(2)}, u32[]{:S(2)}) collective-permute-start(f32[16,128]{1,0:T(8,128)S(1)} %add.30.refs_0_), channel_id=1, source_target_pairs={{0,4},{1,5},{2,6},{3,7},{4,0},{5,1},{6,2},{7,3},{8,12},{9,13},{10,... | collective-permute-start | bytes 24584 | tf_op jit(solution)/shard_map/ppermute | solution.py:237
  18.4 5.4 %collective-permute-start.6 = (f32[16,128]{1,0:T(8,128)S(1)}, f32[16,128]{1,0:T(8,128)S(1)}, u32[]{:S(2)}, u32[]{:S(2)}) collective-permute-start(f32[16,128]{1,0:T(8,128)S(1)} %add.30.refs_0_), channel_id=1, source_target_pairs={{0,6},{1,7},{2,4},{3,5},{4,2},{5,3},{6,0},{7,1},{8,14},{9,15},{10,... | collective-permute-start | bytes 24584 | tf_op jit(solution)/shard_map/ppermute | solution.py:237
  24.1 1.3 %collective-permute-start.7 = (f32[40,128]{1,0:T(8,128)S(1)}, f32[40,128]{1,0:T(8,128)S(1)}, u32[]{:S(2)}, u32[]{:S(2)}) collective-permute-start(f32[40,128]{1,0:T(8,128)S(1)} %get-tuple-element.13), channel_id=1, source_target_pairs={{0,1},{1,0},{2,3},{3,2},{4,5},{5,4},{6,7},{7,6},{8,9},{9,8},{10,11... | collective-permute-start | bytes 61448 | tf_op jit(solution)/shard_map/ppermute | solution.py:237
  25.4 5.6 %collective-permute-start.10 = (f32[40,128]{1,0:T(8,128)S(1)}, f32[40,128]{1,0:T(8,128)S(1)}, u32[]{:S(2)}, u32[]{:S(2)}) collective-permute-start(f32[40,128]{1,0:T(8,128)S(1)} %add.31.refs_0_), channel_id=1, source_target_pairs={{0,6},{1,7},{2,4},{3,5},{4,2},{5,3},{6,0},{7,1},{8,14},{9,15},{10,... | collective-permute-start | bytes 61448 | tf_op jit(solution)/shard_map/ppermute | solution.py:237
  25.6 5.4 %collective-permute-start.8 = (f32[40,128]{1,0:T(8,128)S(1)}, f32[40,128]{1,0:T(8,128)S(1)}, u32[]{:S(2)}, u32[]{:S(2)}) collective-permute-start(f32[40,128]{1,0:T(8,128)S(1)} %add.31.refs_0_), channel_id=1, source_target_pairs={{0,2},{1,3},{2,0},{3,1},{4,6},{5,7},{6,4},{7,5},{8,10},{9,11},{10,... | collective-permute-start | bytes 61448 | tf_op jit(solution)/shard_map/ppermute | solution.py:237
  25.6 5.9 %collective-permute-start.9 = (f32[40,128]{1,0:T(8,128)S(1)}, f32[40,128]{1,0:T(8,128)S(1)}, u32[]{:S(2)}, u32[]{:S(2)}) collective-permute-start(f32[40,128]{1,0:T(8,128)S(1)} %add.31.refs_0_), channel_id=1, source_target_pairs={{0,4},{1,5},{2,6},{3,7},{4,0},{5,1},{6,2},{7,3},{8,12},{9,13},{10,... | collective-permute-start | bytes 61448 | tf_op jit(solution)/shard_map/ppermute | solution.py:237
  32.7 3.6 %collective-permute-start.11 = (f32[1,128]{1,0:T(1,128)S(1)}, f32[1,128]{1,0:T(1,128)S(1)}, u32[]{:S(2)}, u32[]{:S(2)}) collective-permute-start(f32[1,128]{1,0:T(1,128)S(1)} %get-tuple-element.16), channel_id=1, source_target_pairs={{0,8},{8,0},{16,24},{24,16},{1,9},{9,1},{17,25},{25,17},{2,10},{10... | collective-permute-start | bytes 1544 | tf_op jit(solution)/shard_map/ppermute | solution.py:237
  33.2 3.6 %collective-permute-start.12 = (f32[1,128]{1,0:T(1,128)S(1)}, f32[1,128]{1,0:T(1,128)S(1)}, u32[]{:S(2)}, u32[]{:S(2)}) collective-permute-start(f32[1,128]{1,0:T(1,128)S(1)} %get-tuple-element.16), channel_id=1, source_target_pairs={{0,16},{8,24},{16,0},{24,8},{1,17},{9,25},{17,1},{25,9},{2,18},{10... | collective-permute-start | bytes 1544 | tf_op jit(solution)/shard_map/ppermute | solution.py:237
  33.9 4.5 %collective-permute-start.13 = (f32[1,128]{1,0:T(1,128)S(1)}, f32[1,128]{1,0:T(1,128)S(1)}, u32[]{:S(2)}, u32[]{:S(2)}) collective-permute-start(f32[1,128]{1,0:T(1,128)S(1)} %get-tuple-element.16), channel_id=1, source_target_pairs={{0,24},{8,16},{16,8},{24,0},{1,25},{9,17},{17,9},{25,1},{2,26},{10... | collective-permute-start | bytes 1544 | tf_op jit(solution)/shard_map/ppermute | solution.py:237

commit v2 on v1

v2 whole, which is shorter than its diff:
```python
import functools
import math

import jax
import jax.numpy as jnp
from jax import lax
from jax.experimental import pallas as pl
from jax.experimental.pallas import tpu as pltpu
from jax.sharding import PartitionSpec as P

LANES = 128
TILE = 8
BF16 = jnp.bfloat16
F32 = jnp.float32
LIMIT = 24 * 1024 * 1024
SHIFTS = (1, 2, 4, 8)
NT = (((1,), (1,)), ((), ()))
TARGET, HEAD, FIRST, LAST, UPWARD, DOWNWARD = 0, 1, 2, 3, 4, 4 + len(SHIFTS)
AUX = 4 + 2 * len(SHIFTS)
BACK, TAIL_LAST, HEAD_LAST, TAIL_FIRST, SQUARE_LAST, LEAD_LAST, SQUARE_FIRST = range(7)


def params():
    return pltpu.CompilerParams(vmem_limit_bytes=LIMIT)


def vmem():
    return pl.BlockSpec(memory_space=pltpu.VMEM)


def smem():
    return pl.BlockSpec(memory_space=pltpu.SMEM)


def hbm(x):
    return pltpu.with_memory_space_constraint(x, pltpu.HBM)


def tree(terms):
    terms = list(terms)
    while len(terms) > 1:
        terms = [a + b for a, b in zip(terms[::2], terms[1::2])]
    return terms[0]


def split(x):
    high = x.astype(BF16)
    return high, (x - high.astype(F32)).astype(BF16)


def shifted(x, step):
    rows, lanes = x.shape
    lane = lax.broadcasted_iota(jnp.int32, x.shape, 1)
    turned = pltpu.roll(x, step % lanes, 1)
    carried = pltpu.roll(turned, (1 if step > 0 else -1) % rows, 0)
    return jnp.where(lane < step if step > 0 else lane >= lanes + step, carried, turned)


def dims(hist, local):
    wide = -(-(hist + 1) // 16) * 16
    return wide, LANES // local, wide * local // LANES


def pack_kernel(hist, local, x_any, f_any, out_ref, x_ref, f_ref, dirs_ref, diff_ref, sems):
    wide, group, rows = dims(hist, local)
    copies = [pltpu.make_async_copy(a, b, sems.at[i]) for i, (a, b) in enumerate(((x_any, x_ref), (f_any, f_ref)))]
    for copy in copies:
        copy.start()
    dirs_ref[...] = jnp.zeros_like(dirs_ref)
    diff_ref[...] = jnp.zeros_like(diff_ref)
    for copy in copies:
        copy.wait()
    delta_f = f_ref[1 : hist + 1, :] - f_ref[0:hist, :]
    delta_x = x_ref[1 : hist + 1, :] - x_ref[0:hist, :]
    last_f = f_ref[hist : hist + 1, :]
    diff_ref[0:hist, :] = delta_f
    diff_ref[hist : hist + 1, :] = last_f
    dirs_ref[0:hist, 0:local] = delta_x + delta_f
    dirs_ref[hist : hist + 1, 0:local] = x_ref[hist : hist + 1, :] + last_f
    gram = lax.dot_general(diff_ref[0:wide, :], diff_ref[...], NT, precision=lax.Precision.HIGHEST, preferred_element_type=F32)
    sub = lax.broadcasted_iota(jnp.int32, gram.shape, 0)
    gram = jnp.where(sub < hist, gram, 0.0)
    flat = jnp.zeros((TILE, LANES), F32)
    for start in range(0, wide, TILE):
        turned = pltpu.roll(gram[start : start + TILE, :], 0, 1, stride=hist + 1, stride_axis=0)
        flat = flat + (pltpu.roll(turned, start * (hist + 1) % LANES, 1) if start else turned)
    message = dirs_ref[pl.ds(0, rows, stride=group), :]
    for place in range(1, group):
        message = message + pltpu.roll(dirs_ref[pl.ds(place, rows, stride=group), :], place * local, 1)
    sub = lax.broadcasted_iota(jnp.int32, message.shape, 0)
    message = jnp.where(sub == rows - 1, jnp.sum(flat, axis=0, keepdims=True), message)
    message = jnp.concatenate([message] * (TILE // rows), axis=0)
    for start in range(0, out_ref.shape[0], TILE):
        out_ref[start : start + TILE, :] = message


def split_kernel(message_any, oper_ref, cat_ref):
    width = oper_ref.shape[1]
    high, low = split(oper_ref[...])
    cat_ref[:, 0:width] = high
    cat_ref[:, width : 2 * width] = low


def image_kernel(hist, local, row_count, chunk, where_ref, recv_ref, cat_ref, part_ref, blend_ref, dirs_ref, img_ref):
    wide, group, rows = dims(hist, local)
    row_block, width = cat_ref.shape[0], cat_ref.shape[1] // 2
    own_rows = row_block // LANES
    mine = recv_ref[pl.ds(pl.multiple_of(where_ref[1] * (row_count * rows), TILE), row_count * rows), :]
    lane = lax.broadcasted_iota(jnp.int32, (rows, LANES), 1)
    for start in range(0, width, LANES):
        for place in range(group):
            spread = jnp.zeros((rows, LANES), F32)
            for slot in range(group):
                block = start // local + slot
                moved = mine[block * rows : (block + 1) * rows, :]
                if slot != place:
                    moved = pltpu.roll(moved, (slot - place) * local % LANES, 1)
                spread = jnp.where(lane // local == slot, moved, spread)
            dirs_ref.at[start // LANES][pl.ds(place, rows, stride=group), :] = spread
    sub = lax.broadcasted_iota(jnp.int32, (wide, width), 0)
    dirs = jnp.concatenate([dirs_ref[i] for i in range(width // LANES)], axis=1)
    dirs = jnp.where(sub <= hist, dirs, 0.0)
    high, low = split(dirs)
    left = jnp.concatenate(
        [jnp.concatenate([high, high], axis=1), jnp.concatenate([low, jnp.zeros_like(low)], axis=1)], axis=0
    )
    for start in range(0, row_block, chunk):
        both = lax.dot_general(left, cat_ref[start : start + chunk, :], NT, preferred_element_type=F32)
        image = both[0:wide, :] + both[wide : 2 * wide, :]
        for piece in range(chunk // LANES):
            tile = image[:, piece * LANES : (piece + 1) * LANES]
            img_ref[pl.ds(start // LANES + piece, hist + 1, stride=own_rows), :] = tile[0 : hist + 1, :]

    flat = jnp.sum(recv_ref[pl.ds(rows - 1, recv_ref.shape[0] // rows, stride=rows), :], axis=0, keepdims=True)
    index = lax.broadcasted_iota(jnp.int32, (wide, LANES), 0)
    gram = jnp.where(index == 0, flat, 0.0)
    for k in range(1, hist):
        gram = jnp.where(index == k, pltpu.roll(flat, LANES - k * (hist + 1), 1), gram)
    cols = [jnp.broadcast_to(gram[:, j : j + 1], (wide, LANES)) for j in range(hist + 1)]

    def row_of(x, k):
        return jnp.broadcast_to(x[k : k + 1, :], (wide, LANES))

    trace = row_of(cols[0], 0)
    for k in range(1, hist):
        trace = trace + row_of(cols[k], k)
    ridge = 0.01 * (trace / hist)
    for k in range(hist):
        cols[k] = jnp.where(index == k, cols[k] + ridge, cols[k])
    for k in range(hist):
        inverse = 1.0 / row_of(cols[k], k)
        for j in range(k + 1, hist + 1):
            ratio = row_of(cols[j], k) * inverse
            cols[j] = jnp.where(index == k, ratio, cols[j] - cols[k] * ratio)
    weights = cols[hist]
    total = img_ref[hist * own_rows : (hist + 1) * own_rows, :]
    for k in range(hist):
        total = total - jnp.broadcast_to(weights[k : k + 1, :], (own_rows, LANES)) * img_ref[k * own_rows : (k + 1) * own_rows, :]
    part_ref[...] = total
    factors = jnp.where(index < hist, -weights, jnp.where(index == hist, 1.0, 0.0))
    for start in range(0, width, LANES):
        blend_ref[:, start : start + LANES] = jnp.sum(factors * dirs[:, start : start + LANES], axis=0, keepdims=True)


def mask_kernel(row_count, where_ref, ids_ref, target_ref, blend_ref, aux_ref):
    own_rows = aux_ref.shape[1]
    row = where_ref[0]
    first = row * own_rows
    ids = ids_ref[pl.ds(first, own_rows), :]
    before = ids_ref[pl.ds(jnp.maximum(first - 1, 0), 1), :]
    after = ids_ref[pl.ds(jnp.minimum(first + own_rows, ids_ref.shape[0] - 1), 1), :]
    before = jnp.broadcast_to(before[:, LANES - 1 :], (1, LANES))
    after = jnp.broadcast_to(after[:, 0:1], (1, LANES))
    opens = ((ids == before) & (row > 0)).astype(F32)
    aux_ref[TARGET] = target_ref[pl.ds(first, own_rows), :]
    aux_ref[FIRST] = opens
    aux_ref[LAST] = ((ids == after) & (row < row_count - 1)).astype(F32)
    for index, step in enumerate(SHIFTS):
        same = (shifted(ids, step) == ids).astype(F32)
        aux_ref[UPWARD + index] = same
        aux_ref[DOWNWARD + index] = (shifted(ids, -step) == ids).astype(F32)
        if step == 1:
            aux_ref[HEAD] = (1.0 - same) * (1.0 - opens)


def cone_kernel(count, *refs):
    parts = refs[:count]
    aux_ref, cat_ref, proj_ref, edge_ref, out_ref = refs[count:]
    own_rows = proj_ref.shape[0]
    width = out_ref.shape[1]
    slack = aux_ref[TARGET] - tree(p[...] for p in parts)
    head, first, last = aux_ref[HEAD], aux_ref[FIRST], aux_ref[LAST]
    square = (1.0 - head) * slack * slack
    lead, ahead, behind = head * slack, square, square
    for index, step in enumerate(SHIFTS):
        same = aux_ref[UPWARD + index]
        lead = lead + same * shifted(lead, step)
        ahead = ahead + same * shifted(ahead, step)
        behind = behind + aux_ref[DOWNWARD + index] * shifted(behind, -step)
    norm = jnp.sqrt(jnp.maximum(ahead + behind - square, 0.0))
    inside = norm <= lead
    killed = norm <= -lead
    safe = jnp.where(norm > 0, norm, 1.0)
    middle = 0.5 * (lead + norm)
    outside = jnp.where(head > 0, middle, middle * slack / safe)
    projected = jnp.where(inside, slack, jnp.where(killed, 0.0, outside))
    proj_ref[...] = projected
    correction = jnp.where(first + last > 0, 0.0, projected - slack)

    sub = lax.broadcasted_iota(jnp.int32, (TILE, LANES), 0)
    final = own_rows - 1
    begin = (first * slack)[0:1, :]
    tail = (last * (1.0 - head) * slack)[final:, :]
    lead = (last * head)[final:, :]
    closing = jnp.where(sub == TAIL_LAST, tail, jnp.where(sub == HEAD_LAST, lead, 0.0))
    opening = jnp.where(sub == TAIL_FIRST, begin, 0.0)
    pieces = []
    for piece in range(own_rows):
        base = piece // TILE * TILE
        interior = jnp.where(sub == piece % TILE, correction[base : base + TILE, :], 0.0)
        edge = opening if piece == 0 else closing if piece == final else jnp.zeros_like(opening)
        high = jnp.concatenate([interior, edge], axis=0).astype(BF16)
        low = (jnp.concatenate([interior, edge], axis=0) - high.astype(F32)).astype(BF16)
        pieces.append(jnp.concatenate([high, low], axis=0))
    left = jnp.concatenate(pieces, axis=1)
    both = jnp.dot(left, cat_ref[...], preferred_element_type=F32)
    half = 2 * TILE
    sums = both[0:half, 0:width] + both[0:half, width : 2 * width] + both[half : 2 * half, 0:width]
    ends = slack[final:, :]
    scalars = jnp.where(
        sub == SQUARE_LAST,
        tail * ends,
        jnp.where(sub == LEAD_LAST, lead * ends, jnp.where(sub == SQUARE_FIRST, begin * slack[0:1, :], 0.0)),
    )
    scalars = jnp.broadcast_to(jnp.sum(scalars, axis=1, keepdims=True), (TILE, width))
    wide_sub = lax.broadcasted_iota(jnp.int32, (TILE, width), 0)
    out_ref[...] = jnp.where(
        wide_sub == BACK,
        jnp.sum(sums[0:TILE, :], axis=0, keepdims=True),
        jnp.where(wide_sub <= TAIL_FIRST, sums[TILE:half, :], scalars),
    )
    edge_ref[...] = jnp.where(sub == 0, slack[0:1, :], ends)


def finish_kernel(scale_back, local, row_count, where_ref, *refs):
    messages = refs[:row_count]
    proj_ref, edge_ref, aux_ref, blend_ref, next_ref, out_ref = refs[row_count:]
    row = where_ref[0]
    own_rows, width = proj_ref.shape[0], blend_ref.shape[1]
    received = [m[...] for m in messages]
    blocks = []
    for block in range(row_count):
        mine = received[0]
        for turn in range(1, row_count):
            mine = jnp.where(lax.bitwise_xor(row, turn) == block, received[turn], mine)
        blocks.append(mine)
    total = tree(b[BACK : BACK + 1, :] for b in blocks)
    ones = jnp.ones((1, LANES), F32)
    zeros = jnp.zeros((1, LANES), F32)
    tail_last, lead_last, tail_first = ones, zeros, ones
    for block in range(row_count - 1):
        this, that = blocks[block], blocks[block + 1]
        lead = this[LEAD_LAST : LEAD_LAST + 1, :]
        norm = jnp.sqrt(this[SQUARE_LAST : SQUARE_LAST + 1, :] + that[SQUARE_FIRST : SQUARE_FIRST + 1, :])
        inside = norm <= lead
        killed = norm <= -lead
        safe = jnp.where(norm > 0, norm, 1.0)
        middle = 0.5 * (lead + norm)
        factor = jnp.where(inside, 1.0, jnp.where(killed, 0.0, middle / safe))
        new = jnp.where(inside, lead, jnp.where(killed, 0.0, middle))
        tails = this[TAIL_LAST : TAIL_LAST + 1, :] + that[TAIL_FIRST : TAIL_FIRST + 1, :]
        total = total + ((factor - 1.0) * tails + (new - lead) * this[HEAD_LAST : HEAD_LAST + 1, :])
        tail_last = jnp.where(row == block, factor[:, 0:LANES], tail_last)
        lead_last = jnp.where(row == block, new[:, 0:LANES], lead_last)
        tail_first = jnp.where(row == block + 1, factor[:, 0:LANES], tail_first)
    moved = blend_ref[...] - scale_back * total
    mine = moved[:, 0:local]
    for block in range(1, row_count):
        mine = jnp.where(row == block, moved[:, block * local : (block + 1) * local], mine)
    next_ref[...] = mine
    final = own_rows - 1
    begin, end = edge_ref[0:1, :], edge_ref[1:2, :]
    ahead = jnp.where(aux_ref[FIRST, 0:1, :] > 0, tail_first * begin, proj_ref[0:1, :])
    closing = jnp.where(aux_ref[HEAD, final : final + 1, :] > 0, lead_last, tail_last * end)
    closing = jnp.where(aux_ref[LAST, final : final + 1, :] > 0, closing, proj_ref[final : final + 1, :])
    sub = lax.broadcasted_iota(jnp.int32, (own_rows, LANES), 0)
    out_ref[...] = jnp.where(sub == 0, ahead, jnp.where(sub == final, closing, proj_ref[...]))


def exchange(x, axis, turns):
    count = lax.axis_size(axis)
    return [lax.ppermute(x, axis, [(i, i ^ turn) for i in range(count)]) for turn in turns]


def reduce_col(x, count):
    stages, bit = [[1]], 2
    while bit < count:
        stages.append([bit, 2 * bit, 3 * bit] if 2 * bit < count else [bit])
        bit *= 4
    for turns in stages[:-1]:
        x = tree([x, *exchange(x, "col", turns)])
    return [x, *exchange(x, "col", stages[-1])]


def body(iterates, residuals, operator, target, cone_id):
    row_count = lax.axis_size("row")
    col_count = lax.axis_size("col")
    row_block, width = operator.shape
    hist, local = iterates.shape[0] - 1, iterates.shape[1]
    all_rows = row_block * row_count
    scale_back = math.sqrt(local * row_count * col_count / all_rows)
    wide, _, rows = dims(hist, local)
    own_rows = row_block // LANES
    where = jnp.stack([lax.axis_index("row"), lax.axis_index("col")]).astype(jnp.int32)

    message = pl.pallas_call(
        functools.partial(pack_kernel, hist, local),
        name="pack",
        in_specs=[pl.BlockSpec(memory_space=pltpu.HBM)] * 2,
        out_specs=vmem(),
        out_shape=jax.ShapeDtypeStruct((row_count * col_count * rows, LANES), F32),
        scratch_shapes=[
            pltpu.VMEM((hist + 1, local), F32),
            pltpu.VMEM((hist + 1, local), F32),
            pltpu.VMEM((wide, LANES), F32),
            pltpu.VMEM((LANES, local), F32),
            pltpu.SemaphoreType.DMA((2,)),
        ],
        compiler_params=params(),
    )(hbm(iterates), hbm(residuals))
    received = lax.all_to_all(message, ("col", "row"), 0, 0, tiled=True)

    step = min(512, row_block)
    cat = pl.pallas_call(
        split_kernel,
        name="split",
        grid=(row_block // step,),
        in_specs=[pl.BlockSpec(memory_space=pl.ANY), pl.BlockSpec((step, width), lambda i: (i, 0))],
        out_specs=pl.BlockSpec((step, 2 * width), lambda i: (i, 0)),
        out_shape=jax.ShapeDtypeStruct((row_block, 2 * width), BF16),
        compiler_params=params(),
    )(message, hbm(operator))

    part, blended = pl.pallas_call(
        functools.partial(image_kernel, hist, local, row_count, step),
        name="image",
        in_specs=[smem(), vmem(), vmem()],
        out_specs=[vmem()] * 2,
        out_shape=[
            jax.ShapeDtypeStruct((own_rows, LANES), F32),
            jax.ShapeDtypeStruct((1, width), F32),
        ],
        scratch_shapes=[pltpu.VMEM((width // LANES, wide, LANES), F32), pltpu.VMEM(((hist + 1) * own_rows, LANES), F32)],
        compiler_params=params(),
    )(where, received, cat)

    aux = pl.pallas_call(
        functools.partial(mask_kernel, row_count),
        name="masks",
        in_specs=[smem(), vmem(), vmem(), vmem()],
        out_specs=vmem(),
        out_shape=jax.ShapeDtypeStruct((AUX, own_rows, LANES), F32),
        compiler_params=params(),
    )(where, cone_id.reshape(-1, LANES), target.reshape(-1, LANES), blended)

    parts = reduce_col(part, col_count)
    projected, edge, back = pl.pallas_call(
        functools.partial(cone_kernel, len(parts)),
        name="cones",
        in_specs=[vmem()] * (len(parts) + 2),
        out_specs=[vmem()] * 3,
        out_shape=[
            jax.ShapeDtypeStruct((own_rows, LANES), F32),
            jax.ShapeDtypeStruct((TILE, LANES), F32),
            jax.ShapeDtypeStruct((TILE, width), F32),
        ],
        compiler_params=params(),
    )(*parts, aux, cat)

    next_point, projected = pl.pallas_call(
        functools.partial(finish_kernel, scale_back, local, row_count),
        name="finish",
        in_specs=[smem()] + [vmem()] * (row_count + 4),
        out_specs=[vmem()] * 2,
        out_shape=[jax.ShapeDtypeStruct((1, local), F32), jax.ShapeDtypeStruct((own_rows, LANES), F32)],
        compiler_params=params(),
    )(where, back, *exchange(back, "row", range(1, row_count)), projected, edge, aux, blended)
    return (next_point.reshape(local), projected.reshape(row_block))


def solution(mesh):
    return jax.shard_map(
        body,
        mesh=mesh,
        in_specs=(P(None, ("col", "row")), P(None, ("col", "row")), P("row", "col"), P(), P()),
        out_specs=(P(("col", "row")), P("row")),
        check_vma=False,
    )
```

time: 39.3 us -> 34 us (0.87)
  waiting for transfers between devices: 15.5 us -> 7.59 us
  Pallas kernels: 2.42 us -> 10 us
  local copies, waits for them, and re-layouts: 3.57 us -> 0.01 us
  starting transfers between devices: 16.8 us -> 15.3 us
    ppermute x14 -> x7, waiting for transfers between devices: 15.5 us -> 4.4 us  [exchange(): lax.ppermute(x, axis, [(i, i ^ turn) for i in range(count)])]
    ppermute x14 -> x7, starting transfers between devices: 16.8 us -> 8.01 us  [exchange(): lax.ppermute(x, axis, [(i, i ^ turn) for i in range(count)])]
    all_to_all x0 -> x1, starting transfers between devices: none -> 7.33 us  [body(): received = lax.all_to_all(message, ('col', 'row'), 0, 0, tiled=True)]
    pallas_call x2 -> x4, Pallas kernels: 1.05 us -> 7.54 us  [the longest x1 4.19 us: body(): pl.pallas_call(split_kernel, name='split', grid=(row_block // step,), in_...]
    all_to_all x0 -> x1, waiting for transfers between devices: none -> 3.19 us  [body(): received = lax.all_to_all(message, ('col', 'row'), 0, 0, tiled=True)]
    unnamed x12 -> x4, local copies, waits for them, and re-layouts: 2.99 us -> 0.01 us
    pallas_call x1, Pallas kernels: 0.2 us -> 1.72 us  [body(): pl.pallas_call(functools.partial(pack_kernel, hist, local), name='pack',...]
    reshape x1 -> x0, local copies, waits for them, and re-layouts: 0.58 us -> none  [body(): return (next_point.reshape(local), projected.reshape(row_block))]
  transfers between devices with their start and end apart: 14 -> 8, of which waited for: 12 -> 7; matrix products, arithmetic and copies ran while one was open for 0% -> 0% of each run, Pallas kernels for 2% -> 14%
where the time goes in v2:
time: 34 us; the launch traced here: 33.7 us
  starting transfers between devices  15.3 us (45%)
  Pallas kernels  10 us (29%)
  waiting for transfers between devices  7.59 us (22%)
  between operations  0.71 us (2%)
    ppermute x7, starting transfers between devices, exchange(): lax.ppermute(x, axis, [(i, i ^ turn) for i in range(count)])  8.01 us
    all_to_all x1, starting transfers between devices, body(): received = lax.all_to_all(message, ('col', 'row'), 0, 0, tiled=True)  7.33 us
    ppermute x7, waiting for transfers between devices, exchange(): lax.ppermute(x, axis, [(i, i ^ turn) for i in range(count)])  4.4 us
    pallas_call x1, Pallas kernels, body(): pl.pallas_call(split_kernel, name='split', grid=(row_block // step,), in_...  4.19 us
    all_to_all x1, waiting for transfers between devices, body(): received = lax.all_to_all(message, ('col', 'row'), 0, 0, tiled=True)  3.19 us
    pallas_call x1, Pallas kernels, body(): pl.pallas_call(functools.partial(pack_kernel, hist, local), name='pack',...  1.72 us
    pallas_call x1, Pallas kernels, body(): pl.pallas_call(functools.partial(finish_kernel, scale_back, local, row_co...  1.37 us
    pallas_call x1, Pallas kernels, body(): pl.pallas_call(functools.partial(image_kernel, hist, local, row_count, st...  1.32 us
  transfers between devices with their start and end apart: 8, of which 7 were waited for; matrix products, arithmetic and copies ran while one was open for 0% of the time, Pallas kernels for 14%

profile of v2, /device:TPU:0, one launch (start us, length us, event | category | flops | bytes accessed | tf_op | source)
XLA Modules:
  0.0 33.7 jit_solution(15390862559253611300)
XLA Ops:
  0.6 1.7 %pack.1.message_any = f32[128,128]{1,0:T(8,128)} custom-call(f32[11,32]{1,0:T(8,128)} %x_any.1, f32[11,32]{1,0:T(8,128)} %f_any.1), custom_call_target="tpu_custom_call" | custom-call | tf_op jit(solution)/shard_map/pack/pallas_call | solution.py:316
  2.4 7.3 %all-to-all-start = ((f32[32,4,128]{2,1,0:T(4,128)}), f32[32,4,128]{2,1,0:T(4,128)S(1)}, u32[]{:S(2)}, u32[]{:S(2)}) async-start(f32[32,4,128]{2,1,0:T(4,128)} %bitcast.2), calls=%async_computation | async-start | bytes 131072 | tf_op jit(solution)/shard_map/all_to_all | solution.py:331
  9.7 4.2 %split.1.cat_ref.refs_5_ = bf16[4096,256]{1,0:T(8,128)(2,1)S(1)} custom-call(f32[128,128]{1,0:T(8,128)} %pack.1.message_any, f32[4096,128]{1,0:T(8,128)} %oper_ref.1), custom_call_target="tpu_custom_call" | custom-call | tf_op jit(solution)/shard_map/split/pallas_call | solution.py:334
  13.9 0.0 copy-start
  13.9 0.0 copy-start.1
  13.9 0.1 pad_add_fusion.where_ref
  14.0 3.2 %all-to-all-done = f32[32,4,128]{2,1,0:T(4,128)S(1)} async-done(((f32[32,4,128]{2,1,0:T(4,128)}), f32[32,4,128]{2,1,0:T(4,128)S(1)}, u32[]{:S(2)}, u32[]{:S(2)}) %all-to-all-start) | async-done | bytes 65568 | tf_op jit(solution)/shard_map/all_to_all | solution.py:331
  17.2 1.3 %image.1 = (f32[32,128]{1,0:T(8,128)S(1)}, f32[1,128]{1,0:T(1,128)S(1)}) custom-call(s32[2]{0:T(128)S(1)} %pad_add_fusion.where_ref, f32[128,128]{1,0:T(8,128)S(1)} %bitcast.8, bf16[4096,256]{1,0:T(8,128)(2,1)S(1)} %split.1.cat_ref.refs_5_), custom_call_target="tpu_custom_call" | custom-call | tf_op jit(solution)/shard_map/image/pallas_call | solution.py:344
  18.5 0.1 collective-permute-start
  18.6 1.2 %collective-permute-done = f32[32,128]{1,0:T(8,128)S(1)} collective-permute-done((f32[32,128]{1,0:T(8,128)S(1)}, f32[32,128]{1,0:T(8,128)S(1)}, u32[]{:S(2)}, u32[]{:S(2)}) %collective-permute-start) | collective-permute-done | bytes 16416 | tf_op jit(solution)/shard_map/ppermute | solution.py:292
  19.8 0.9 %collective-permute-start.3 = (f32[32,128]{1,0:T(8,128)S(1)}, f32[32,128]{1,0:T(8,128)S(1)}, u32[]{:S(2)}, u32[]{:S(2)}) collective-permute-start(f32[32,128]{1,0:T(8,128)S(1)} %add.3.refs_0_), channel_id=1, source_target_pairs={{0,6},{1,7},{2,4},{3,5},{4,2},{5,3},{6,0},{7,1},{8,14},{9,15},{10,... | collective-permute-start | bytes 49160 | tf_op jit(solution)/shard_map/ppermute | solution.py:292
  20.6 1.2 %collective-permute-start.2 = (f32[32,128]{1,0:T(8,128)S(1)}, f32[32,128]{1,0:T(8,128)S(1)}, u32[]{:S(2)}, u32[]{:S(2)}) collective-permute-start(f32[32,128]{1,0:T(8,128)S(1)} %add.3.refs_0_), channel_id=1, source_target_pairs={{0,4},{1,5},{2,6},{3,7},{4,0},{5,1},{6,2},{7,3},{8,12},{9,13},{10,... | collective-permute-start | bytes 49160 | tf_op jit(solution)/shard_map/ppermute | solution.py:292
  21.8 2.3 %collective-permute-start.1 = (f32[32,128]{1,0:T(8,128)S(1)}, f32[32,128]{1,0:T(8,128)S(1)}, u32[]{:S(2)}, u32[]{:S(2)}) collective-permute-start(f32[32,128]{1,0:T(8,128)S(1)} %add.3.refs_0_), channel_id=1, source_target_pairs={{0,2},{1,3},{2,0},{3,1},{4,6},{5,7},{6,4},{7,5},{8,10},{9,11},{10,... | collective-permute-start | bytes 49160 | tf_op jit(solution)/shard_map/ppermute | solution.py:292
  24.2 0.0 copy-done
  24.2 0.0 copy-done.1
  24.2 0.7 %masks.1.refs_4_.refs_6_ = f32[12,32,128]{2,1,0:T(8,128)S(1)} custom-call(s32[2]{0:T(128)S(1)} %pad_add_fusion.where_ref, s32[128,128]{1,0:T(8,128)S(1)} %bitcast.9, f32[128,128]{1,0:T(8,128)S(1)} %bitcast.10, f32[1,128]{1,0:T(1,128)S(1)} %get-tuple-element.10.blend_ref.refs_7_), custom_call_target="tpu_custom_call" | custom-call | tf_op jit(solution)/shard_map/masks/pallas_call | solution.py:357
  24.8 0.6 %collective-permute-done.3.refs_3_ = f32[32,128]{1,0:T(8,128)S(1)} collective-permute-done((f32[32,128]{1,0:T(8,128)S(1)}, f32[32,128]{1,0:T(8,128)S(1)}, u32[]{:S(2)}, u32[]{:S(2)}) %collective-permute-start.3) | collective-permute-done | bytes 16416 | tf_op jit(solution)/shard_map/ppermute | solution.py:292
  25.4 0.0 collective-permute-done.2.refs_2_
  25.4 0.4 %collective-permute-done.1.refs_1_ = f32[32,128]{1,0:T(8,128)S(1)} collective-permute-done((f32[32,128]{1,0:T(8,128)S(1)}, f32[32,128]{1,0:T(8,128)S(1)}, u32[]{:S(2)}, u32[]{:S(2)}) %collective-permute-start.1) | collective-permute-done | bytes 16416 | tf_op jit(solution)/shard_map/ppermute | solution.py:292
  25.9 0.7 %cones.1 = (f32[32,128]{1,0:T(8,128)S(1)}, f32[8,128]{1,0:T(8,128)S(1)}, f32[8,128]{1,0:T(8,128)S(1)}) custom-call(f32[32,128]{1,0:T(8,128)S(1)} %add.3.refs_0_, f32[32,128]{1,0:T(8,128)S(1)} %collective-permute-done.1.refs_1_, f32[32,128]{1,0:T(8,128)S(1)} %collective-permute-done.2.refs_2_, f32[32,128]{1,0:T(8,128)S(1)} %collective-permute-done.3.refs_3_, ...), custom_call_target="tpu_custom_call" | custom-call | tf_op jit(solution)/shard_map/cones/pallas_call | solution.py:367
  26.6 1.4 %collective-permute-start.6 = (f32[8,128]{1,0:T(8,128)S(1)}, f32[8,128]{1,0:T(8,128)S(1)}, u32[]{:S(2)}, u32[]{:S(2)}) collective-permute-start(f32[8,128]{1,0:T(8,128)S(1)} %get-tuple-element.11.refs_0_), channel_id=1, source_target_pairs={{0,24},{8,16},{16,8},{24,0},{1,25},{9,17},{17,9},{25,1},{2,26},{10... | collective-permute-start | bytes 12296 | tf_op jit(solution)/shard_map/ppermute | solution.py:292
  28.1 0.7 %collective-permute-start.5 = (f32[8,128]{1,0:T(8,128)S(1)}, f32[8,128]{1,0:T(8,128)S(1)}, u32[]{:S(2)}, u32[]{:S(2)}) collective-permute-start(f32[8,128]{1,0:T(8,128)S(1)} %get-tuple-element.11.refs_0_), channel_id=1, source_target_pairs={{0,16},{8,24},{16,0},{24,8},{1,17},{9,25},{17,1},{25,9},{2,18},{10... | collective-permute-start | bytes 12296 | tf_op jit(solution)/shard_map/ppermute | solution.py:292
  28.8 1.4 %collective-permute-start.4 = (f32[8,128]{1,0:T(8,128)S(1)}, f32[8,128]{1,0:T(8,128)S(1)}, u32[]{:S(2)}, u32[]{:S(2)}) collective-permute-start(f32[8,128]{1,0:T(8,128)S(1)} %get-tuple-element.11.refs_0_), channel_id=1, source_target_pairs={{0,8},{8,0},{16,24},{24,16},{1,9},{9,1},{17,25},{25,17},{2,10},{10... | collective-permute-start | bytes 12296 | tf_op jit(solution)/shard_map/ppermute | solution.py:292
  30.2 1.0 %collective-permute-done.6.refs_3_ = f32[8,128]{1,0:T(8,128)S(1)} collective-permute-done((f32[8,128]{1,0:T(8,128)S(1)}, f32[8,128]{1,0:T(8,128)S(1)}, u32[]{:S(2)}, u32[]{:S(2)}) %collective-permute-start.6) | collective-permute-done | bytes 4128 | tf_op jit(solution)/shard_map/ppermute | solution.py:292
  31.2 0.5 %collective-permute-done.5.refs_2_ = f32[8,128]{1,0:T(8,128)S(1)} collective-permute-done((f32[8,128]{1,0:T(8,128)S(1)}, f32[8,128]{1,0:T(8,128)S(1)}, u32[]{:S(2)}, u32[]{:S(2)}) %collective-permute-start.5) | collective-permute-done | bytes 4128 | tf_op jit(solution)/shard_map/ppermute | solution.py:292
  31.7 0.7 %collective-permute-done.4.refs_1_ = f32[8,128]{1,0:T(8,128)S(1)} collective-permute-done((f32[8,128]{1,0:T(8,128)S(1)}, f32[8,128]{1,0:T(8,128)S(1)}, u32[]{:S(2)}, u32[]{:S(2)}) %collective-permute-start.4) | collective-permute-done | bytes 4128 | tf_op jit(solution)/shard_map/ppermute | solution.py:292
  32.4 1.4 %finish.1 = (f32[1,32]{1,0:T(1,128)}, f32[32,128]{1,0:T(8,128)}) custom-call(s32[2]{0:T(128)S(1)} %pad_add_fusion.where_ref, f32[8,128]{1,0:T(8,128)S(1)} %get-tuple-element.11.refs_0_, f32[8,128]{1,0:T(8,128)S(1)} %collective-permute-done.4.refs_1_, f32[8,128]{1,0:T(8,128)S(1)} %collective-permute-done.5.refs_2_, ...), custom_call_target="tpu_custom_call" | custom-call | tf_op jit(solution)/shard_map/finish/pallas_call | solution.py:380
  (1 shorter events, 0.0 us)
Async XLA Ops:
  2.4 14.8 %all-to-all-start = ((f32[32,4,128]{2,1,0:T(4,128)}), f32[32,4,128]{2,1,0:T(4,128)S(1)}, u32[]{:S(2)}, u32[]{:S(2)}) async-start(f32[32,4,128]{2,1,0:T(4,128)} %bitcast.2), calls=%async_computation | async-start | bytes 131072 | tf_op jit(solution)/shard_map/all_to_all | solution.py:331
  13.9 10.3 %copy-start = (s32[16384]{0:T(1024)S(1)}, s32[16384]{0:T(1024)}, u32[]{:S(2)}) copy-start(s32[16384]{0:T(1024)} %param.9) | copy-start | bytes 196612
  13.9 10.3 %copy-start.1 = (f32[16384]{0:T(1024)S(1)}, f32[16384]{0:T(1024)}, u32[]{:S(2)}) copy-start(f32[16384]{0:T(1024)} %param.8) | copy-start | bytes 196612
  18.5 1.2 %collective-permute-start = (f32[32,128]{1,0:T(8,128)S(1)}, f32[32,128]{1,0:T(8,128)S(1)}, u32[]{:S(2)}, u32[]{:S(2)}) collective-permute-start(f32[32,128]{1,0:T(8,128)S(1)} %get-tuple-element.9), channel_id=1, source_target_pairs={{0,1},{1,0},{2,3},{3,2},{4,5},{5,4},{6,7},{7,6},{8,9},{9,8},{10,11... | collective-permute-start | bytes 49160 | tf_op jit(solution)/shard_map/ppermute | solution.py:292
  19.8 5.7 %collective-permute-start.3 = (f32[32,128]{1,0:T(8,128)S(1)}, f32[32,128]{1,0:T(8,128)S(1)}, u32[]{:S(2)}, u32[]{:S(2)}) collective-permute-start(f32[32,128]{1,0:T(8,128)S(1)} %add.3.refs_0_), channel_id=1, source_target_pairs={{0,6},{1,7},{2,4},{3,5},{4,2},{5,3},{6,0},{7,1},{8,14},{9,15},{10,... | collective-permute-start | bytes 49160 | tf_op jit(solution)/shard_map/ppermute | solution.py:292
  20.6 4.8 %collective-permute-start.2 = (f32[32,128]{1,0:T(8,128)S(1)}, f32[32,128]{1,0:T(8,128)S(1)}, u32[]{:S(2)}, u32[]{:S(2)}) collective-permute-start(f32[32,128]{1,0:T(8,128)S(1)} %add.3.refs_0_), channel_id=1, source_target_pairs={{0,4},{1,5},{2,6},{3,7},{4,0},{5,1},{6,2},{7,3},{8,12},{9,13},{10,... | collective-permute-start | bytes 49160 | tf_op jit(solution)/shard_map/ppermute | solution.py:292
  21.8 4.0 %collective-permute-start.1 = (f32[32,128]{1,0:T(8,128)S(1)}, f32[32,128]{1,0:T(8,128)S(1)}, u32[]{:S(2)}, u32[]{:S(2)}) collective-permute-start(f32[32,128]{1,0:T(8,128)S(1)} %add.3.refs_0_), channel_id=1, source_target_pairs={{0,2},{1,3},{2,0},{3,1},{4,6},{5,7},{6,4},{7,5},{8,10},{9,11},{10,... | collective-permute-start | bytes 49160 | tf_op jit(solution)/shard_map/ppermute | solution.py:292
  26.6 4.6 %collective-permute-start.6 = (f32[8,128]{1,0:T(8,128)S(1)}, f32[8,128]{1,0:T(8,128)S(1)}, u32[]{:S(2)}, u32[]{:S(2)}) collective-permute-start(f32[8,128]{1,0:T(8,128)S(1)} %get-tuple-element.11.refs_0_), channel_id=1, source_target_pairs={{0,24},{8,16},{16,8},{24,0},{1,25},{9,17},{17,9},{25,1},{2,26},{10... | collective-permute-start | bytes 12296 | tf_op jit(solution)/shard_map/ppermute | solution.py:292
  28.1 3.6 %collective-permute-start.5 = (f32[8,128]{1,0:T(8,128)S(1)}, f32[8,128]{1,0:T(8,128)S(1)}, u32[]{:S(2)}, u32[]{:S(2)}) collective-permute-start(f32[8,128]{1,0:T(8,128)S(1)} %get-tuple-element.11.refs_0_), channel_id=1, source_target_pairs={{0,16},{8,24},{16,0},{24,8},{1,17},{9,25},{17,1},{25,9},{2,18},{10... | collective-permute-start | bytes 12296 | tf_op jit(solution)/shard_map/ppermute | solution.py:292
  28.8 3.6 %collective-permute-start.4 = (f32[8,128]{1,0:T(8,128)S(1)}, f32[8,128]{1,0:T(8,128)S(1)}, u32[]{:S(2)}, u32[]{:S(2)}) collective-permute-start(f32[8,128]{1,0:T(8,128)S(1)} %get-tuple-element.11.refs_0_), channel_id=1, source_target_pairs={{0,8},{8,0},{16,24},{24,16},{1,9},{9,1},{17,25},{25,17},{2,10},{10... | collective-permute-start | bytes 12296 | tf_op jit(solution)/shard_map/ppermute | solution.py:292

commit v3 on v2

--- a/solution.py
+++ b/solution.py
@@ -26,10 +26,6 @@
 
 def vmem():
     return pl.BlockSpec(memory_space=pltpu.VMEM)
-
-
-def smem():
-    return pl.BlockSpec(memory_space=pltpu.SMEM)
 
 
 def hbm(x):
@@ -94,18 +90,11 @@
         out_ref[start : start + TILE, :] = message
 
 
-def split_kernel(message_any, oper_ref, cat_ref):
-    width = oper_ref.shape[1]
-    high, low = split(oper_ref[...])
-    cat_ref[:, 0:width] = high
-    cat_ref[:, width : 2 * width] = low
-
-
-def image_kernel(hist, local, row_count, chunk, where_ref, recv_ref, cat_ref, part_ref, blend_ref, dirs_ref, img_ref):
+def image_kernel(hist, local, row_count, chunk, recv_ref, oper_ref, cat_ref, part_ref, blend_ref, dirs_ref, img_ref):
     wide, group, rows = dims(hist, local)
-    row_block, width = cat_ref.shape[0], cat_ref.shape[1] // 2
+    row_block, width = oper_ref.shape
     own_rows = row_block // LANES
-    mine = recv_ref[pl.ds(pl.multiple_of(where_ref[1] * (row_count * rows), TILE), row_count * rows), :]
+    mine = recv_ref[pl.ds(pl.multiple_of(lax.axis_index("col") * (row_count * rows), TILE), row_count * rows), :]
     lane = lax.broadcasted_iota(jnp.int32, (rows, LANES), 1)
     for start in range(0, width, LANES):
         for place in range(group):
@@ -125,7 +114,10 @@
         [jnp.concatenate([high, high], axis=1), jnp.concatenate([low, jnp.zeros_like(low)], axis=1)], axis=0
     )
     for start in range(0, row_block, chunk):
-        both = lax.dot_general(left, cat_ref[start : start + chunk, :], NT, preferred_element_type=F32)
+        high, low = split(oper_ref[start : start + chunk, :])
+        cat_ref[start : start + chunk, 0:width] = high
+        cat_ref[start : start + chunk, width : 2 * width] = low
+        both = lax.dot_general(left, jnp.concatenate([high, low], axis=1), NT, preferred_element_type=F32)
         image = both[0:wide, :] + both[wide : 2 * wide, :]
         for piece in range(chunk // LANES):
             tile = image[:, piece * LANES : (piece + 1) * LANES]
@@ -162,9 +154,9 @@
         blend_ref[:, start : start + LANES] = jnp.sum(factors * dirs[:, start : start + LANES], axis=0, keepdims=True)
 
 
-def mask_kernel(row_count, where_ref, ids_ref, target_ref, blend_ref, aux_ref):
+def mask_kernel(row_count, ids_ref, target_ref, blend_ref, aux_ref):
     own_rows = aux_ref.shape[1]
-    row = where_ref[0]
+    row = lax.axis_index("row")
     first = row * own_rows
     ids = ids_ref[pl.ds(first, own_rows), :]
     before = ids_ref[pl.ds(jnp.maximum(first - 1, 0), 1), :]
@@ -242,10 +234,10 @@
     edge_ref[...] = jnp.where(sub == 0, slack[0:1, :], ends)
 
 
-def finish_kernel(scale_back, local, row_count, where_ref, *refs):
+def finish_kernel(scale_back, local, row_count, *refs):
     messages = refs[:row_count]
     proj_ref, edge_ref, aux_ref, blend_ref, next_ref, out_ref = refs[row_count:]
-    row = where_ref[0]
+    row = lax.axis_index("row")
     own_rows, width = proj_ref.shape[0], blend_ref.shape[1]
     received = [m[...] for m in messages]
     blocks = []
@@ -293,13 +285,19 @@
 
 
 def reduce_col(x, count):
-    stages, bit = [[1]], 2
+    core = lax.axis_index("col") % 2
+    terms, bit = [x, *exchange(x, "col", [1])], 2
     while bit < count:
-        stages.append([bit, 2 * bit, 3 * bit] if 2 * bit < count else [bit])
+        x = tree(terms)
+        if 2 * bit < count:
+            far = lax.ppermute(x, "col", [(i, i ^ (3 * bit if i % 2 else bit)) for i in range(count)])
+            near = lax.ppermute(x, "col", [(i, i ^ (2 * bit if i % 2 else bit)) for i in range(count)])
+            x = near + jnp.where(core == 1, far, x)
+            terms = [x, *exchange(x, "col", [1])]
+        else:
+            terms = [x, *exchange(x, "col", [bit])]
         bit *= 4
-    for turns in stages[:-1]:
-        x = tree([x, *exchange(x, "col", turns)])
-    return [x, *exchange(x, "col", stages[-1])]
+    return terms
 
 
 def body(iterates, residuals, operator, target, cone_id):
@@ -311,7 +309,6 @@
     scale_back = math.sqrt(local * row_count * col_count / all_rows)
     wide, _, rows = dims(hist, local)
     own_rows = row_block // LANES
-    where = jnp.stack([lax.axis_index("row"), lax.axis_index("col")]).astype(jnp.int32)
 
     message = pl.pallas_call(
         functools.partial(pack_kernel, hist, local),
@@ -326,42 +323,33 @@
             pltpu.VMEM((LANES, local), F32),
             pltpu.SemaphoreType.DMA((2,)),
         ],
+        cost_estimate=pl.CostEstimate(flops=10**10, bytes_accessed=4 * 10**7, transcendentals=0),
         compiler_params=params(),
     )(hbm(iterates), hbm(residuals))
     received = lax.all_to_all(message, ("col", "row"), 0, 0, tiled=True)
 
-    step = min(512, row_block)
-    cat = pl.pallas_call(
-        split_kernel,
-        name="split",
-        grid=(row_block // step,),
-        in_specs=[pl.BlockSpec(memory_space=pl.ANY), pl.BlockSpec((step, width), lambda i: (i, 0))],
-        out_specs=pl.BlockSpec((step, 2 * width), lambda i: (i, 0)),
-        out_shape=jax.ShapeDtypeStruct((row_block, 2 * width), BF16),
-        compiler_params=params(),
-    )(message, hbm(operator))
-
-    part, blended = pl.pallas_call(
-        functools.partial(image_kernel, hist, local, row_count, step),
+    cat, part, blended = pl.pallas_call(
+        functools.partial(image_kernel, hist, local, row_count, min(512, row_block)),
         name="image",
-        in_specs=[smem(), vmem(), vmem()],
-        out_specs=[vmem()] * 2,
+        in_specs=[vmem()] * 2,
+        out_specs=[vmem()] * 3,
         out_shape=[
+            jax.ShapeDtypeStruct((row_block, 2 * width), BF16),
             jax.ShapeDtypeStruct((own_rows, LANES), F32),
             jax.ShapeDtypeStruct((1, width), F32),
         ],
         scratch_shapes=[pltpu.VMEM((width // LANES, wide, LANES), F32), pltpu.VMEM(((hist + 1) * own_rows, LANES), F32)],
         compiler_params=params(),
-    )(where, received, cat)
+    )(received, operator)
 
     aux = pl.pallas_call(
         functools.partial(mask_kernel, row_count),
         name="masks",
-        in_specs=[smem(), vmem(), vmem(), vmem()],
+        in_specs=[vmem()] * 3,
         out_specs=vmem(),
         out_shape=jax.ShapeDtypeStruct((AUX, own_rows, LANES), F32),
         compiler_params=params(),
-    )(where, cone_id.reshape(-1, LANES), target.reshape(-1, LANES), blended)
+    )(cone_id.reshape(-1, LANES), target.reshape(-1, LANES), blended)
 
     parts = reduce_col(part, col_count)
     projected, edge, back = pl.pallas_call(
@@ -380,11 +368,11 @@
     next_point, projected = pl.pallas_call(
         functools.partial(finish_kernel, scale_back, local, row_count),
         name="finish",
-        in_specs=[smem()] + [vmem()] * (row_count + 4),
+        in_specs=[vmem()] * (row_count + 4),
         out_specs=[vmem()] * 2,
         out_shape=[jax.ShapeDtypeStruct((1, local), F32), jax.ShapeDtypeStruct((own_rows, LANES), F32)],
         compiler_params=params(),
-    )(where, back, *exchange(back, "row", range(1, row_count)), projected, edge, aux, blended)
+    )(back, *exchange(back, "row", range(1, row_count)), projected, edge, aux, blended)
     return (next_point.reshape(local), projected.reshape(row_block))
 
 

time: 34 us -> 31.6 us (0.929)
  blocking collectives: 0 us -> 14.6 us
  starting transfers between devices: 15.3 us -> 5.79 us
  Pallas kernels: 10 us -> 3.79 us
  waiting for transfers between devices: 7.59 us -> 6.43 us
    all_to_all x0 -> x1, blocking collectives: none -> 14.6 us  [body(): received = lax.all_to_all(message, ('col', 'row'), 0, 0, tiled=True)]
    all_to_all x1 -> x0, starting transfers between devices: 7.33 us -> none  [body(): received = lax.all_to_all(message, ('col', 'row'), 0, 0, tiled=True)]
    pallas_call x2 -> x1, Pallas kernels: 5.51 us -> 0.87 us  [body(): pl.pallas_call(functools.partial(image_kernel, hist, local, row_count, mi...]
    ppermute x7 -> x5, starting transfers between devices: 8.01 us -> 3.76 us  [exchange(): lax.ppermute(x, axis, [(i, i ^ turn) for i in range(count)])]
    all_to_all x1 -> x0, waiting for transfers between devices: 3.19 us -> none  [body(): received = lax.all_to_all(message, ('col', 'row'), 0, 0, tiled=True)]
    ppermute x0 -> x2, waiting for transfers between devices: none -> 2.5 us  [the longest x1 1.71 us: reduce_col(): lax.ppermute(x, 'col', [(i, i ^ (3 * bit if i % 2 else bit)) for i in ran...]
    ppermute x0 -> x2, starting transfers between devices: none -> 2.03 us  [the longest x1 1.42 us: reduce_col(): lax.ppermute(x, 'col', [(i, i ^ (2 * bit if i % 2 else bit)) for i in ran...]
    pallas_call x1, Pallas kernels: 1.37 us -> 0.83 us  [body(): pl.pallas_call(functools.partial(finish_kernel, scale_back, local, row_co...]
  transfers between devices with their start and end apart: 8 -> 7, of which waited for: 7 -> 6; matrix products, arithmetic and copies ran while one was open for 0% -> 0% of each run, Pallas kernels for 14% -> 0%
where the time goes in v3:
time: 31.6 us; the launch traced here: 31.4 us
  blocking collectives  14.6 us (46%)
  waiting for transfers between devices  6.43 us (20%)
  starting transfers between devices  5.79 us (18%)
  Pallas kernels  3.79 us (12%)
  between operations  0.7 us (2%)
    all_to_all x1, blocking collectives, body(): received = lax.all_to_all(message, ('col', 'row'), 0, 0, tiled=True)  14.6 us
    ppermute x5, waiting for transfers between devices, exchange(): lax.ppermute(x, axis, [(i, i ^ turn) for i in range(count)])  3.94 us
    ppermute x5, starting transfers between devices, exchange(): lax.ppermute(x, axis, [(i, i ^ turn) for i in range(count)])  3.76 us
    ppermute x1, waiting for transfers between devices, reduce_col(): lax.ppermute(x, 'col', [(i, i ^ (3 * bit if i % 2 else bit)) for i in ran...  1.71 us
    ppermute x1, starting transfers between devices, reduce_col(): lax.ppermute(x, 'col', [(i, i ^ (2 * bit if i % 2 else bit)) for i in ran...  1.42 us
    pallas_call x1, Pallas kernels, body(): pl.pallas_call(functools.partial(pack_kernel, hist, local), name='pack',...  1.25 us
    pallas_call x1, Pallas kernels, body(): pl.pallas_call(functools.partial(image_kernel, hist, local, row_count, mi...  0.87 us
    pallas_call x1, Pallas kernels, body(): pl.pallas_call(functools.partial(finish_kernel, scale_back, local, row_co...  0.83 us
  transfers between devices with their start and end apart: 7, of which 6 were waited for; matrix products, arithmetic and copies ran while one was open for 0% of the time, Pallas kernels for 0%

profile of v3, /device:TPU:0, one launch (start us, length us, event | category | flops | bytes accessed | tf_op | source)
XLA Modules:
  0.0 31.4 jit_solution(4917739767678690145)
XLA Ops:
  0.6 0.0 copy-start
  0.6 1.2 %pack.1 = f32[128,128]{1,0:T(8,128)S(1)} custom-call(f32[11,32]{1,0:T(8,128)} %x_any.1, f32[11,32]{1,0:T(8,128)} %f_any.1), custom_call_target="tpu_custom_call" | custom-call | flops 10000000000 | bytes 40000000 | tf_op jit(solution)/shard_map/pack/pallas_call | solution.py:313
  1.9 0.0 copy-start.1
  1.9 0.0 copy-start.2
  1.9 14.6 %all_to_all.11 = f32[32,4,128]{2,1,0:T(4,128)S(1)} all-to-all(f32[32,4,128]{2,1,0:T(4,128)S(1)} %bitcast.9), channel_id=1, replica_groups=mesh['row'=4,'col'=8] {'col','row'}, dimensions={0} | all-to-all | bytes 131072 | tf_op jit(solution)/shard_map/all_to_all | solution.py:329
  16.5 0.0 copy-done
  16.6 0.9 %image.1 = (bf16[4096,256]{1,0:T(8,128)(2,1)S(1)}, f32[32,128]{1,0:T(8,128)S(1)}, f32[1,128]{1,0:T(1,128)S(1)}) custom-call(f32[128,128]{1,0:T(8,128)S(1)} %bitcast.6, f32[4096,128]{1,0:T(8,128)S(1)} %copy-done), custom_call_target="tpu_custom_call" | custom-call | tf_op jit(solution)/shard_map/image/pallas_call | solution.py:331
  17.4 0.1 collective-permute-start
  17.5 1.2 %collective-permute-done = f32[32,128]{1,0:T(8,128)S(1)} collective-permute-done((f32[32,128]{1,0:T(8,128)S(1)}, f32[32,128]{1,0:T(8,128)S(1)}, u32[]{:S(2)}, u32[]{:S(2)}) %collective-permute-start) | collective-permute-done | bytes 16416 | tf_op jit(solution)/shard_map/ppermute | solution.py:284
  18.7 0.6 %collective-permute-start.2 = (f32[32,128]{1,0:T(8,128)S(1)}, f32[32,128]{1,0:T(8,128)S(1)}, u32[]{:S(2)}, u32[]{:S(2)}) collective-permute-start(f32[32,128]{1,0:T(8,128)S(1)} %add.10), channel_id=1, source_target_pairs={{0,2},{1,7},{2,0},{3,5},{4,6},{5,3},{6,4},{7,1},{8,10},{9,15},{10,... | collective-permute-start | bytes 49160 | tf_op jit(solution)/shard_map/ppermute | solution.py:293
  19.3 1.4 %collective-permute-start.1 = (f32[32,128]{1,0:T(8,128)S(1)}, f32[32,128]{1,0:T(8,128)S(1)}, u32[]{:S(2)}, u32[]{:S(2)}) collective-permute-start(f32[32,128]{1,0:T(8,128)S(1)} %add.10), channel_id=1, source_target_pairs={{0,2},{1,5},{2,0},{3,7},{4,6},{5,1},{6,4},{7,3},{8,10},{9,13},{10,... | collective-permute-start | bytes 49160 | tf_op jit(solution)/shard_map/ppermute | solution.py:294
  20.7 1.7 %collective-permute-done.2 = f32[32,128]{1,0:T(8,128)S(1)} collective-permute-done((f32[32,128]{1,0:T(8,128)S(1)}, f32[32,128]{1,0:T(8,128)S(1)}, u32[]{:S(2)}, u32[]{:S(2)}) %collective-permute-start.2) | collective-permute-done | bytes 16416 | tf_op jit(solution)/shard_map/ppermute | solution.py:293
  22.4 0.8 %collective-permute-done.1 = f32[32,128]{1,0:T(8,128)S(1)} collective-permute-done((f32[32,128]{1,0:T(8,128)S(1)}, f32[32,128]{1,0:T(8,128)S(1)}, u32[]{:S(2)}, u32[]{:S(2)}) %collective-permute-start.1) | collective-permute-done | bytes 16416 | tf_op jit(solution)/shard_map/ppermute | solution.py:294
  23.2 0.1 collective-permute-start.3
  23.3 0.0 copy-done.1
  23.3 0.0 copy-done.2
  23.3 0.1 masks.1.refs_2_.refs_6_
  23.5 0.9 %collective-permute-done.3.refs_1_ = f32[32,128]{1,0:T(8,128)S(1)} collective-permute-done((f32[32,128]{1,0:T(8,128)S(1)}, f32[32,128]{1,0:T(8,128)S(1)}, u32[]{:S(2)}, u32[]{:S(2)}) %collective-permute-start.3) | collective-permute-done | bytes 16416 | tf_op jit(solution)/shard_map/ppermute | solution.py:284
  24.4 0.7 %cones.1 = (f32[32,128]{1,0:T(8,128)S(1)}, f32[8,128]{1,0:T(8,128)S(1)}, f32[8,128]{1,0:T(8,128)S(1)}) custom-call(f32[32,128]{1,0:T(8,128)S(1)} %select_add_fusion.refs_0_, f32[32,128]{1,0:T(8,128)S(1)} %collective-permute-done.3.refs_1_, f32[12,32,128]{2,1,0:T(8,128)S(1)} %masks.1.refs_2_.refs_6_, bf16[4096,256]{1,0:T(8,128)(2,1)S(1)} %get-tuple-element.12.refs_3_), custom_call_target="tpu_custom_call" | custom-call | tf_op jit(solution)/shard_map/cones/pallas_call | solution.py:355
  25.1 0.7 %collective-permute-start.6 = (f32[8,128]{1,0:T(8,128)S(1)}, f32[8,128]{1,0:T(8,128)S(1)}, u32[]{:S(2)}, u32[]{:S(2)}) collective-permute-start(f32[8,128]{1,0:T(8,128)S(1)} %get-tuple-element.13.refs_0_), channel_id=1, source_target_pairs={{0,24},{8,16},{16,8},{24,0},{1,25},{9,17},{17,9},{25,1},{2,26},{10... | collective-permute-start | bytes 12296 | tf_op jit(solution)/shard_map/ppermute | solution.py:284
  25.9 1.1 %collective-permute-start.5 = (f32[8,128]{1,0:T(8,128)S(1)}, f32[8,128]{1,0:T(8,128)S(1)}, u32[]{:S(2)}, u32[]{:S(2)}) collective-permute-start(f32[8,128]{1,0:T(8,128)S(1)} %get-tuple-element.13.refs_0_), channel_id=1, source_target_pairs={{0,16},{8,24},{16,0},{24,8},{1,17},{9,25},{17,1},{25,9},{2,18},{10... | collective-permute-start | bytes 12296 | tf_op jit(solution)/shard_map/ppermute | solution.py:284
  26.9 1.8 %collective-permute-start.4 = (f32[8,128]{1,0:T(8,128)S(1)}, f32[8,128]{1,0:T(8,128)S(1)}, u32[]{:S(2)}, u32[]{:S(2)}) collective-permute-start(f32[8,128]{1,0:T(8,128)S(1)} %get-tuple-element.13.refs_0_), channel_id=1, source_target_pairs={{0,8},{8,0},{16,24},{24,16},{1,9},{9,1},{17,25},{25,17},{2,10},{10... | collective-permute-start | bytes 12296 | tf_op jit(solution)/shard_map/ppermute | solution.py:284
  28.7 1.0 %collective-permute-done.6.refs_3_ = f32[8,128]{1,0:T(8,128)S(1)} collective-permute-done((f32[8,128]{1,0:T(8,128)S(1)}, f32[8,128]{1,0:T(8,128)S(1)}, u32[]{:S(2)}, u32[]{:S(2)}) %collective-permute-start.6) | collective-permute-done | bytes 4128 | tf_op jit(solution)/shard_map/ppermute | solution.py:284
  29.7 0.0 collective-permute-done.5.refs_2_
  29.7 0.8 %collective-permute-done.4.refs_1_ = f32[8,128]{1,0:T(8,128)S(1)} collective-permute-done((f32[8,128]{1,0:T(8,128)S(1)}, f32[8,128]{1,0:T(8,128)S(1)}, u32[]{:S(2)}, u32[]{:S(2)}) %collective-permute-start.4) | collective-permute-done | bytes 4128 | tf_op jit(solution)/shard_map/ppermute | solution.py:284
  30.5 0.8 %finish.1 = (f32[1,32]{1,0:T(1,128)}, f32[32,128]{1,0:T(8,128)}) custom-call(f32[8,128]{1,0:T(8,128)S(1)} %get-tuple-element.13.refs_0_, f32[8,128]{1,0:T(8,128)S(1)} %collective-permute-done.4.refs_1_, f32[8,128]{1,0:T(8,128)S(1)} %collective-permute-done.5.refs_2_, f32[8,128]{1,0:T(8,128)S(1)} %collective-permute-done.6.refs_3_, ...), custom_call_target="tpu_custom_call" | custom-call | tf_op jit(solution)/shard_map/finish/pallas_call | solution.py:368
  (2 shorter events, 0.0 us)
Async XLA Ops:
  0.6 15.9 %copy-start = (f32[4096,128]{1,0:T(8,128)S(1)}, f32[4096,128]{1,0:T(8,128)}, u32[]{:S(2)}) copy-start(f32[4096,128]{1,0:T(8,128)} %oper_ref.1) | copy-start | bytes 6291460
  1.9 21.5 %copy-start.1 = (s32[16384]{0:T(1024)S(1)}, s32[16384]{0:T(1024)}, u32[]{:S(2)}) copy-start(s32[16384]{0:T(1024)} %param.9) | copy-start | bytes 196612
  1.9 21.4 %copy-start.2 = (f32[16384]{0:T(1024)S(1)}, f32[16384]{0:T(1024)}, u32[]{:S(2)}) copy-start(f32[16384]{0:T(1024)} %param.8) | copy-start | bytes 196612
  17.4 1.2 %collective-permute-start = (f32[32,128]{1,0:T(8,128)S(1)}, f32[32,128]{1,0:T(8,128)S(1)}, u32[]{:S(2)}, u32[]{:S(2)}) collective-permute-start(f32[32,128]{1,0:T(8,128)S(1)} %get-tuple-element.10), channel_id=1, source_target_pairs={{0,1},{1,0},{2,3},{3,2},{4,5},{5,4},{6,7},{7,6},{8,9},{9,8},{10,11... | collective-permute-start | bytes 49160 | tf_op jit(solution)/shard_map/ppermute | solution.py:284
  18.7 3.7 %collective-permute-start.2 = (f32[32,128]{1,0:T(8,128)S(1)}, f32[32,128]{1,0:T(8,128)S(1)}, u32[]{:S(2)}, u32[]{:S(2)}) collective-permute-start(f32[32,128]{1,0:T(8,128)S(1)} %add.10), channel_id=1, source_target_pairs={{0,2},{1,7},{2,0},{3,5},{4,6},{5,3},{6,4},{7,1},{8,10},{9,15},{10,... | collective-permute-start | bytes 49160 | tf_op jit(solution)/shard_map/ppermute | solution.py:293
  19.3 3.9 %collective-permute-start.1 = (f32[32,128]{1,0:T(8,128)S(1)}, f32[32,128]{1,0:T(8,128)S(1)}, u32[]{:S(2)}, u32[]{:S(2)}) collective-permute-start(f32[32,128]{1,0:T(8,128)S(1)} %add.10), channel_id=1, source_target_pairs={{0,2},{1,5},{2,0},{3,7},{4,6},{5,1},{6,4},{7,3},{8,10},{9,13},{10,... | collective-permute-start | bytes 49160 | tf_op jit(solution)/shard_map/ppermute | solution.py:294
  23.2 1.2 %collective-permute-start.3 = (f32[32,128]{1,0:T(8,128)S(1)}, f32[32,128]{1,0:T(8,128)S(1)}, u32[]{:S(2)}, u32[]{:S(2)}) collective-permute-start(f32[32,128]{1,0:T(8,128)S(1)} %select_add_fusion.refs_0_), channel_id=1, source_target_pairs={{0,1},{1,0},{2,3},{3,2},{4,5},{5,4},{6,7},{7,6},{8,9},{9,8},{10,11... | collective-permute-start | bytes 49160 | tf_op jit(solution)/shard_map/ppermute | solution.py:284
  25.1 4.6 %collective-permute-start.6 = (f32[8,128]{1,0:T(8,128)S(1)}, f32[8,128]{1,0:T(8,128)S(1)}, u32[]{:S(2)}, u32[]{:S(2)}) collective-permute-start(f32[8,128]{1,0:T(8,128)S(1)} %get-tuple-element.13.refs_0_), channel_id=1, source_target_pairs={{0,24},{8,16},{16,8},{24,0},{1,25},{9,17},{17,9},{25,1},{2,26},{10... | collective-permute-start | bytes 12296 | tf_op jit(solution)/shard_map/ppermute | solution.py:284
  25.9 3.9 %collective-permute-start.5 = (f32[8,128]{1,0:T(8,128)S(1)}, f32[8,128]{1,0:T(8,128)S(1)}, u32[]{:S(2)}, u32[]{:S(2)}) collective-permute-start(f32[8,128]{1,0:T(8,128)S(1)} %get-tuple-element.13.refs_0_), channel_id=1, source_target_pairs={{0,16},{8,24},{16,0},{24,8},{1,17},{9,25},{17,1},{25,9},{2,18},{10... | collective-permute-start | bytes 12296 | tf_op jit(solution)/shard_map/ppermute | solution.py:284
  26.9 3.6 %collective-permute-start.4 = (f32[8,128]{1,0:T(8,128)S(1)}, f32[8,128]{1,0:T(8,128)S(1)}, u32[]{:S(2)}, u32[]{:S(2)}) collective-permute-start(f32[8,128]{1,0:T(8,128)S(1)} %get-tuple-element.13.refs_0_), channel_id=1, source_target_pairs={{0,8},{8,0},{16,24},{24,16},{1,9},{9,1},{17,25},{25,17},{2,10},{10... | collective-permute-start | bytes 12296 | tf_op jit(solution)/shard_map/ppermute | solution.py:284

commit v4 on v3

--- a/solution.py
+++ b/solution.py
@@ -13,7 +13,8 @@
 BF16 = jnp.bfloat16
 F32 = jnp.float32
 LIMIT = 24 * 1024 * 1024
-SHIFTS = (1, 2, 4, 8)
+SHIFTS = (1, 2, 3, 4, 8, 12)
+LEVEL = 3
 NT = (((1,), (1,)), ((), ()))
 TARGET, HEAD, FIRST, LAST, UPWARD, DOWNWARD = 0, 1, 2, 3, 4, 4 + len(SHIFTS)
 AUX = 4 + 2 * len(SHIFTS)
@@ -59,6 +60,7 @@
 
 def pack_kernel(hist, local, x_any, f_any, out_ref, x_ref, f_ref, dirs_ref, diff_ref, sems):
     wide, group, rows = dims(hist, local)
+    pieces = -(-hist // TILE)
     copies = [pltpu.make_async_copy(a, b, sems.at[i]) for i, (a, b) in enumerate(((x_any, x_ref), (f_any, f_ref)))]
     for copy in copies:
         copy.start()
@@ -69,17 +71,19 @@
     delta_f = f_ref[1 : hist + 1, :] - f_ref[0:hist, :]
     delta_x = x_ref[1 : hist + 1, :] - x_ref[0:hist, :]
     last_f = f_ref[hist : hist + 1, :]
-    diff_ref[0:hist, :] = delta_f
-    diff_ref[hist : hist + 1, :] = last_f
+    for piece in range(pieces):
+        base = piece * (LANES + TILE * (hist + 1))
+        diff_ref[base : base + hist, :] = delta_f
+        diff_ref[base + hist : base + hist + 1, :] = last_f
     dirs_ref[0:hist, 0:local] = delta_x + delta_f
     dirs_ref[hist : hist + 1, 0:local] = x_ref[hist : hist + 1, :] + last_f
     gram = lax.dot_general(diff_ref[0:wide, :], diff_ref[...], NT, precision=lax.Precision.HIGHEST, preferred_element_type=F32)
-    sub = lax.broadcasted_iota(jnp.int32, gram.shape, 0)
-    gram = jnp.where(sub < hist, gram, 0.0)
+    sub = lax.broadcasted_iota(jnp.int32, (TILE, LANES), 0)
     flat = jnp.zeros((TILE, LANES), F32)
-    for start in range(0, wide, TILE):
-        turned = pltpu.roll(gram[start : start + TILE, :], 0, 1, stride=hist + 1, stride_axis=0)
-        flat = flat + (pltpu.roll(turned, start * (hist + 1) % LANES, 1) if start else turned)
+    for piece in range(pieces):
+        block = gram[piece * TILE : (piece + 1) * TILE, piece * LANES : (piece + 1) * LANES]
+        block = jnp.where(sub < hist - piece * TILE, block, 0.0)
+        flat = flat + pltpu.roll(block, 0, 1, stride=hist + 1, stride_axis=0)
     message = dirs_ref[pl.ds(0, rows, stride=group), :]
     for place in range(1, group):
         message = message + pltpu.roll(dirs_ref[pl.ds(place, rows, stride=group), :], place * local, 1)
@@ -90,7 +94,7 @@
         out_ref[start : start + TILE, :] = message
 
 
-def image_kernel(hist, local, row_count, chunk, recv_ref, oper_ref, cat_ref, part_ref, blend_ref, dirs_ref, img_ref):
+def image_kernel(hist, local, row_count, chunk, recv_ref, oper_ref, high_ref, low_ref, part_ref, blend_ref, dirs_ref, img_ref):
     wide, group, rows = dims(hist, local)
     row_block, width = oper_ref.shape
     own_rows = row_block // LANES
@@ -115,8 +119,8 @@
     )
     for start in range(0, row_block, chunk):
         high, low = split(oper_ref[start : start + chunk, :])
-        cat_ref[start : start + chunk, 0:width] = high
-        cat_ref[start : start + chunk, width : 2 * width] = low
+        high_ref[start : start + chunk, :] = high
+        low_ref[start : start + chunk, :] = low
         both = lax.dot_general(left, jnp.concatenate([high, low], axis=1), NT, preferred_element_type=F32)
         image = both[0:wide, :] + both[wide : 2 * wide, :]
         for piece in range(chunk // LANES):
@@ -177,18 +181,18 @@
 
 def cone_kernel(count, *refs):
     parts = refs[:count]
-    aux_ref, cat_ref, proj_ref, edge_ref, out_ref = refs[count:]
+    aux_ref, high_ref, low_ref, proj_ref, edge_ref, out_ref = refs[count:]
     own_rows = proj_ref.shape[0]
     width = out_ref.shape[1]
     slack = aux_ref[TARGET] - tree(p[...] for p in parts)
     head, first, last = aux_ref[HEAD], aux_ref[FIRST], aux_ref[LAST]
     square = (1.0 - head) * slack * slack
     lead, ahead, behind = head * slack, square, square
-    for index, step in enumerate(SHIFTS):
-        same = aux_ref[UPWARD + index]
-        lead = lead + same * shifted(lead, step)
-        ahead = ahead + same * shifted(ahead, step)
-        behind = behind + aux_ref[DOWNWARD + index] * shifted(behind, -step)
+    for level in range(0, len(SHIFTS), LEVEL):
+        places = range(level, level + LEVEL)
+        lead = lead + sum(aux_ref[UPWARD + i] * shifted(lead, SHIFTS[i]) for i in places)
+        ahead = ahead + sum(aux_ref[UPWARD + i] * shifted(ahead, SHIFTS[i]) for i in places)
+        behind = behind + sum(aux_ref[DOWNWARD + i] * shifted(behind, -SHIFTS[i]) for i in places)
     norm = jnp.sqrt(jnp.maximum(ahead + behind - square, 0.0))
     inside = norm <= lead
     killed = norm <= -lead
@@ -215,7 +219,7 @@
         low = (jnp.concatenate([interior, edge], axis=0) - high.astype(F32)).astype(BF16)
         pieces.append(jnp.concatenate([high, low], axis=0))
     left = jnp.concatenate(pieces, axis=1)
-    both = jnp.dot(left, cat_ref[...], preferred_element_type=F32)
+    both = jnp.dot(left, jnp.concatenate([high_ref[...], low_ref[...]], axis=1), preferred_element_type=F32)
     half = 2 * TILE
     sums = both[0:half, 0:width] + both[0:half, width : 2 * width] + both[half : 2 * half, 0:width]
     ends = slack[final:, :]
@@ -239,19 +243,32 @@
     proj_ref, edge_ref, aux_ref, blend_ref, next_ref, out_ref = refs[row_count:]
     row = lax.axis_index("row")
     own_rows, width = proj_ref.shape[0], blend_ref.shape[1]
+    group = LANES // local
+
+    def own_lanes(x):
+        mine = x[:, 0:LANES]
+        for start in range(1, width // LANES):
+            mine = jnp.where(row // group == start, x[:, start * LANES : (start + 1) * LANES], mine)
+        return pltpu.roll(mine, (LANES - row % group * local) % LANES, 1)
+
+    def by_block(received):
+        blocks = []
+        for block in range(row_count):
+            mine = received[0]
+            for turn in range(1, row_count):
+                mine = jnp.where(lax.bitwise_xor(row, turn) == block, received[turn], mine)
+            blocks.append(mine)
+        return blocks
+
     received = [m[...] for m in messages]
-    blocks = []
-    for block in range(row_count):
-        mine = received[0]
-        for turn in range(1, row_count):
-            mine = jnp.where(lax.bitwise_xor(row, turn) == block, received[turn], mine)
-        blocks.append(mine)
-    total = tree(b[BACK : BACK + 1, :] for b in blocks)
+    scalars = by_block([m[:, 0:LANES] for m in received])
+    vectors = by_block([own_lanes(m) for m in received])
+    total = tree(b[BACK : BACK + 1, :] for b in vectors)
     ones = jnp.ones((1, LANES), F32)
     zeros = jnp.zeros((1, LANES), F32)
     tail_last, lead_last, tail_first = ones, zeros, ones
     for block in range(row_count - 1):
-        this, that = blocks[block], blocks[block + 1]
+        this, that = scalars[block], scalars[block + 1]
         lead = this[LEAD_LAST : LEAD_LAST + 1, :]
         norm = jnp.sqrt(this[SQUARE_LAST : SQUARE_LAST + 1, :] + that[SQUARE_FIRST : SQUARE_FIRST + 1, :])
         inside = norm <= lead
@@ -260,16 +277,12 @@
         middle = 0.5 * (lead + norm)
         factor = jnp.where(inside, 1.0, jnp.where(killed, 0.0, middle / safe))
         new = jnp.where(inside, lead, jnp.where(killed, 0.0, middle))
-        tails = this[TAIL_LAST : TAIL_LAST + 1, :] + that[TAIL_FIRST : TAIL_FIRST + 1, :]
-        total = total + ((factor - 1.0) * tails + (new - lead) * this[HEAD_LAST : HEAD_LAST + 1, :])
-        tail_last = jnp.where(row == block, factor[:, 0:LANES], tail_last)
-        lead_last = jnp.where(row == block, new[:, 0:LANES], lead_last)
-        tail_first = jnp.where(row == block + 1, factor[:, 0:LANES], tail_first)
-    moved = blend_ref[...] - scale_back * total
-    mine = moved[:, 0:local]
-    for block in range(1, row_count):
-        mine = jnp.where(row == block, moved[:, block * local : (block + 1) * local], mine)
-    next_ref[...] = mine
+        tails = vectors[block][TAIL_LAST : TAIL_LAST + 1, :] + vectors[block + 1][TAIL_FIRST : TAIL_FIRST + 1, :]
+        total = total + ((factor - 1.0) * tails + (new - lead) * vectors[block][HEAD_LAST : HEAD_LAST + 1, :])
+        tail_last = jnp.where(row == block, factor, tail_last)
+        lead_last = jnp.where(row == block, new, lead_last)
+        tail_first = jnp.where(row == block + 1, factor, tail_first)
+    next_ref[...] = (own_lanes(blend_ref[...]) - scale_back * total)[:, 0:local]
     final = own_rows - 1
     begin, end = edge_ref[0:1, :], edge_ref[1:2, :]
     ahead = jnp.where(aux_ref[FIRST, 0:1, :] > 0, tail_first * begin, proj_ref[0:1, :])
@@ -320,7 +333,7 @@
             pltpu.VMEM((hist + 1, local), F32),
             pltpu.VMEM((hist + 1, local), F32),
             pltpu.VMEM((wide, LANES), F32),
-            pltpu.VMEM((LANES, local), F32),
+            pltpu.VMEM((-(-hist // TILE) * LANES, local), F32),
             pltpu.SemaphoreType.DMA((2,)),
         ],
         cost_estimate=pl.CostEstimate(flops=10**10, bytes_accessed=4 * 10**7, transcendentals=0),
@@ -328,13 +341,14 @@
     )(hbm(iterates), hbm(residuals))
     received = lax.all_to_all(message, ("col", "row"), 0, 0, tiled=True)
 
-    cat, part, blended = pl.pallas_call(
+    high, low, part, blended = pl.pallas_call(
         functools.partial(image_kernel, hist, local, row_count, min(512, row_block)),
         name="image",
         in_specs=[vmem()] * 2,
-        out_specs=[vmem()] * 3,
+        out_specs=[vmem()] * 4,
         out_shape=[
-            jax.ShapeDtypeStruct((row_block, 2 * width), BF16),
+            jax.ShapeDtypeStruct((row_block, width), BF16),
+            jax.ShapeDtypeStruct((row_block, width), BF16),
             jax.ShapeDtypeStruct((own_rows, LANES), F32),
             jax.ShapeDtypeStruct((1, width), F32),
         ],
@@ -355,7 +369,7 @@
     projected, edge, back = pl.pallas_call(
         functools.partial(cone_kernel, len(parts)),
         name="cones",
-        in_specs=[vmem()] * (len(parts) + 2),
+        in_specs=[vmem()] * (len(parts) + 3),
         out_specs=[vmem()] * 3,
         out_shape=[
             jax.ShapeDtypeStruct((own_rows, LANES), F32),
@@ -363,7 +377,7 @@
             jax.ShapeDtypeStruct((TILE, width), F32),
         ],
         compiler_params=params(),
-    )(*parts, aux, cat)
+    )(*parts, aux, high, low)
 
     next_point, projected = pl.pallas_call(
         functools.partial(finish_kernel, scale_back, local, row_count),

time: 31.6 us -> 31.1 us (0.984)
  Pallas kernels: 3.79 us -> 3.37 us
where the time goes in v4:
time: 31.1 us; the launch traced here: 30.9 us
  blocking collectives  14.6 us (47%)
  waiting for transfers between devices  6.42 us (21%)
  starting transfers between devices  5.79 us (19%)
  Pallas kernels  3.37 us (11%)
  between operations  0.7 us (2%)
    all_to_all x1, blocking collectives, body(): received = lax.all_to_all(message, ('col', 'row'), 0, 0, tiled=True)  14.6 us
    ppermute x5, waiting for transfers between devices, exchange(): lax.ppermute(x, axis, [(i, i ^ turn) for i in range(count)])  3.92 us
    ppermute x5, starting transfers between devices, exchange(): lax.ppermute(x, axis, [(i, i ^ turn) for i in range(count)])  3.76 us
    ppermute x1, waiting for transfers between devices, reduce_col(): lax.ppermute(x, 'col', [(i, i ^ (3 * bit if i % 2 else bit)) for i in ran...  1.71 us
    ppermute x1, starting transfers between devices, reduce_col(): lax.ppermute(x, 'col', [(i, i ^ (2 * bit if i % 2 else bit)) for i in ran...  1.42 us
    pallas_call x1, Pallas kernels, body(): pl.pallas_call(functools.partial(pack_kernel, hist, local), name='pack',...  1.18 us
    pallas_call x1, Pallas kernels, body(): pl.pallas_call(functools.partial(image_kernel, hist, local, row_count, mi...  0.83 us
    ppermute x1, waiting for transfers between devices, reduce_col(): lax.ppermute(x, 'col', [(i, i ^ (2 * bit if i % 2 else bit)) for i in ran...  0.78 us
  transfers between devices with their start and end apart: 7, of which 6 were waited for; matrix products, arithmetic and copies ran while one was open for 0% of the time, Pallas kernels for 0%

profile of v4, /device:TPU:0, one launch (start us, length us, event | category | flops | bytes accessed | tf_op | source)
XLA Modules:
  0.0 30.9 jit_solution(12985635559234599401)
XLA Ops:
  0.6 0.0 copy-start
  0.6 1.2 %pack.1 = f32[128,128]{1,0:T(8,128)S(1)} custom-call(f32[11,32]{1,0:T(8,128)} %x_any.1, f32[11,32]{1,0:T(8,128)} %f_any.1), custom_call_target="tpu_custom_call" | custom-call | flops 10000000000 | bytes 40000000 | tf_op jit(solution)/shard_map/pack/pallas_call | solution.py:326
  1.8 0.0 copy-start.1
  1.8 0.0 copy-start.2
  1.9 14.6 %all_to_all.11 = f32[32,4,128]{2,1,0:T(4,128)S(1)} all-to-all(f32[32,4,128]{2,1,0:T(4,128)S(1)} %bitcast.7), channel_id=1, replica_groups=mesh['row'=4,'col'=8] {'col','row'}, dimensions={0} | all-to-all | bytes 131072 | tf_op jit(solution)/shard_map/all_to_all | solution.py:342
  16.5 0.0 copy-done
  16.5 0.8 %image.1 = (bf16[4096,128]{1,0:T(8,128)(2,1)S(1)}, bf16[4096,128]{1,0:T(8,128)(2,1)S(1)}, f32[32,128]{1,0:T(8,128)S(1)}, f32[1,128]{1,0:T(1,128)S(1)}) custom-call(f32[128,128]{1,0:T(8,128)S(1)} %bitcast.6, f32[4096,128]{1,0:T(8,128)S(1)} %copy-done), custom_call_target="tpu_custom_call" | custom-call | tf_op jit(solution)/shard_map/image/pallas_call | solution.py:344
  17.3 0.1 collective-permute-start
  17.4 1.2 %collective-permute-done = f32[32,128]{1,0:T(8,128)S(1)} collective-permute-done((f32[32,128]{1,0:T(8,128)S(1)}, f32[32,128]{1,0:T(8,128)S(1)}, u32[]{:S(2)}, u32[]{:S(2)}) %collective-permute-start) | collective-permute-done | bytes 16416 | tf_op jit(solution)/shard_map/ppermute | solution.py:297
  18.6 0.6 %collective-permute-start.2 = (f32[32,128]{1,0:T(8,128)S(1)}, f32[32,128]{1,0:T(8,128)S(1)}, u32[]{:S(2)}, u32[]{:S(2)}) collective-permute-start(f32[32,128]{1,0:T(8,128)S(1)} %add.10), channel_id=1, source_target_pairs={{0,2},{1,7},{2,0},{3,5},{4,6},{5,3},{6,4},{7,1},{8,10},{9,15},{10,... | collective-permute-start | bytes 49160 | tf_op jit(solution)/shard_map/ppermute | solution.py:306
  19.2 1.4 %collective-permute-start.1 = (f32[32,128]{1,0:T(8,128)S(1)}, f32[32,128]{1,0:T(8,128)S(1)}, u32[]{:S(2)}, u32[]{:S(2)}) collective-permute-start(f32[32,128]{1,0:T(8,128)S(1)} %add.10), channel_id=1, source_target_pairs={{0,2},{1,5},{2,0},{3,7},{4,6},{5,1},{6,4},{7,3},{8,10},{9,13},{10,... | collective-permute-start | bytes 49160 | tf_op jit(solution)/shard_map/ppermute | solution.py:307
  20.6 1.7 %collective-permute-done.2 = f32[32,128]{1,0:T(8,128)S(1)} collective-permute-done((f32[32,128]{1,0:T(8,128)S(1)}, f32[32,128]{1,0:T(8,128)S(1)}, u32[]{:S(2)}, u32[]{:S(2)}) %collective-permute-start.2) | collective-permute-done | bytes 16416 | tf_op jit(solution)/shard_map/ppermute | solution.py:306
  22.3 0.8 %collective-permute-done.1 = f32[32,128]{1,0:T(8,128)S(1)} collective-permute-done((f32[32,128]{1,0:T(8,128)S(1)}, f32[32,128]{1,0:T(8,128)S(1)}, u32[]{:S(2)}, u32[]{:S(2)}) %collective-permute-start.1) | collective-permute-done | bytes 16416 | tf_op jit(solution)/shard_map/ppermute | solution.py:307
  23.1 0.1 collective-permute-start.3
  23.2 0.0 copy-done.1
  23.2 0.0 copy-done.2
  23.2 0.1 masks.1.refs_2_.refs_6_
  23.4 0.9 %collective-permute-done.3.refs_1_ = f32[32,128]{1,0:T(8,128)S(1)} collective-permute-done((f32[32,128]{1,0:T(8,128)S(1)}, f32[32,128]{1,0:T(8,128)S(1)}, u32[]{:S(2)}, u32[]{:S(2)}) %collective-permute-start.3) | collective-permute-done | bytes 16416 | tf_op jit(solution)/shard_map/ppermute | solution.py:297
  24.3 0.6 %cones.1 = (f32[32,128]{1,0:T(8,128)S(1)}, f32[8,128]{1,0:T(8,128)S(1)}, f32[8,128]{1,0:T(8,128)S(1)}) custom-call(f32[32,128]{1,0:T(8,128)S(1)} %select_add_fusion.refs_0_, f32[32,128]{1,0:T(8,128)S(1)} %collective-permute-done.3.refs_1_, f32[16,32,128]{2,1,0:T(8,128)S(1)} %masks.1.refs_2_.refs_6_, bf16[4096,128]{1,0:T(8,128)(2,1)S(1)} %get-tuple-element.13.refs_3_, ...), custom_call_target="tpu_custom_call" | custom-call | tf_op jit(solution)/shard_map/cones/pallas_call | solution.py:369
  24.9 0.7 %collective-permute-start.6 = (f32[8,128]{1,0:T(8,128)S(1)}, f32[8,128]{1,0:T(8,128)S(1)}, u32[]{:S(2)}, u32[]{:S(2)}) collective-permute-start(f32[8,128]{1,0:T(8,128)S(1)} %get-tuple-element.15.refs_0_), channel_id=1, source_target_pairs={{0,24},{8,16},{16,8},{24,0},{1,25},{9,17},{17,9},{25,1},{2,26},{10... | collective-permute-start | bytes 12296 | tf_op jit(solution)/shard_map/ppermute | solution.py:297
  25.6 1.1 %collective-permute-start.5 = (f32[8,128]{1,0:T(8,128)S(1)}, f32[8,128]{1,0:T(8,128)S(1)}, u32[]{:S(2)}, u32[]{:S(2)}) collective-permute-start(f32[8,128]{1,0:T(8,128)S(1)} %get-tuple-element.15.refs_0_), channel_id=1, source_target_pairs={{0,16},{8,24},{16,0},{24,8},{1,17},{9,25},{17,1},{25,9},{2,18},{10... | collective-permute-start | bytes 12296 | tf_op jit(solution)/shard_map/ppermute | solution.py:297
  26.7 1.8 %collective-permute-start.4 = (f32[8,128]{1,0:T(8,128)S(1)}, f32[8,128]{1,0:T(8,128)S(1)}, u32[]{:S(2)}, u32[]{:S(2)}) collective-permute-start(f32[8,128]{1,0:T(8,128)S(1)} %get-tuple-element.15.refs_0_), channel_id=1, source_target_pairs={{0,8},{8,0},{16,24},{24,16},{1,9},{9,1},{17,25},{25,17},{2,10},{10... | collective-permute-start | bytes 12296 | tf_op jit(solution)/shard_map/ppermute | solution.py:297
  28.4 1.0 %collective-permute-done.6.refs_3_ = f32[8,128]{1,0:T(8,128)S(1)} collective-permute-done((f32[8,128]{1,0:T(8,128)S(1)}, f32[8,128]{1,0:T(8,128)S(1)}, u32[]{:S(2)}, u32[]{:S(2)}) %collective-permute-start.6) | collective-permute-done | bytes 4128 | tf_op jit(solution)/shard_map/ppermute | solution.py:297
  29.4 0.0 collective-permute-done.5.refs_2_
  29.4 0.8 %collective-permute-done.4.refs_1_ = f32[8,128]{1,0:T(8,128)S(1)} collective-permute-done((f32[8,128]{1,0:T(8,128)S(1)}, f32[8,128]{1,0:T(8,128)S(1)}, u32[]{:S(2)}, u32[]{:S(2)}) %collective-permute-start.4) | collective-permute-done | bytes 4128 | tf_op jit(solution)/shard_map/ppermute | solution.py:297
  30.3 0.6 %finish.1 = (f32[1,32]{1,0:T(1,128)}, f32[32,128]{1,0:T(8,128)}) custom-call(f32[8,128]{1,0:T(8,128)S(1)} %get-tuple-element.15.refs_0_, f32[8,128]{1,0:T(8,128)S(1)} %collective-permute-done.4.refs_1_, f32[8,128]{1,0:T(8,128)S(1)} %collective-permute-done.5.refs_2_, f32[8,128]{1,0:T(8,128)S(1)} %collective-permute-done.6.refs_3_, ...), custom_call_target="tpu_custom_call" | custom-call | tf_op jit(solution)/shard_map/finish/pallas_call | solution.py:382
  (2 shorter events, 0.0 us)
Async XLA Ops:
  0.6 15.9 %copy-start = (f32[4096,128]{1,0:T(8,128)S(1)}, f32[4096,128]{1,0:T(8,128)}, u32[]{:S(2)}) copy-start(f32[4096,128]{1,0:T(8,128)} %oper_ref.1) | copy-start | bytes 6291460
  1.8 21.4 %copy-start.1 = (s32[16384]{0:T(1024)S(1)}, s32[16384]{0:T(1024)}, u32[]{:S(2)}) copy-start(s32[16384]{0:T(1024)} %param.9) | copy-start | bytes 196612
  1.8 21.4 %copy-start.2 = (f32[16384]{0:T(1024)S(1)}, f32[16384]{0:T(1024)}, u32[]{:S(2)}) copy-start(f32[16384]{0:T(1024)} %param.8) | copy-start | bytes 196612
  17.3 1.2 %collective-permute-start = (f32[32,128]{1,0:T(8,128)S(1)}, f32[32,128]{1,0:T(8,128)S(1)}, u32[]{:S(2)}, u32[]{:S(2)}) collective-permute-start(f32[32,128]{1,0:T(8,128)S(1)} %get-tuple-element.11), channel_id=1, source_target_pairs={{0,1},{1,0},{2,3},{3,2},{4,5},{5,4},{6,7},{7,6},{8,9},{9,8},{10,11... | collective-permute-start | bytes 49160 | tf_op jit(solution)/shard_map/ppermute | solution.py:297
  18.6 3.7 %collective-permute-start.2 = (f32[32,128]{1,0:T(8,128)S(1)}, f32[32,128]{1,0:T(8,128)S(1)}, u32[]{:S(2)}, u32[]{:S(2)}) collective-permute-start(f32[32,128]{1,0:T(8,128)S(1)} %add.10), channel_id=1, source_target_pairs={{0,2},{1,7},{2,0},{3,5},{4,6},{5,3},{6,4},{7,1},{8,10},{9,15},{10,... | collective-permute-start | bytes 49160 | tf_op jit(solution)/shard_map/ppermute | solution.py:306
  19.2 3.9 %collective-permute-start.1 = (f32[32,128]{1,0:T(8,128)S(1)}, f32[32,128]{1,0:T(8,128)S(1)}, u32[]{:S(2)}, u32[]{:S(2)}) collective-permute-start(f32[32,128]{1,0:T(8,128)S(1)} %add.10), channel_id=1, source_target_pairs={{0,2},{1,5},{2,0},{3,7},{4,6},{5,1},{6,4},{7,3},{8,10},{9,13},{10,... | collective-permute-start | bytes 49160 | tf_op jit(solution)/shard_map/ppermute | solution.py:307
  23.1 1.2 %collective-permute-start.3 = (f32[32,128]{1,0:T(8,128)S(1)}, f32[32,128]{1,0:T(8,128)S(1)}, u32[]{:S(2)}, u32[]{:S(2)}) collective-permute-start(f32[32,128]{1,0:T(8,128)S(1)} %select_add_fusion.refs_0_), channel_id=1, source_target_pairs={{0,1},{1,0},{2,3},{3,2},{4,5},{5,4},{6,7},{7,6},{8,9},{9,8},{10,11... | collective-permute-start | bytes 49160 | tf_op jit(solution)/shard_map/ppermute | solution.py:297
  24.9 4.6 %collective-permute-start.6 = (f32[8,128]{1,0:T(8,128)S(1)}, f32[8,128]{1,0:T(8,128)S(1)}, u32[]{:S(2)}, u32[]{:S(2)}) collective-permute-start(f32[8,128]{1,0:T(8,128)S(1)} %get-tuple-element.15.refs_0_), channel_id=1, source_target_pairs={{0,24},{8,16},{16,8},{24,0},{1,25},{9,17},{17,9},{25,1},{2,26},{10... | collective-permute-start | bytes 12296 | tf_op jit(solution)/shard_map/ppermute | solution.py:297
  25.6 3.9 %collective-permute-start.5 = (f32[8,128]{1,0:T(8,128)S(1)}, f32[8,128]{1,0:T(8,128)S(1)}, u32[]{:S(2)}, u32[]{:S(2)}) collective-permute-start(f32[8,128]{1,0:T(8,128)S(1)} %get-tuple-element.15.refs_0_), channel_id=1, source_target_pairs={{0,16},{8,24},{16,0},{24,8},{1,17},{9,25},{17,1},{25,9},{2,18},{10... | collective-permute-start | bytes 12296 | tf_op jit(solution)/shard_map/ppermute | solution.py:297
  26.7 3.6 %collective-permute-start.4 = (f32[8,128]{1,0:T(8,128)S(1)}, f32[8,128]{1,0:T(8,128)S(1)}, u32[]{:S(2)}, u32[]{:S(2)}) collective-permute-start(f32[8,128]{1,0:T(8,128)S(1)} %get-tuple-element.15.refs_0_), channel_id=1, source_target_pairs={{0,8},{8,0},{16,24},{24,16},{1,9},{9,1},{17,25},{25,17},{2,10},{10... | collective-permute-start | bytes 12296 | tf_op jit(solution)/shard_map/ppermute | solution.py:297

commit v5 on v4

--- a/solution.py
+++ b/solution.py
@@ -12,7 +12,7 @@
 TILE = 8
 BF16 = jnp.bfloat16
 F32 = jnp.float32
-LIMIT = 24 * 1024 * 1024
+LIMIT = 32 * 1024 * 1024
 SHIFTS = (1, 2, 3, 4, 8, 12)
 LEVEL = 3
 NT = (((1,), (1,)), ((), ()))
@@ -94,12 +94,11 @@
         out_ref[start : start + TILE, :] = message
 
 
-def image_kernel(hist, local, row_count, chunk, recv_ref, oper_ref, high_ref, low_ref, part_ref, blend_ref, dirs_ref, img_ref):
+def directions(hist, local, row_count, col, recv_ref, dirs_ref):
     wide, group, rows = dims(hist, local)
-    row_block, width = oper_ref.shape
-    own_rows = row_block // LANES
-    mine = recv_ref[pl.ds(pl.multiple_of(lax.axis_index("col") * (row_count * rows), TILE), row_count * rows), :]
+    mine = recv_ref[pl.ds(pl.multiple_of(col * (row_count * rows), TILE), row_count * rows), :]
     lane = lax.broadcasted_iota(jnp.int32, (rows, LANES), 1)
+    width = row_count * local
     for start in range(0, width, LANES):
         for place in range(group):
             spread = jnp.zeros((rows, LANES), F32)
@@ -112,17 +111,35 @@
             dirs_ref.at[start // LANES][pl.ds(place, rows, stride=group), :] = spread
     sub = lax.broadcasted_iota(jnp.int32, (wide, width), 0)
     dirs = jnp.concatenate([dirs_ref[i] for i in range(width // LANES)], axis=1)
-    dirs = jnp.where(sub <= hist, dirs, 0.0)
+    return jnp.where(sub <= hist, dirs, 0.0)
+
+
+def left_operand(dirs):
     high, low = split(dirs)
-    left = jnp.concatenate(
+    return jnp.concatenate(
         [jnp.concatenate([high, high], axis=1), jnp.concatenate([low, jnp.zeros_like(low)], axis=1)], axis=0
     )
+
+
+def image_kernel(hist, local, row_count, chunk, recv_ref, *refs):
+    oper_ref, other_ref, high_ref, low_ref, part_ref, blend_ref, dirs_ref, far_ref, img_ref = refs
+    wide, _, rows = dims(hist, local)
+    row_block, width = oper_ref.shape
+    own_rows = row_block // LANES
+    col = lax.axis_index("col")
+    dirs = directions(hist, local, row_count, col, recv_ref, dirs_ref)
+    left = left_operand(dirs)
+    far = left_operand(directions(hist, local, row_count, lax.bitwise_xor(col, 1), recv_ref, far_ref))
+
+    def multiply(left, high, low):
+        both = lax.dot_general(left, jnp.concatenate([high, low], axis=1), NT, preferred_element_type=F32)
+        return both[0:wide, :] + both[wide : 2 * wide, :]
+
     for start in range(0, row_block, chunk):
         high, low = split(oper_ref[start : start + chunk, :])
         high_ref[start : start + chunk, :] = high
         low_ref[start : start + chunk, :] = low
-        both = lax.dot_general(left, jnp.concatenate([high, low], axis=1), NT, preferred_element_type=F32)
-        image = both[0:wide, :] + both[wide : 2 * wide, :]
+        image = multiply(left, high, low) + multiply(far, *split(other_ref[start : start + chunk, :]))
         for piece in range(chunk // LANES):
             tile = image[:, piece * LANES : (piece + 1) * LANES]
             img_ref[pl.ds(start // LANES + piece, hist + 1, stride=own_rows), :] = tile[0 : hist + 1, :]
@@ -297,9 +314,9 @@
     return [lax.ppermute(x, axis, [(i, i ^ turn) for i in range(count)]) for turn in turns]
 
 
-def reduce_col(x, count):
+def reduce_chips(x, count):
     core = lax.axis_index("col") % 2
-    terms, bit = [x, *exchange(x, "col", [1])], 2
+    terms, bit = [x], 2
     while bit < count:
         x = tree(terms)
         if 2 * bit < count:
@@ -323,6 +340,7 @@
     wide, _, rows = dims(hist, local)
     own_rows = row_block // LANES
 
+    (other,) = exchange(operator, "col", [1])
     message = pl.pallas_call(
         functools.partial(pack_kernel, hist, local),
         name="pack",
@@ -344,7 +362,7 @@
     high, low, part, blended = pl.pallas_call(
         functools.partial(image_kernel, hist, local, row_count, min(512, row_block)),
         name="image",
-        in_specs=[vmem()] * 2,
+        in_specs=[vmem()] * 3,
         out_specs=[vmem()] * 4,
         out_shape=[
             jax.ShapeDtypeStruct((row_block, width), BF16),
@@ -352,9 +370,13 @@
             jax.ShapeDtypeStruct((own_rows, LANES), F32),
             jax.ShapeDtypeStruct((1, width), F32),
         ],
-        scratch_shapes=[pltpu.VMEM((width // LANES, wide, LANES), F32), pltpu.VMEM(((hist + 1) * own_rows, LANES), F32)],
+        scratch_shapes=[
+            pltpu.VMEM((width // LANES, wide, LANES), F32),
+            pltpu.VMEM((width // LANES, wide, LANES), F32),
+            pltpu.VMEM(((hist + 1) * own_rows, LANES), F32),
+        ],
         compiler_params=params(),
-    )(received, operator)
+    )(received, operator, other)
 
     aux = pl.pallas_call(
         functools.partial(mask_kernel, row_count),
@@ -365,7 +387,7 @@
         compiler_params=params(),
     )(cone_id.reshape(-1, LANES), target.reshape(-1, LANES), blended)
 
-    parts = reduce_col(part, col_count)
+    parts = reduce_chips(part, col_count)
     projected, edge, back = pl.pallas_call(
         functools.partial(cone_kernel, len(parts)),
         name="cones",

time: 31.1 us -> 30.8 us (level)
  waiting for transfers between devices: 6.42 us -> 5.5 us
  Pallas kernels: 3.37 us -> 3.91 us
  starting transfers between devices: 5.79 us -> 6.29 us
  blocking collectives: 14.6 us -> 14.2 us
    ppermute x5, waiting for transfers between devices: 3.92 us -> 3.18 us  [exchange(): lax.ppermute(x, axis, [(i, i ^ turn) for i in range(count)])]
    pallas_call x1, Pallas kernels: 0.83 us -> 1.45 us  [body(): pl.pallas_call(functools.partial(image_kernel, hist, local, row_count, mi...]
    ppermute x5, starting transfers between devices: 3.76 us -> 4.2 us  [exchange(): lax.ppermute(x, axis, [(i, i ^ turn) for i in range(count)])]
    all_to_all x1, blocking collectives: 14.6 us -> 14.2 us  [body(): received = lax.all_to_all(message, ('col', 'row'), 0, 0, tiled=True)]
  transfers between devices with their start and end apart: 7 -> 7, of which waited for: 6 -> 6; matrix products, arithmetic and copies ran while one was open for 0% -> 0% of each run, Pallas kernels for 0% -> 4%
where the time goes in v5:
time: 30.8 us; the launch traced here: 30.6 us
  blocking collectives  14.2 us (46%)
  starting transfers between devices  6.29 us (20%)
  waiting for transfers between devices  5.5 us (18%)
  Pallas kernels  3.91 us (13%)
  between operations  0.68 us (2%)
    all_to_all x1, blocking collectives, body(): received = lax.all_to_all(message, ('col', 'row'), 0, 0, tiled=True)  14.2 us
    ppermute x5, starting transfers between devices, exchange(): lax.ppermute(x, axis, [(i, i ^ turn) for i in range(count)])  4.2 us
    ppermute x5, waiting for transfers between devices, exchange(): lax.ppermute(x, axis, [(i, i ^ turn) for i in range(count)])  3.18 us
    ppermute x1, waiting for transfers between devices, reduce_chips(): lax.ppermute(x, 'col', [(i, i ^ (2 * bit if i % 2 else bit)) for i in ran...  1.71 us
    pallas_call x1, Pallas kernels, body(): pl.pallas_call(functools.partial(image_kernel, hist, local, row_count, mi...  1.45 us
    ppermute x1, starting transfers between devices, reduce_chips(): lax.ppermute(x, 'col', [(i, i ^ (3 * bit if i % 2 else bit)) for i in ran...  1.42 us
    pallas_call x1, Pallas kernels, body(): pl.pallas_call(functools.partial(pack_kernel, hist, local), name='pack',...  1.1 us
    ppermute x1, starting transfers between devices, reduce_chips(): lax.ppermute(x, 'col', [(i, i ^ (2 * bit if i % 2 else bit)) for i in ran...  0.67 us
  transfers between devices with their start and end apart: 7, of which 6 were waited for; matrix products, arithmetic and copies ran while one was open for 0% of the time, Pallas kernels for 4%

profile of v5, /device:TPU:0, one launch (start us, length us, event | category | flops | bytes accessed | tf_op | source)
XLA Modules:
  0.0 30.6 jit_solution(10170050842940504340)
XLA Ops:
  0.6 0.0 copy-start
  0.6 0.6 %collective-permute-start = (f32[4096,128]{1,0:T(8,128)}, f32[4096,128]{1,0:T(8,128)S(1)}, u32[]{:S(2)}, u32[]{:S(2)}) collective-permute-start(f32[4096,128]{1,0:T(8,128)} %refs_0_.1), channel_id=1, source_target_pairs={{0,1},{1,0},{2,3},{3,2},{4,5},{5,4},{6,7},{7,6},{8,9},{9,8},{10,11... | collective-permute-start | bytes 6291464 | tf_op jit(solution)/shard_map/ppermute | solution.py:314
  1.2 1.1 %pack.1 = f32[128,128]{1,0:T(8,128)S(1)} custom-call(f32[11,32]{1,0:T(8,128)} %x_any.1, f32[11,32]{1,0:T(8,128)} %f_any.1), custom_call_target="tpu_custom_call" | custom-call | flops 10000000000 | bytes 40000000 | tf_op jit(solution)/shard_map/pack/pallas_call | solution.py:344
  2.3 14.2 %all_to_all.11 = f32[32,4,128]{2,1,0:T(4,128)S(1)} all-to-all(f32[32,4,128]{2,1,0:T(4,128)S(1)} %bitcast.7), channel_id=1, replica_groups=mesh['row'=4,'col'=8] {'col','row'}, dimensions={0} | all-to-all | bytes 131072 | tf_op jit(solution)/shard_map/all_to_all | solution.py:360
  16.5 0.0 collective-permute-done.refs_1_
  16.5 0.0 copy-done
  16.5 0.0 copy-start.1
  16.5 0.0 copy-start.2
  16.5 1.5 %image.1 = (bf16[4096,128]{1,0:T(8,128)(2,1)S(1)}, bf16[4096,128]{1,0:T(8,128)(2,1)S(1)}, f32[32,128]{1,0:T(8,128)S(1)}, f32[1,128]{1,0:T(1,128)S(1)}) custom-call(f32[128,128]{1,0:T(8,128)S(1)} %bitcast.6, f32[4096,128]{1,0:T(8,128)S(1)} %copy-done, f32[4096,128]{1,0:T(8,128)S(1)} %collective-permute-done.refs_1_), custom_call_target="tpu_custom_call" | custom-call | tf_op jit(solution)/shard_map/image/pallas_call | solution.py:362
  18.0 0.7 %collective-permute-start.1 = (f32[32,128]{1,0:T(8,128)S(1)}, f32[32,128]{1,0:T(8,128)S(1)}, u32[]{:S(2)}, u32[]{:S(2)}) collective-permute-start(f32[32,128]{1,0:T(8,128)S(1)} %get-tuple-element.11), channel_id=1, source_target_pairs={{0,2},{1,5},{2,0},{3,7},{4,6},{5,1},{6,4},{7,3},{8,10},{9,13},{10,... | collective-permute-start | bytes 49160 | tf_op jit(solution)/shard_map/ppermute | solution.py:324
  18.7 1.4 %collective-permute-start.2 = (f32[32,128]{1,0:T(8,128)S(1)}, f32[32,128]{1,0:T(8,128)S(1)}, u32[]{:S(2)}, u32[]{:S(2)}) collective-permute-start(f32[32,128]{1,0:T(8,128)S(1)} %get-tuple-element.11), channel_id=1, source_target_pairs={{0,2},{1,7},{2,0},{3,5},{4,6},{5,3},{6,4},{7,1},{8,10},{9,15},{10,... | collective-permute-start | bytes 49160 | tf_op jit(solution)/shard_map/ppermute | solution.py:323
  20.1 1.7 %collective-permute-done.1 = f32[32,128]{1,0:T(8,128)S(1)} collective-permute-done((f32[32,128]{1,0:T(8,128)S(1)}, f32[32,128]{1,0:T(8,128)S(1)}, u32[]{:S(2)}, u32[]{:S(2)}) %collective-permute-start.1) | collective-permute-done | bytes 16416 | tf_op jit(solution)/shard_map/ppermute | solution.py:324
  21.8 0.6 %collective-permute-done.2 = f32[32,128]{1,0:T(8,128)S(1)} collective-permute-done((f32[32,128]{1,0:T(8,128)S(1)}, f32[32,128]{1,0:T(8,128)S(1)}, u32[]{:S(2)}, u32[]{:S(2)}) %collective-permute-start.2) | collective-permute-done | bytes 16416 | tf_op jit(solution)/shard_map/ppermute | solution.py:323
  22.4 0.1 collective-permute-start.3
  22.5 0.0 copy-done.1
  22.5 0.0 copy-done.2
  22.5 0.1 masks.1.refs_2_.refs_6_
  22.7 0.9 %collective-permute-done.3.refs_1_ = f32[32,128]{1,0:T(8,128)S(1)} collective-permute-done((f32[32,128]{1,0:T(8,128)S(1)}, f32[32,128]{1,0:T(8,128)S(1)}, u32[]{:S(2)}, u32[]{:S(2)}) %collective-permute-start.3) | collective-permute-done | bytes 16416 | tf_op jit(solution)/shard_map/ppermute | solution.py:314
  23.6 0.6 %cones.1 = (f32[32,128]{1,0:T(8,128)S(1)}, f32[8,128]{1,0:T(8,128)S(1)}, f32[8,128]{1,0:T(8,128)S(1)}) custom-call(f32[32,128]{1,0:T(8,128)S(1)} %select_add_fusion.refs_0_, f32[32,128]{1,0:T(8,128)S(1)} %collective-permute-done.3.refs_1_, f32[16,32,128]{2,1,0:T(8,128)S(1)} %masks.1.refs_2_.refs_6_, bf16[4096,128]{1,0:T(8,128)(2,1)S(1)} %get-tuple-element.13.refs_3_, ...), custom_call_target="tpu_custom_call" | custom-call | tf_op jit(solution)/shard_map/cones/pallas_call | solution.py:391
  24.2 0.7 %collective-permute-start.4 = (f32[8,128]{1,0:T(8,128)S(1)}, f32[8,128]{1,0:T(8,128)S(1)}, u32[]{:S(2)}, u32[]{:S(2)}) collective-permute-start(f32[8,128]{1,0:T(8,128)S(1)} %get-tuple-element.15.refs_0_), channel_id=1, source_target_pairs={{0,8},{8,0},{16,24},{24,16},{1,9},{9,1},{17,25},{25,17},{2,10},{10... | collective-permute-start | bytes 12296 | tf_op jit(solution)/shard_map/ppermute | solution.py:314
  24.9 0.6 %collective-permute-start.5 = (f32[8,128]{1,0:T(8,128)S(1)}, f32[8,128]{1,0:T(8,128)S(1)}, u32[]{:S(2)}, u32[]{:S(2)}) collective-permute-start(f32[8,128]{1,0:T(8,128)S(1)} %get-tuple-element.15.refs_0_), channel_id=1, source_target_pairs={{0,16},{8,24},{16,0},{24,8},{1,17},{9,25},{17,1},{25,9},{2,18},{10... | collective-permute-start | bytes 12296 | tf_op jit(solution)/shard_map/ppermute | solution.py:314
  25.5 2.3 %collective-permute-start.6 = (f32[8,128]{1,0:T(8,128)S(1)}, f32[8,128]{1,0:T(8,128)S(1)}, u32[]{:S(2)}, u32[]{:S(2)}) collective-permute-start(f32[8,128]{1,0:T(8,128)S(1)} %get-tuple-element.15.refs_0_), channel_id=1, source_target_pairs={{0,24},{8,16},{16,8},{24,0},{1,25},{9,17},{17,9},{25,1},{2,26},{10... | collective-permute-start | bytes 12296 | tf_op jit(solution)/shard_map/ppermute | solution.py:314
  27.7 0.1 collective-permute-done.4.refs_1_
  27.9 0.6 %collective-permute-done.5.refs_2_ = f32[8,128]{1,0:T(8,128)S(1)} collective-permute-done((f32[8,128]{1,0:T(8,128)S(1)}, f32[8,128]{1,0:T(8,128)S(1)}, u32[]{:S(2)}, u32[]{:S(2)}) %collective-permute-start.5) | collective-permute-done | bytes 4128 | tf_op jit(solution)/shard_map/ppermute | solution.py:314
  28.5 1.5 %collective-permute-done.6.refs_3_ = f32[8,128]{1,0:T(8,128)S(1)} collective-permute-done((f32[8,128]{1,0:T(8,128)S(1)}, f32[8,128]{1,0:T(8,128)S(1)}, u32[]{:S(2)}, u32[]{:S(2)}) %collective-permute-start.6) | collective-permute-done | bytes 4128 | tf_op jit(solution)/shard_map/ppermute | solution.py:314
  30.0 0.6 %finish.1 = (f32[1,32]{1,0:T(1,128)}, f32[32,128]{1,0:T(8,128)}) custom-call(f32[8,128]{1,0:T(8,128)S(1)} %get-tuple-element.15.refs_0_, f32[8,128]{1,0:T(8,128)S(1)} %collective-permute-done.4.refs_1_, f32[8,128]{1,0:T(8,128)S(1)} %collective-permute-done.5.refs_2_, f32[8,128]{1,0:T(8,128)S(1)} %collective-permute-done.6.refs_3_, ...), custom_call_target="tpu_custom_call" | custom-call | tf_op jit(solution)/shard_map/finish/pallas_call | solution.py:404
  (1 shorter events, 0.0 us)
Async XLA Ops:
  0.6 15.9 %copy-start = (f32[4096,128]{1,0:T(8,128)S(1)}, f32[4096,128]{1,0:T(8,128)}, u32[]{:S(2)}) copy-start(f32[4096,128]{1,0:T(8,128)} %refs_0_.1) | copy-start | bytes 6291460
  0.6 15.9 %collective-permute-start = (f32[4096,128]{1,0:T(8,128)}, f32[4096,128]{1,0:T(8,128)S(1)}, u32[]{:S(2)}, u32[]{:S(2)}) collective-permute-start(f32[4096,128]{1,0:T(8,128)} %refs_0_.1), channel_id=1, source_target_pairs={{0,1},{1,0},{2,3},{3,2},{4,5},{5,4},{6,7},{7,6},{8,9},{9,8},{10,11... | collective-permute-start | bytes 6291464 | tf_op jit(solution)/shard_map/ppermute | solution.py:314
  16.5 6.0 %copy-start.1 = (s32[16384]{0:T(1024)S(1)}, s32[16384]{0:T(1024)}, u32[]{:S(2)}) copy-start(s32[16384]{0:T(1024)} %param.9) | copy-start | bytes 196612
  16.5 6.0 %copy-start.2 = (f32[16384]{0:T(1024)S(1)}, f32[16384]{0:T(1024)}, u32[]{:S(2)}) copy-start(f32[16384]{0:T(1024)} %param.8) | copy-start | bytes 196612
  18.0 3.8 %collective-permute-start.1 = (f32[32,128]{1,0:T(8,128)S(1)}, f32[32,128]{1,0:T(8,128)S(1)}, u32[]{:S(2)}, u32[]{:S(2)}) collective-permute-start(f32[32,128]{1,0:T(8,128)S(1)} %get-tuple-element.11), channel_id=1, source_target_pairs={{0,2},{1,5},{2,0},{3,7},{4,6},{5,1},{6,4},{7,3},{8,10},{9,13},{10,... | collective-permute-start | bytes 49160 | tf_op jit(solution)/shard_map/ppermute | solution.py:324
  18.7 3.7 %collective-permute-start.2 = (f32[32,128]{1,0:T(8,128)S(1)}, f32[32,128]{1,0:T(8,128)S(1)}, u32[]{:S(2)}, u32[]{:S(2)}) collective-permute-start(f32[32,128]{1,0:T(8,128)S(1)} %get-tuple-element.11), channel_id=1, source_target_pairs={{0,2},{1,7},{2,0},{3,5},{4,6},{5,3},{6,4},{7,1},{8,10},{9,15},{10,... | collective-permute-start | bytes 49160 | tf_op jit(solution)/shard_map/ppermute | solution.py:323
  22.4 1.2 %collective-permute-start.3 = (f32[32,128]{1,0:T(8,128)S(1)}, f32[32,128]{1,0:T(8,128)S(1)}, u32[]{:S(2)}, u32[]{:S(2)}) collective-permute-start(f32[32,128]{1,0:T(8,128)S(1)} %select_add_fusion.refs_0_), channel_id=1, source_target_pairs={{0,1},{1,0},{2,3},{3,2},{4,5},{5,4},{6,7},{7,6},{8,9},{9,8},{10,11... | collective-permute-start | bytes 49160 | tf_op jit(solution)/shard_map/ppermute | solution.py:314
  24.2 3.7 %collective-permute-start.4 = (f32[8,128]{1,0:T(8,128)S(1)}, f32[8,128]{1,0:T(8,128)S(1)}, u32[]{:S(2)}, u32[]{:S(2)}) collective-permute-start(f32[8,128]{1,0:T(8,128)S(1)} %get-tuple-element.15.refs_0_), channel_id=1, source_target_pairs={{0,8},{8,0},{16,24},{24,16},{1,9},{9,1},{17,25},{25,17},{2,10},{10... | collective-permute-start | bytes 12296 | tf_op jit(solution)/shard_map/ppermute | solution.py:314
  24.9 3.6 %collective-permute-start.5 = (f32[8,128]{1,0:T(8,128)S(1)}, f32[8,128]{1,0:T(8,128)S(1)}, u32[]{:S(2)}, u32[]{:S(2)}) collective-permute-start(f32[8,128]{1,0:T(8,128)S(1)} %get-tuple-element.15.refs_0_), channel_id=1, source_target_pairs={{0,16},{8,24},{16,0},{24,8},{1,17},{9,25},{17,1},{25,9},{2,18},{10... | collective-permute-start | bytes 12296 | tf_op jit(solution)/shard_map/ppermute | solution.py:314
  25.5 4.5 %collective-permute-start.6 = (f32[8,128]{1,0:T(8,128)S(1)}, f32[8,128]{1,0:T(8,128)S(1)}, u32[]{:S(2)}, u32[]{:S(2)}) collective-permute-start(f32[8,128]{1,0:T(8,128)S(1)} %get-tuple-element.15.refs_0_), channel_id=1, source_target_pairs={{0,24},{8,16},{16,8},{24,0},{1,25},{9,17},{17,9},{25,1},{2,26},{10... | collective-permute-start | bytes 12296 | tf_op jit(solution)/shard_map/ppermute | solution.py:314

commit v6 on v5

--- a/solution.py
+++ b/solution.py
@@ -12,7 +12,7 @@
 TILE = 8
 BF16 = jnp.bfloat16
 F32 = jnp.float32
-LIMIT = 32 * 1024 * 1024
+SMALL = 8 * 1024 * 1024
 SHIFTS = (1, 2, 3, 4, 8, 12)
 LEVEL = 3
 NT = (((1,), (1,)), ((), ()))
@@ -21,8 +21,8 @@
 BACK, TAIL_LAST, HEAD_LAST, TAIL_FIRST, SQUARE_LAST, LEAD_LAST, SQUARE_FIRST = range(7)
 
 
-def params():
-    return pltpu.CompilerParams(vmem_limit_bytes=LIMIT)
+def params(blocks=0):
+    return pltpu.CompilerParams(vmem_limit_bytes=SMALL + blocks)
 
 
 def vmem():
@@ -122,7 +122,7 @@
 
 
 def image_kernel(hist, local, row_count, chunk, recv_ref, *refs):
-    oper_ref, other_ref, high_ref, low_ref, part_ref, blend_ref, dirs_ref, far_ref, img_ref = refs
+    oper_ref, other_ref, *split_refs, part_ref, blend_ref, dirs_ref, far_ref, img_ref = refs
     wide, _, rows = dims(hist, local)
     row_block, width = oper_ref.shape
     own_rows = row_block // LANES
@@ -136,10 +136,11 @@
         return both[0:wide, :] + both[wide : 2 * wide, :]
 
     for start in range(0, row_block, chunk):
-        high, low = split(oper_ref[start : start + chunk, :])
-        high_ref[start : start + chunk, :] = high
-        low_ref[start : start + chunk, :] = low
-        image = multiply(left, high, low) + multiply(far, *split(other_ref[start : start + chunk, :]))
+        own = split(oper_ref[start : start + chunk, :])
+        other = split(other_ref[start : start + chunk, :])
+        for ref, value in zip(split_refs, (*own, *other)):
+            ref[start : start + chunk, :] = value
+        image = multiply(left, *own) + multiply(far, *other)
         for piece in range(chunk // LANES):
             tile = image[:, piece * LANES : (piece + 1) * LANES]
             img_ref[pl.ds(start // LANES + piece, hist + 1, stride=own_rows), :] = tile[0 : hist + 1, :]
@@ -198,9 +199,9 @@
 
 def cone_kernel(count, *refs):
     parts = refs[:count]
-    aux_ref, high_ref, low_ref, proj_ref, edge_ref, out_ref = refs[count:]
+    aux_ref, *split_refs, proj_ref, edge_ref, own_ref, other_ref = refs[count:]
     own_rows = proj_ref.shape[0]
-    width = out_ref.shape[1]
+    width = own_ref.shape[1]
     slack = aux_ref[TARGET] - tree(p[...] for p in parts)
     head, first, last = aux_ref[HEAD], aux_ref[FIRST], aux_ref[LAST]
     square = (1.0 - head) * slack * slack
@@ -236,9 +237,7 @@
         low = (jnp.concatenate([interior, edge], axis=0) - high.astype(F32)).astype(BF16)
         pieces.append(jnp.concatenate([high, low], axis=0))
     left = jnp.concatenate(pieces, axis=1)
-    both = jnp.dot(left, jnp.concatenate([high_ref[...], low_ref[...]], axis=1), preferred_element_type=F32)
-    half = 2 * TILE
-    sums = both[0:half, 0:width] + both[0:half, width : 2 * width] + both[half : 2 * half, 0:width]
+    both = jnp.dot(left, jnp.concatenate([ref[...] for ref in split_refs], axis=1), preferred_element_type=F32)
     ends = slack[final:, :]
     scalars = jnp.where(
         sub == SQUARE_LAST,
@@ -247,15 +246,19 @@
     )
     scalars = jnp.broadcast_to(jnp.sum(scalars, axis=1, keepdims=True), (TILE, width))
     wide_sub = lax.broadcasted_iota(jnp.int32, (TILE, width), 0)
-    out_ref[...] = jnp.where(
-        wide_sub == BACK,
-        jnp.sum(sums[0:TILE, :], axis=0, keepdims=True),
-        jnp.where(wide_sub <= TAIL_FIRST, sums[TILE:half, :], scalars),
-    )
+    half = 2 * TILE
+    for place, ref in enumerate((own_ref, other_ref)):
+        block = both[:, place * 2 * width : (place + 1) * 2 * width]
+        sums = block[0:half, 0:width] + block[0:half, width : 2 * width] + block[half : 2 * half, 0:width]
+        ref[...] = jnp.where(
+            wide_sub == BACK,
+            jnp.sum(sums[0:TILE, :], axis=0, keepdims=True),
+            jnp.where(wide_sub <= TAIL_FIRST, sums[TILE:half, :], scalars),
+        )
     edge_ref[...] = jnp.where(sub == 0, slack[0:1, :], ends)
 
 
-def finish_kernel(scale_back, local, row_count, *refs):
+def finish_kernel(scale_back, local, row_count, turns, *refs):
     messages = refs[:row_count]
     proj_ref, edge_ref, aux_ref, blend_ref, next_ref, out_ref = refs[row_count:]
     row = lax.axis_index("row")
@@ -277,7 +280,7 @@
             blocks.append(mine)
         return blocks
 
-    received = [m[...] for m in messages]
+    received = [messages[turns.index(turn)][...] for turn in range(row_count)]
     scalars = by_block([m[:, 0:LANES] for m in received])
     vectors = by_block([own_lanes(m) for m in received])
     total = tree(b[BACK : BACK + 1, :] for b in vectors)
@@ -314,15 +317,34 @@
     return [lax.ppermute(x, axis, [(i, i ^ turn) for i in range(count)]) for turn in turns]
 
 
+def exchange_rows(x):
+    rows, cols = lax.axis_size("row"), lax.axis_size("col")
+    return [
+        lax.ppermute(x, ("row", "col"), [(r * cols + c, (r ^ turn) * cols + (c ^ 1)) for r in range(rows) for c in range(cols)])
+        for turn in range(1, rows)
+    ]
+
+
+def merge_kernel(own_ref, far_ref, near_ref, out_ref):
+    fetched = lax.bitwise_and(lax.axis_index("col"), 1) == 1
+    out_ref[...] = near_ref[...] + jnp.where(fetched, far_ref[...], own_ref[...])
+
+
 def reduce_chips(x, count):
-    core = lax.axis_index("col") % 2
     terms, bit = [x], 2
     while bit < count:
         x = tree(terms)
         if 2 * bit < count:
             far = lax.ppermute(x, "col", [(i, i ^ (3 * bit if i % 2 else bit)) for i in range(count)])
             near = lax.ppermute(x, "col", [(i, i ^ (2 * bit if i % 2 else bit)) for i in range(count)])
-            x = near + jnp.where(core == 1, far, x)
+            x = pl.pallas_call(
+                merge_kernel,
+                name="merge",
+                in_specs=[vmem()] * 3,
+                out_specs=vmem(),
+                out_shape=jax.ShapeDtypeStruct(x.shape, F32),
+                compiler_params=params(),
+            )(x, far, near)
             terms = [x, *exchange(x, "col", [1])]
         else:
             terms = [x, *exchange(x, "col", [bit])]
@@ -359,14 +381,13 @@
     )(hbm(iterates), hbm(residuals))
     received = lax.all_to_all(message, ("col", "row"), 0, 0, tiled=True)
 
-    high, low, part, blended = pl.pallas_call(
+    *halves, part, blended = pl.pallas_call(
         functools.partial(image_kernel, hist, local, row_count, min(512, row_block)),
         name="image",
         in_specs=[vmem()] * 3,
-        out_specs=[vmem()] * 4,
+        out_specs=[vmem()] * 6,
         out_shape=[
-            jax.ShapeDtypeStruct((row_block, width), BF16),
-            jax.ShapeDtypeStruct((row_block, width), BF16),
+            *[jax.ShapeDtypeStruct((row_block, width), BF16)] * 4,
             jax.ShapeDtypeStruct((own_rows, LANES), F32),
             jax.ShapeDtypeStruct((1, width), F32),
         ],
@@ -375,7 +396,7 @@
             pltpu.VMEM((width // LANES, wide, LANES), F32),
             pltpu.VMEM(((hist + 1) * own_rows, LANES), F32),
         ],
-        compiler_params=params(),
+        compiler_params=params(8 * operator.size),
     )(received, operator, other)
 
     aux = pl.pallas_call(
@@ -388,27 +409,30 @@
     )(cone_id.reshape(-1, LANES), target.reshape(-1, LANES), blended)
 
     parts = reduce_chips(part, col_count)
-    projected, edge, back = pl.pallas_call(
+    projected, edge, own, other = pl.pallas_call(
         functools.partial(cone_kernel, len(parts)),
         name="cones",
-        in_specs=[vmem()] * (len(parts) + 3),
-        out_specs=[vmem()] * 3,
+        in_specs=[vmem()] * (len(parts) + 5),
+        out_specs=[vmem()] * 4,
         out_shape=[
             jax.ShapeDtypeStruct((own_rows, LANES), F32),
             jax.ShapeDtypeStruct((TILE, LANES), F32),
             jax.ShapeDtypeStruct((TILE, width), F32),
+            jax.ShapeDtypeStruct((TILE, width), F32),
         ],
-        compiler_params=params(),
-    )(*parts, aux, high, low)
-
+        compiler_params=params(8 * operator.size),
+    )(*parts, aux, *halves)
+
+    turns = [0, 1, *range(3, row_count), 2]
+    messages = [own, *exchange_rows(other)]
     next_point, projected = pl.pallas_call(
-        functools.partial(finish_kernel, scale_back, local, row_count),
+        functools.partial(finish_kernel, scale_back, local, row_count, turns),
         name="finish",
         in_specs=[vmem()] * (row_count + 4),
         out_specs=[vmem()] * 2,
         out_shape=[jax.ShapeDtypeStruct((1, local), F32), jax.ShapeDtypeStruct((own_rows, LANES), F32)],
         compiler_params=params(),
-    )(back, *exchange(back, "row", range(1, row_count)), projected, edge, aux, blended)
+    )(*[messages[turn] for turn in turns], projected, edge, aux, blended)
     return (next_point.reshape(local), projected.reshape(row_block))
 
 

time: 30.8 us -> 30.4 us (0.987)
  starting transfers between devices: 6.29 us -> 5.78 us
  Pallas kernels: 3.91 us -> 4.37 us
  waiting for transfers between devices: 5.5 us -> 5.14 us
    ppermute x5 -> x2, starting transfers between devices: 4.2 us -> 0.65 us  [exchange(): lax.ppermute(x, axis, [(i, i ^ turn) for i in range(count)])]
    ppermute x0 -> x3, starting transfers between devices: none -> 3.04 us  [exchange_rows(): lax.ppermute(x, ('row', 'col'), [(r * cols + c, (r ^ turn) * cols + (c ^...]
    ppermute x5 -> x2, waiting for transfers between devices: 3.18 us -> 0.95 us  [exchange(): lax.ppermute(x, axis, [(i, i ^ turn) for i in range(count)])]
    ppermute x0 -> x3, waiting for transfers between devices: none -> 1.88 us  [exchange_rows(): lax.ppermute(x, ('row', 'col'), [(r * cols + c, (r ^ turn) * cols + (c ^...]
    pallas_call x1, Pallas kernels: 0.58 us -> 1.02 us  [body(): pl.pallas_call(functools.partial(cone_kernel, len(parts)), name='cones',...]
where the time goes in v6:
time: 30.4 us; the launch traced here: 30.2 us
  blocking collectives  14.2 us (47%)
  starting transfers between devices  5.78 us (19%)
  waiting for transfers between devices  5.14 us (17%)
  Pallas kernels  4.37 us (14%)
  between operations  0.69 us (2%)
    all_to_all x1, blocking collectives, body(): received = lax.all_to_all(message, ('col', 'row'), 0, 0, tiled=True)  14.2 us
    ppermute x3, starting transfers between devices, exchange_rows(): lax.ppermute(x, ('row', 'col'), [(r * cols + c, (r ^ turn) * cols + (c ^...  3.04 us
    ppermute x3, waiting for transfers between devices, exchange_rows(): lax.ppermute(x, ('row', 'col'), [(r * cols + c, (r ^ turn) * cols + (c ^...  1.88 us
    ppermute x1, waiting for transfers between devices, reduce_chips(): lax.ppermute(x, 'col', [(i, i ^ (2 * bit if i % 2 else bit)) for i in ran...  1.71 us
    pallas_call x1, Pallas kernels, body(): pl.pallas_call(functools.partial(image_kernel, hist, local, row_count, mi...  1.47 us
    ppermute x1, starting transfers between devices, reduce_chips(): lax.ppermute(x, 'col', [(i, i ^ (3 * bit if i % 2 else bit)) for i in ran...  1.42 us
    pallas_call x1, Pallas kernels, body(): pl.pallas_call(functools.partial(pack_kernel, hist, local), name='pack',...  1.1 us
    pallas_call x1, Pallas kernels, body(): pl.pallas_call(functools.partial(cone_kernel, len(parts)), name='cones',...  1.02 us
  transfers between devices with their start and end apart: 7, of which 6 were waited for; matrix products, arithmetic and copies ran while one was open for 0% of the time, Pallas kernels for 4%

profile of v6, /device:TPU:0, one launch (start us, length us, event | category | flops | bytes accessed | tf_op | source)
XLA Modules:
  0.0 30.2 jit_solution(7059900827883286616)
XLA Ops:
  0.6 0.0 copy-start
  0.6 0.6 %collective-permute-start = (f32[4096,128]{1,0:T(8,128)}, f32[4096,128]{1,0:T(8,128)S(1)}, u32[]{:S(2)}, u32[]{:S(2)}) collective-permute-start(f32[4096,128]{1,0:T(8,128)} %refs_0_.1), channel_id=1, source_target_pairs={{0,1},{1,0},{2,3},{3,2},{4,5},{5,4},{6,7},{7,6},{8,9},{9,8},{10,11... | collective-permute-start | bytes 6291464 | tf_op jit(solution)/shard_map/ppermute | solution.py:317
  1.2 1.1 %pack.1 = f32[128,128]{1,0:T(8,128)S(1)} custom-call(f32[11,32]{1,0:T(8,128)} %x_any.1, f32[11,32]{1,0:T(8,128)} %f_any.1), custom_call_target="tpu_custom_call" | custom-call | flops 10000000000 | bytes 40000000 | tf_op jit(solution)/shard_map/pack/pallas_call | solution.py:366
  2.3 14.2 %all_to_all.11 = f32[32,4,128]{2,1,0:T(4,128)S(1)} all-to-all(f32[32,4,128]{2,1,0:T(4,128)S(1)} %bitcast.7), channel_id=1, replica_groups=mesh['row'=4,'col'=8] {'col','row'}, dimensions={0} | all-to-all | bytes 131072 | tf_op jit(solution)/shard_map/all_to_all | solution.py:382
  16.5 0.0 collective-permute-done.refs_1_
  16.5 0.0 copy-done
  16.5 0.0 copy-start.1
  16.5 0.0 copy-start.2
  16.5 1.5 %image.1 = (bf16[4096,128]{1,0:T(8,128)(2,1)S(1)}, bf16[4096,128]{1,0:T(8,128)(2,1)S(1)}, bf16[4096,128]{1,0:T(8,128)(2,1)S(1)}, bf16[4096,128]{1,0:T(8,128)(2,1...) custom-call(f32[128,128]{1,0:T(8,128)S(1)} %bitcast.6, f32[4096,128]{1,0:T(8,128)S(1)} %copy-done, ...), custom_call_target="tpu_custom_call" | custom-call | tf_op jit(solution)/shard_map/image/pallas_call | solution.py:384
  18.0 0.7 %collective-permute-start.2 = (f32[32,128]{1,0:T(8,128)S(1)}, f32[32,128]{1,0:T(8,128)S(1)}, u32[]{:S(2)}, u32[]{:S(2)}) collective-permute-start(f32[32,128]{1,0:T(8,128)S(1)} %get-tuple-element.14.own_ref), channel_id=1, source_target_pairs={{0,2},{1,5},{2,0},{3,7},{4,6},{5,1},{6,4},{7,3},{8,10},{9,13},{10,... | collective-permute-start | bytes 49160 | tf_op jit(solution)/shard_map/ppermute | solution.py:339
  18.7 1.4 %collective-permute-start.1 = (f32[32,128]{1,0:T(8,128)S(1)}, f32[32,128]{1,0:T(8,128)S(1)}, u32[]{:S(2)}, u32[]{:S(2)}) collective-permute-start(f32[32,128]{1,0:T(8,128)S(1)} %get-tuple-element.14.own_ref), channel_id=1, source_target_pairs={{0,2},{1,7},{2,0},{3,5},{4,6},{5,3},{6,4},{7,1},{8,10},{9,15},{10,... | collective-permute-start | bytes 49160 | tf_op jit(solution)/shard_map/ppermute | solution.py:338
  20.1 1.7 %collective-permute-done.2.near_ref = f32[32,128]{1,0:T(8,128)S(1)} collective-permute-done((f32[32,128]{1,0:T(8,128)S(1)}, f32[32,128]{1,0:T(8,128)S(1)}, u32[]{:S(2)}, u32[]{:S(2)}) %collective-permute-start.2) | collective-permute-done | bytes 16416 | tf_op jit(solution)/shard_map/ppermute | solution.py:339
  21.8 0.6 %collective-permute-done.1.far_ref = f32[32,128]{1,0:T(8,128)S(1)} collective-permute-done((f32[32,128]{1,0:T(8,128)S(1)}, f32[32,128]{1,0:T(8,128)S(1)}, u32[]{:S(2)}, u32[]{:S(2)}) %collective-permute-start.1) | collective-permute-done | bytes 16416 | tf_op jit(solution)/shard_map/ppermute | solution.py:338
  22.4 0.1 collective-permute-start.3
  22.5 0.0 copy-done.1
  22.5 0.0 copy-done.2
  22.5 0.1 masks.1.refs_2_.refs_6_
  22.7 0.9 %collective-permute-done.3.refs_1_ = f32[32,128]{1,0:T(8,128)S(1)} collective-permute-done((f32[32,128]{1,0:T(8,128)S(1)}, f32[32,128]{1,0:T(8,128)S(1)}, u32[]{:S(2)}, u32[]{:S(2)}) %collective-permute-start.3) | collective-permute-done | bytes 16416 | tf_op jit(solution)/shard_map/ppermute | solution.py:317
  23.6 1.0 %cones.1 = (f32[32,128]{1,0:T(8,128)S(1)}, f32[8,128]{1,0:T(8,128)S(1)}, f32[8,128]{1,0:T(8,128)S(1)}, f32[8,128]{1,0:T(8,128)S(1)}) custom-call(f32[32,128]{1,0:T(8,128)S(1)} %merge.1.refs_0_, f32[32,128]{1,0:T(8,128)S(1)} %collective-permute-done.3.refs_1_, f32[16,32,128]{2,1,0:T(8,128)S(1)} %masks.1.refs_2_.refs_6_, ...), custom_call_target="tpu_custom_call" | custom-call | tf_op jit(solution)/shard_map/cones/pallas_call | solution.py:412
  24.6 0.4 %collective-permute-start.6 = (f32[8,128]{1,0:T(8,128)S(1)}, f32[8,128]{1,0:T(8,128)S(1)}, u32[]{:S(2)}, u32[]{:S(2)}) collective-permute-start(f32[8,128]{1,0:T(8,128)S(1)} %get-tuple-element.21), channel_id=1, source_target_pairs={{0,17},{1,16},{2,19},{3,18},{4,21},{5,20},{6,23},{7,22},{8,25},{9,... | collective-permute-start | bytes 12296 | tf_op jit(solution)/shard_map/ppermute | solution.py:323
  25.1 1.5 %collective-permute-start.5 = (f32[8,128]{1,0:T(8,128)S(1)}, f32[8,128]{1,0:T(8,128)S(1)}, u32[]{:S(2)}, u32[]{:S(2)}) collective-permute-start(f32[8,128]{1,0:T(8,128)S(1)} %get-tuple-element.21), channel_id=1, source_target_pairs={{0,25},{1,24},{2,27},{3,26},{4,29},{5,28},{6,31},{7,30},{8,17},{9,... | collective-permute-start | bytes 12296 | tf_op jit(solution)/shard_map/ppermute | solution.py:323
  26.5 1.2 %collective-permute-start.4 = (f32[8,128]{1,0:T(8,128)S(1)}, f32[8,128]{1,0:T(8,128)S(1)}, u32[]{:S(2)}, u32[]{:S(2)}) collective-permute-start(f32[8,128]{1,0:T(8,128)S(1)} %get-tuple-element.21), channel_id=1, source_target_pairs={{0,9},{1,8},{2,11},{3,10},{4,13},{5,12},{6,15},{7,14},{8,1},{9,0},... | collective-permute-start | bytes 12296 | tf_op jit(solution)/shard_map/ppermute | solution.py:323
  27.7 0.1 collective-permute-done.6.refs_3_
  27.7 1.2 %collective-permute-done.5.refs_2_ = f32[8,128]{1,0:T(8,128)S(1)} collective-permute-done((f32[8,128]{1,0:T(8,128)S(1)}, f32[8,128]{1,0:T(8,128)S(1)}, u32[]{:S(2)}, u32[]{:S(2)}) %collective-permute-start.5) | collective-permute-done | bytes 4128 | tf_op jit(solution)/shard_map/ppermute | solution.py:323
  29.0 0.6 %collective-permute-done.4.refs_1_ = f32[8,128]{1,0:T(8,128)S(1)} collective-permute-done((f32[8,128]{1,0:T(8,128)S(1)}, f32[8,128]{1,0:T(8,128)S(1)}, u32[]{:S(2)}, u32[]{:S(2)}) %collective-permute-start.4) | collective-permute-done | bytes 4128 | tf_op jit(solution)/shard_map/ppermute | solution.py:323
  29.6 0.6 %finish.1 = (f32[1,32]{1,0:T(1,128)}, f32[32,128]{1,0:T(8,128)}) custom-call(f32[8,128]{1,0:T(8,128)S(1)} %get-tuple-element.20.refs_0_, f32[8,128]{1,0:T(8,128)S(1)} %collective-permute-done.4.refs_1_, f32[8,128]{1,0:T(8,128)S(1)} %collective-permute-done.5.refs_2_, f32[8,128]{1,0:T(8,128)S(1)} %collective-permute-done.6.refs_3_, ...), custom_call_target="tpu_custom_call" | custom-call | tf_op jit(solution)/shard_map/finish/pallas_call | solution.py:428
  (1 shorter events, 0.0 us)
Async XLA Ops:
  0.6 15.9 %copy-start = (f32[4096,128]{1,0:T(8,128)S(1)}, f32[4096,128]{1,0:T(8,128)}, u32[]{:S(2)}) copy-start(f32[4096,128]{1,0:T(8,128)} %refs_0_.1) | copy-start | bytes 6291460
  0.6 15.9 %collective-permute-start = (f32[4096,128]{1,0:T(8,128)}, f32[4096,128]{1,0:T(8,128)S(1)}, u32[]{:S(2)}, u32[]{:S(2)}) collective-permute-start(f32[4096,128]{1,0:T(8,128)} %refs_0_.1), channel_id=1, source_target_pairs={{0,1},{1,0},{2,3},{3,2},{4,5},{5,4},{6,7},{7,6},{8,9},{9,8},{10,11... | collective-permute-start | bytes 6291464 | tf_op jit(solution)/shard_map/ppermute | solution.py:317
  16.5 6.0 %copy-start.1 = (s32[16384]{0:T(1024)S(1)}, s32[16384]{0:T(1024)}, u32[]{:S(2)}) copy-start(s32[16384]{0:T(1024)} %param.9) | copy-start | bytes 196612
  16.5 6.0 %copy-start.2 = (f32[16384]{0:T(1024)S(1)}, f32[16384]{0:T(1024)}, u32[]{:S(2)}) copy-start(f32[16384]{0:T(1024)} %param.8) | copy-start | bytes 196612
  18.0 3.8 %collective-permute-start.2 = (f32[32,128]{1,0:T(8,128)S(1)}, f32[32,128]{1,0:T(8,128)S(1)}, u32[]{:S(2)}, u32[]{:S(2)}) collective-permute-start(f32[32,128]{1,0:T(8,128)S(1)} %get-tuple-element.14.own_ref), channel_id=1, source_target_pairs={{0,2},{1,5},{2,0},{3,7},{4,6},{5,1},{6,4},{7,3},{8,10},{9,13},{10,... | collective-permute-start | bytes 49160 | tf_op jit(solution)/shard_map/ppermute | solution.py:339
  18.7 3.7 %collective-permute-start.1 = (f32[32,128]{1,0:T(8,128)S(1)}, f32[32,128]{1,0:T(8,128)S(1)}, u32[]{:S(2)}, u32[]{:S(2)}) collective-permute-start(f32[32,128]{1,0:T(8,128)S(1)} %get-tuple-element.14.own_ref), channel_id=1, source_target_pairs={{0,2},{1,7},{2,0},{3,5},{4,6},{5,3},{6,4},{7,1},{8,10},{9,15},{10,... | collective-permute-start | bytes 49160 | tf_op jit(solution)/shard_map/ppermute | solution.py:338
  22.4 1.2 %collective-permute-start.3 = (f32[32,128]{1,0:T(8,128)S(1)}, f32[32,128]{1,0:T(8,128)S(1)}, u32[]{:S(2)}, u32[]{:S(2)}) collective-permute-start(f32[32,128]{1,0:T(8,128)S(1)} %merge.1.refs_0_), channel_id=1, source_target_pairs={{0,1},{1,0},{2,3},{3,2},{4,5},{5,4},{6,7},{7,6},{8,9},{9,8},{10,11... | collective-permute-start | bytes 49160 | tf_op jit(solution)/shard_map/ppermute | solution.py:317
  24.6 3.1 %collective-permute-start.6 = (f32[8,128]{1,0:T(8,128)S(1)}, f32[8,128]{1,0:T(8,128)S(1)}, u32[]{:S(2)}, u32[]{:S(2)}) collective-permute-start(f32[8,128]{1,0:T(8,128)S(1)} %get-tuple-element.21), channel_id=1, source_target_pairs={{0,17},{1,16},{2,19},{3,18},{4,21},{5,20},{6,23},{7,22},{8,25},{9,... | collective-permute-start | bytes 12296 | tf_op jit(solution)/shard_map/ppermute | solution.py:323
  25.1 3.9 %collective-permute-start.5 = (f32[8,128]{1,0:T(8,128)S(1)}, f32[8,128]{1,0:T(8,128)S(1)}, u32[]{:S(2)}, u32[]{:S(2)}) collective-permute-start(f32[8,128]{1,0:T(8,128)S(1)} %get-tuple-element.21), channel_id=1, source_target_pairs={{0,25},{1,24},{2,27},{3,26},{4,29},{5,28},{6,31},{7,30},{8,17},{9,... | collective-permute-start | bytes 12296 | tf_op jit(solution)/shard_map/ppermute | solution.py:323
  26.5 3.0 %collective-permute-start.4 = (f32[8,128]{1,0:T(8,128)S(1)}, f32[8,128]{1,0:T(8,128)S(1)}, u32[]{:S(2)}, u32[]{:S(2)}) collective-permute-start(f32[8,128]{1,0:T(8,128)S(1)} %get-tuple-element.21), channel_id=1, source_target_pairs={{0,9},{1,8},{2,11},{3,10},{4,13},{5,12},{6,15},{7,14},{8,1},{9,0},... | collective-permute-start | bytes 12296 | tf_op jit(solution)/shard_map/ppermute | solution.py:323

commit v7 on v6

--- a/solution.py
+++ b/solution.py
@@ -197,11 +197,28 @@
             aux_ref[HEAD] = (1.0 - same) * (1.0 - opens)
 
 
+def products(left, high, low, scalars):
+    width = high.shape[1]
+    both = jnp.dot(left, jnp.concatenate([high, low], axis=1), preferred_element_type=F32)
+    half = 2 * TILE
+    sums = both[0:half, 0:width] + both[0:half, width : 2 * width] + both[half : 2 * half, 0:width]
+    sub = lax.broadcasted_iota(jnp.int32, (TILE, width), 0)
+    return jnp.where(
+        sub == BACK,
+        jnp.sum(sums[0:TILE, :], axis=0, keepdims=True),
+        jnp.where(sub <= TAIL_FIRST, sums[TILE:half, :], scalars),
+    )
+
+
+def own_kernel(left_ref, high_ref, low_ref, scalar_ref, out_ref):
+    out_ref[...] = products(left_ref[...], high_ref[...], low_ref[...], scalar_ref[...])
+
+
 def cone_kernel(count, *refs):
     parts = refs[:count]
-    aux_ref, *split_refs, proj_ref, edge_ref, own_ref, other_ref = refs[count:]
+    aux_ref, high_ref, low_ref, proj_ref, edge_ref, left_ref, scalar_ref, out_ref = refs[count:]
     own_rows = proj_ref.shape[0]
-    width = own_ref.shape[1]
+    width = out_ref.shape[1]
     slack = aux_ref[TARGET] - tree(p[...] for p in parts)
     head, first, last = aux_ref[HEAD], aux_ref[FIRST], aux_ref[LAST]
     square = (1.0 - head) * slack * slack
@@ -237,7 +254,6 @@
         low = (jnp.concatenate([interior, edge], axis=0) - high.astype(F32)).astype(BF16)
         pieces.append(jnp.concatenate([high, low], axis=0))
     left = jnp.concatenate(pieces, axis=1)
-    both = jnp.dot(left, jnp.concatenate([ref[...] for ref in split_refs], axis=1), preferred_element_type=F32)
     ends = slack[final:, :]
     scalars = jnp.where(
         sub == SQUARE_LAST,
@@ -245,16 +261,9 @@
         jnp.where(sub == LEAD_LAST, lead * ends, jnp.where(sub == SQUARE_FIRST, begin * slack[0:1, :], 0.0)),
     )
     scalars = jnp.broadcast_to(jnp.sum(scalars, axis=1, keepdims=True), (TILE, width))
-    wide_sub = lax.broadcasted_iota(jnp.int32, (TILE, width), 0)
-    half = 2 * TILE
-    for place, ref in enumerate((own_ref, other_ref)):
-        block = both[:, place * 2 * width : (place + 1) * 2 * width]
-        sums = block[0:half, 0:width] + block[0:half, width : 2 * width] + block[half : 2 * half, 0:width]
-        ref[...] = jnp.where(
-            wide_sub == BACK,
-            jnp.sum(sums[0:TILE, :], axis=0, keepdims=True),
-            jnp.where(wide_sub <= TAIL_FIRST, sums[TILE:half, :], scalars),
-        )
+    left_ref[...] = left
+    scalar_ref[...] = scalars
+    out_ref[...] = products(left, high_ref[...], low_ref[...], scalars)
     edge_ref[...] = jnp.where(sub == 0, slack[0:1, :], ends)
 
 
@@ -409,19 +418,28 @@
     )(cone_id.reshape(-1, LANES), target.reshape(-1, LANES), blended)
 
     parts = reduce_chips(part, col_count)
-    projected, edge, own, other = pl.pallas_call(
+    projected, edge, left, scalars, other = pl.pallas_call(
         functools.partial(cone_kernel, len(parts)),
         name="cones",
-        in_specs=[vmem()] * (len(parts) + 5),
-        out_specs=[vmem()] * 4,
+        in_specs=[vmem()] * (len(parts) + 3),
+        out_specs=[vmem()] * 5,
         out_shape=[
             jax.ShapeDtypeStruct((own_rows, LANES), F32),
             jax.ShapeDtypeStruct((TILE, LANES), F32),
+            jax.ShapeDtypeStruct((4 * TILE, row_block), BF16),
             jax.ShapeDtypeStruct((TILE, width), F32),
             jax.ShapeDtypeStruct((TILE, width), F32),
         ],
         compiler_params=params(8 * operator.size),
-    )(*parts, aux, *halves)
+    )(*parts, aux, *halves[2:])
+    own = pl.pallas_call(
+        own_kernel,
+        name="own",
+        in_specs=[vmem()] * 4,
+        out_specs=vmem(),
+        out_shape=jax.ShapeDtypeStruct((TILE, width), F32),
+        compiler_params=params(8 * operator.size),
+    )(left, *halves[:2], scalars)
 
     turns = [0, 1, *range(3, row_count), 2]
     messages = [own, *exchange_rows(other)]

time: 30.4 us -> 30 us (0.987)
  waiting for transfers between devices: 5.14 us -> 4.66 us
    ppermute x3, waiting for transfers between devices: 1.88 us -> 1.37 us  [exchange_rows(): lax.ppermute(x, ('row', 'col'), [(r * cols + c, (r ^ turn) * cols + (c ^...]
    pallas_call x0 -> x1, Pallas kernels: none -> 0.48 us  [body(): pl.pallas_call(own_kernel, name='own', in_specs=[vmem()] * 4, out_specs=v...]
    pallas_call x1, Pallas kernels: 1.02 us -> 0.58 us  [body(): pl.pallas_call(functools.partial(cone_kernel, len(parts)), name='cones',...]
  transfers between devices with their start and end apart: 7 -> 7, of which waited for: 6 -> 5; matrix products, arithmetic and copies ran while one was open for 0% -> 0% of each run, Pallas kernels for 4% -> 6%
where the time goes in v7:
time: 30 us; the launch traced here: 29.8 us
  blocking collectives  14.2 us (47%)
  starting transfers between devices  5.77 us (19%)
  waiting for transfers between devices  4.66 us (16%)
  Pallas kernels  4.41 us (15%)
  between operations  0.7 us (2%)
    all_to_all x1, blocking collectives, body(): received = lax.all_to_all(message, ('col', 'row'), 0, 0, tiled=True)  14.2 us
    ppermute x3, starting transfers between devices, exchange_rows(): lax.ppermute(x, ('row', 'col'), [(r * cols + c, (r ^ turn) * cols + (c ^...  3.04 us
    ppermute x1, waiting for transfers between devices, reduce_chips(): lax.ppermute(x, 'col', [(i, i ^ (2 * bit if i % 2 else bit)) for i in ran...  1.71 us
    pallas_call x1, Pallas kernels, body(): pl.pallas_call(functools.partial(image_kernel, hist, local, row_count, mi...  1.46 us
    ppermute x1, starting transfers between devices, reduce_chips(): lax.ppermute(x, 'col', [(i, i ^ (3 * bit if i % 2 else bit)) for i in ran...  1.42 us
    ppermute x3, waiting for transfers between devices, exchange_rows(): lax.ppermute(x, ('row', 'col'), [(r * cols + c, (r ^ turn) * cols + (c ^...  1.37 us
    pallas_call x1, Pallas kernels, body(): pl.pallas_call(functools.partial(pack_kernel, hist, local), name='pack',...  1.1 us
    ppermute x2, waiting for transfers between devices, exchange(): lax.ppermute(x, axis, [(i, i ^ turn) for i in range(count)])  0.96 us
  transfers between devices with their start and end apart: 7, of which 5 were waited for; matrix products, arithmetic and copies ran while one was open for 0% of the time, Pallas kernels for 6%

profile of v7, /device:TPU:0, one launch (start us, length us, event | category | flops | bytes accessed | tf_op | source)
XLA Modules:
  0.0 29.8 jit_solution(16900362300455860652)
XLA Ops:
  0.6 0.0 copy-start
  0.6 0.6 %collective-permute-start = (f32[4096,128]{1,0:T(8,128)}, f32[4096,128]{1,0:T(8,128)S(1)}, u32[]{:S(2)}, u32[]{:S(2)}) collective-permute-start(f32[4096,128]{1,0:T(8,128)} %refs_0_.1), channel_id=1, source_target_pairs={{0,1},{1,0},{2,3},{3,2},{4,5},{5,4},{6,7},{7,6},{8,9},{9,8},{10,11... | collective-permute-start | bytes 6291464 | tf_op jit(solution)/shard_map/ppermute | solution.py:326
  1.2 1.1 %pack.1 = f32[128,128]{1,0:T(8,128)S(1)} custom-call(f32[11,32]{1,0:T(8,128)} %x_any.1, f32[11,32]{1,0:T(8,128)} %f_any.1), custom_call_target="tpu_custom_call" | custom-call | flops 10000000000 | bytes 40000000 | tf_op jit(solution)/shard_map/pack/pallas_call | solution.py:375
  2.3 14.2 %all_to_all.11 = f32[32,4,128]{2,1,0:T(4,128)S(1)} all-to-all(f32[32,4,128]{2,1,0:T(4,128)S(1)} %bitcast.7), channel_id=1, replica_groups=mesh['row'=4,'col'=8] {'col','row'}, dimensions={0} | all-to-all | bytes 131072 | tf_op jit(solution)/shard_map/all_to_all | solution.py:391
  16.5 0.0 collective-permute-done.refs_1_
  16.5 0.0 copy-done
  16.5 0.0 copy-start.1
  16.5 0.0 copy-start.2
  16.5 1.5 %image.1 = (bf16[4096,128]{1,0:T(8,128)(2,1)S(1)}, bf16[4096,128]{1,0:T(8,128)(2,1)S(1)}, bf16[4096,128]{1,0:T(8,128)(2,1)S(1)}, bf16[4096,128]{1,0:T(8,128)(2,1...) custom-call(f32[128,128]{1,0:T(8,128)S(1)} %bitcast.6, f32[4096,128]{1,0:T(8,128)S(1)} %copy-done, ...), custom_call_target="tpu_custom_call" | custom-call | tf_op jit(solution)/shard_map/image/pallas_call | solution.py:393
  18.0 0.7 %collective-permute-start.2 = (f32[32,128]{1,0:T(8,128)S(1)}, f32[32,128]{1,0:T(8,128)S(1)}, u32[]{:S(2)}, u32[]{:S(2)}) collective-permute-start(f32[32,128]{1,0:T(8,128)S(1)} %get-tuple-element.15.own_ref), channel_id=1, source_target_pairs={{0,2},{1,5},{2,0},{3,7},{4,6},{5,1},{6,4},{7,3},{8,10},{9,13},{10,... | collective-permute-start | bytes 49160 | tf_op jit(solution)/shard_map/ppermute | solution.py:348
  18.7 1.4 %collective-permute-start.1 = (f32[32,128]{1,0:T(8,128)S(1)}, f32[32,128]{1,0:T(8,128)S(1)}, u32[]{:S(2)}, u32[]{:S(2)}) collective-permute-start(f32[32,128]{1,0:T(8,128)S(1)} %get-tuple-element.15.own_ref), channel_id=1, source_target_pairs={{0,2},{1,7},{2,0},{3,5},{4,6},{5,3},{6,4},{7,1},{8,10},{9,15},{10,... | collective-permute-start | bytes 49160 | tf_op jit(solution)/shard_map/ppermute | solution.py:347
  20.1 1.7 %collective-permute-done.2.near_ref = f32[32,128]{1,0:T(8,128)S(1)} collective-permute-done((f32[32,128]{1,0:T(8,128)S(1)}, f32[32,128]{1,0:T(8,128)S(1)}, u32[]{:S(2)}, u32[]{:S(2)}) %collective-permute-start.2) | collective-permute-done | bytes 16416 | tf_op jit(solution)/shard_map/ppermute | solution.py:348
  21.8 0.6 %collective-permute-done.1.far_ref = f32[32,128]{1,0:T(8,128)S(1)} collective-permute-done((f32[32,128]{1,0:T(8,128)S(1)}, f32[32,128]{1,0:T(8,128)S(1)}, u32[]{:S(2)}, u32[]{:S(2)}) %collective-permute-start.1) | collective-permute-done | bytes 16416 | tf_op jit(solution)/shard_map/ppermute | solution.py:347
  22.4 0.1 collective-permute-start.3
  22.5 0.0 copy-done.1
  22.5 0.0 copy-done.2
  22.5 0.1 masks.1.refs_2_.refs_6_
  22.7 1.0 %collective-permute-done.3.refs_1_ = f32[32,128]{1,0:T(8,128)S(1)} collective-permute-done((f32[32,128]{1,0:T(8,128)S(1)}, f32[32,128]{1,0:T(8,128)S(1)}, u32[]{:S(2)}, u32[]{:S(2)}) %collective-permute-start.3) | collective-permute-done | bytes 16416 | tf_op jit(solution)/shard_map/ppermute | solution.py:326
  23.6 0.6 %cones.1 = (f32[32,128]{1,0:T(8,128)S(1)}, f32[8,128]{1,0:T(8,128)S(1)}, bf16[32,4096]{1,0:T(8,128)(2,1)S(1)}, f32[8,128]{1,0:T(8,128)S(1)}, f32[8,128]{1,0:T(8,128)S(1)}) custom-call(f32[32,128]{1,0:T(8,128)S(1)} %merge.1.refs_0_, f32[32,128]{1,0:T(8,128)S(1)} %collective-permute-done.3.refs_1_, f32[16,32,128]{2,1,0:T(8,128)S(1)} %masks.1.refs_2_.refs_6_, ...), custom_call_target="tpu_custom_call" | custom-call | tf_op jit(solution)/shard_map/cones/pallas_call | solution.py:421
  24.2 0.4 %collective-permute-start.6 = (f32[8,128]{1,0:T(8,128)S(1)}, f32[8,128]{1,0:T(8,128)S(1)}, u32[]{:S(2)}, u32[]{:S(2)}) collective-permute-start(f32[8,128]{1,0:T(8,128)S(1)} %get-tuple-element.23), channel_id=1, source_target_pairs={{0,17},{1,16},{2,19},{3,18},{4,21},{5,20},{6,23},{7,22},{8,25},{9,... | collective-permute-start | bytes 12296 | tf_op jit(solution)/shard_map/ppermute | solution.py:332
  24.6 1.5 %collective-permute-start.5 = (f32[8,128]{1,0:T(8,128)S(1)}, f32[8,128]{1,0:T(8,128)S(1)}, u32[]{:S(2)}, u32[]{:S(2)}) collective-permute-start(f32[8,128]{1,0:T(8,128)S(1)} %get-tuple-element.23), channel_id=1, source_target_pairs={{0,25},{1,24},{2,27},{3,26},{4,29},{5,28},{6,31},{7,30},{8,17},{9,... | collective-permute-start | bytes 12296 | tf_op jit(solution)/shard_map/ppermute | solution.py:332
  26.1 1.2 %collective-permute-start.4 = (f32[8,128]{1,0:T(8,128)S(1)}, f32[8,128]{1,0:T(8,128)S(1)}, u32[]{:S(2)}, u32[]{:S(2)}) collective-permute-start(f32[8,128]{1,0:T(8,128)S(1)} %get-tuple-element.23), channel_id=1, source_target_pairs={{0,9},{1,8},{2,11},{3,10},{4,13},{5,12},{6,15},{7,14},{8,1},{9,0},... | collective-permute-start | bytes 12296 | tf_op jit(solution)/shard_map/ppermute | solution.py:332
  27.3 0.5 %own.1.refs_0_ = f32[8,128]{1,0:T(8,128)S(1)} custom-call(bf16[32,4096]{1,0:T(8,128)(2,1)S(1)} %get-tuple-element.19.left_ref, bf16[4096,128]{1,0:T(8,128)(2,1)S(1)} %get-tuple-element.20.high_ref, bf16[4096,128]{1,0:T(8,128)(2,1)S(1)} %get-tuple-element.21.low_ref, f32[8,128]{1,0:T(8,128)S(1)} %get-tuple-element.22.scalar_ref), custom_call_target="tpu_custom_call" | custom-call | tf_op jit(solution)/shard_map/own/pallas_call | solution.py:435
  27.7 0.0 collective-permute-done.6.refs_3_
  27.8 0.8 %collective-permute-done.5.refs_2_ = f32[8,128]{1,0:T(8,128)S(1)} collective-permute-done((f32[8,128]{1,0:T(8,128)S(1)}, f32[8,128]{1,0:T(8,128)S(1)}, u32[]{:S(2)}, u32[]{:S(2)}) %collective-permute-start.5) | collective-permute-done | bytes 4128 | tf_op jit(solution)/shard_map/ppermute | solution.py:332
  28.5 0.6 %collective-permute-done.4.refs_1_ = f32[8,128]{1,0:T(8,128)S(1)} collective-permute-done((f32[8,128]{1,0:T(8,128)S(1)}, f32[8,128]{1,0:T(8,128)S(1)}, u32[]{:S(2)}, u32[]{:S(2)}) %collective-permute-start.4) | collective-permute-done | bytes 4128 | tf_op jit(solution)/shard_map/ppermute | solution.py:332
  29.1 0.6 %finish.1 = (f32[1,32]{1,0:T(1,128)}, f32[32,128]{1,0:T(8,128)}) custom-call(f32[8,128]{1,0:T(8,128)S(1)} %own.1.refs_0_, f32[8,128]{1,0:T(8,128)S(1)} %collective-permute-done.4.refs_1_, f32[8,128]{1,0:T(8,128)S(1)} %collective-permute-done.5.refs_2_, f32[8,128]{1,0:T(8,128)S(1)} %collective-permute-done.6.refs_3_, ...), custom_call_target="tpu_custom_call" | custom-call | tf_op jit(solution)/shard_map/finish/pallas_call | solution.py:446
  (1 shorter events, 0.0 us)
Async XLA Ops:
  0.6 15.9 %copy-start = (f32[4096,128]{1,0:T(8,128)S(1)}, f32[4096,128]{1,0:T(8,128)}, u32[]{:S(2)}) copy-start(f32[4096,128]{1,0:T(8,128)} %refs_0_.1) | copy-start | bytes 6291460
  0.6 15.9 %collective-permute-start = (f32[4096,128]{1,0:T(8,128)}, f32[4096,128]{1,0:T(8,128)S(1)}, u32[]{:S(2)}, u32[]{:S(2)}) collective-permute-start(f32[4096,128]{1,0:T(8,128)} %refs_0_.1), channel_id=1, source_target_pairs={{0,1},{1,0},{2,3},{3,2},{4,5},{5,4},{6,7},{7,6},{8,9},{9,8},{10,11... | collective-permute-start | bytes 6291464 | tf_op jit(solution)/shard_map/ppermute | solution.py:326
  16.5 6.0 %copy-start.1 = (s32[16384]{0:T(1024)S(1)}, s32[16384]{0:T(1024)}, u32[]{:S(2)}) copy-start(s32[16384]{0:T(1024)} %param.9) | copy-start | bytes 196612
  16.5 6.0 %copy-start.2 = (f32[16384]{0:T(1024)S(1)}, f32[16384]{0:T(1024)}, u32[]{:S(2)}) copy-start(f32[16384]{0:T(1024)} %param.8) | copy-start | bytes 196612
  18.0 3.8 %collective-permute-start.2 = (f32[32,128]{1,0:T(8,128)S(1)}, f32[32,128]{1,0:T(8,128)S(1)}, u32[]{:S(2)}, u32[]{:S(2)}) collective-permute-start(f32[32,128]{1,0:T(8,128)S(1)} %get-tuple-element.15.own_ref), channel_id=1, source_target_pairs={{0,2},{1,5},{2,0},{3,7},{4,6},{5,1},{6,4},{7,3},{8,10},{9,13},{10,... | collective-permute-start | bytes 49160 | tf_op jit(solution)/shard_map/ppermute | solution.py:348
  18.7 3.8 %collective-permute-start.1 = (f32[32,128]{1,0:T(8,128)S(1)}, f32[32,128]{1,0:T(8,128)S(1)}, u32[]{:S(2)}, u32[]{:S(2)}) collective-permute-start(f32[32,128]{1,0:T(8,128)S(1)} %get-tuple-element.15.own_ref), channel_id=1, source_target_pairs={{0,2},{1,7},{2,0},{3,5},{4,6},{5,3},{6,4},{7,1},{8,10},{9,15},{10,... | collective-permute-start | bytes 49160 | tf_op jit(solution)/shard_map/ppermute | solution.py:347
  22.4 1.2 %collective-permute-start.3 = (f32[32,128]{1,0:T(8,128)S(1)}, f32[32,128]{1,0:T(8,128)S(1)}, u32[]{:S(2)}, u32[]{:S(2)}) collective-permute-start(f32[32,128]{1,0:T(8,128)S(1)} %merge.1.refs_0_), channel_id=1, source_target_pairs={{0,1},{1,0},{2,3},{3,2},{4,5},{5,4},{6,7},{7,6},{8,9},{9,8},{10,11... | collective-permute-start | bytes 49160 | tf_op jit(solution)/shard_map/ppermute | solution.py:326
  24.2 3.5 %collective-permute-start.6 = (f32[8,128]{1,0:T(8,128)S(1)}, f32[8,128]{1,0:T(8,128)S(1)}, u32[]{:S(2)}, u32[]{:S(2)}) collective-permute-start(f32[8,128]{1,0:T(8,128)S(1)} %get-tuple-element.23), channel_id=1, source_target_pairs={{0,17},{1,16},{2,19},{3,18},{4,21},{5,20},{6,23},{7,22},{8,25},{9,... | collective-permute-start | bytes 12296 | tf_op jit(solution)/shard_map/ppermute | solution.py:332
  24.6 3.9 %collective-permute-start.5 = (f32[8,128]{1,0:T(8,128)S(1)}, f32[8,128]{1,0:T(8,128)S(1)}, u32[]{:S(2)}, u32[]{:S(2)}) collective-permute-start(f32[8,128]{1,0:T(8,128)S(1)} %get-tuple-element.23), channel_id=1, source_target_pairs={{0,25},{1,24},{2,27},{3,26},{4,29},{5,28},{6,31},{7,30},{8,17},{9,... | collective-permute-start | bytes 12296 | tf_op jit(solution)/shard_map/ppermute | solution.py:332
  26.1 3.0 %collective-permute-start.4 = (f32[8,128]{1,0:T(8,128)S(1)}, f32[8,128]{1,0:T(8,128)S(1)}, u32[]{:S(2)}, u32[]{:S(2)}) collective-permute-start(f32[8,128]{1,0:T(8,128)S(1)} %get-tuple-element.23), channel_id=1, source_target_pairs={{0,9},{1,8},{2,11},{3,10},{4,13},{5,12},{6,15},{7,14},{8,1},{9,0},... | collective-permute-start | bytes 12296 | tf_op jit(solution)/shard_map/ppermute | solution.py:332

commit v8 on v7

--- a/solution.py
+++ b/solution.py
@@ -29,10 +29,6 @@
     return pl.BlockSpec(memory_space=pltpu.VMEM)
 
 
-def hbm(x):
-    return pltpu.with_memory_space_constraint(x, pltpu.HBM)
-
-
 def tree(terms):
     terms = list(terms)
     while len(terms) > 1:
@@ -58,16 +54,15 @@
     return wide, LANES // local, wide * local // LANES
 
 
-def pack_kernel(hist, local, x_any, f_any, out_ref, x_ref, f_ref, dirs_ref, diff_ref, sems):
+def token_kernel(out_ref):
+    out_ref[...] = jnp.zeros_like(out_ref)
+
+
+def pack_kernel(hist, local, token_ref, x_ref, f_ref, out_ref, dirs_ref, diff_ref):
     wide, group, rows = dims(hist, local)
     pieces = -(-hist // TILE)
-    copies = [pltpu.make_async_copy(a, b, sems.at[i]) for i, (a, b) in enumerate(((x_any, x_ref), (f_any, f_ref)))]
-    for copy in copies:
-        copy.start()
     dirs_ref[...] = jnp.zeros_like(dirs_ref)
     diff_ref[...] = jnp.zeros_like(diff_ref)
-    for copy in copies:
-        copy.wait()
     delta_f = f_ref[1 : hist + 1, :] - f_ref[0:hist, :]
     delta_x = x_ref[1 : hist + 1, :] - x_ref[0:hist, :]
     last_f = f_ref[hist : hist + 1, :]
@@ -372,22 +367,27 @@
     own_rows = row_block // LANES
 
     (other,) = exchange(operator, "col", [1])
+    token = pl.pallas_call(
+        token_kernel,
+        name="token",
+        out_specs=vmem(),
+        out_shape=jax.ShapeDtypeStruct((TILE, LANES), F32),
+        cost_estimate=pl.CostEstimate(flops=10**10, bytes_accessed=4 * 10**7, transcendentals=0),
+        compiler_params=params(),
+    )()
     message = pl.pallas_call(
         functools.partial(pack_kernel, hist, local),
         name="pack",
-        in_specs=[pl.BlockSpec(memory_space=pltpu.HBM)] * 2,
+        in_specs=[vmem()] * 3,
         out_specs=vmem(),
         out_shape=jax.ShapeDtypeStruct((row_count * col_count * rows, LANES), F32),
         scratch_shapes=[
-            pltpu.VMEM((hist + 1, local), F32),
-            pltpu.VMEM((hist + 1, local), F32),
             pltpu.VMEM((wide, LANES), F32),
             pltpu.VMEM((-(-hist // TILE) * LANES, local), F32),
-            pltpu.SemaphoreType.DMA((2,)),
         ],
         cost_estimate=pl.CostEstimate(flops=10**10, bytes_accessed=4 * 10**7, transcendentals=0),
         compiler_params=params(),
-    )(hbm(iterates), hbm(residuals))
+    )(token, iterates, residuals)
     received = lax.all_to_all(message, ("col", "row"), 0, 0, tiled=True)
 
     *halves, part, blended = pl.pallas_call(

time: 30 us -> 29.8 us (level)
  Pallas kernels: 4.41 us -> 3.62 us
  blocking collectives: 14.2 us -> 14.6 us
    pallas_call x1, Pallas kernels: 1.1 us -> 0.31 us  [body(): pl.pallas_call(functools.partial(pack_kernel, hist, local), name='pack',...]
    all_to_all x1, blocking collectives: 14.2 us -> 14.6 us  [body(): received = lax.all_to_all(message, ('col', 'row'), 0, 0, tiled=True)]
  transfers between devices with their start and end apart: 7 -> 7, of which waited for: 5 -> 5; matrix products, arithmetic and copies ran while one was open for 0% -> 0% of each run, Pallas kernels for 6% -> 3%
where the time goes in v8:
time: 29.8 us; the launch traced here: 29.5 us
  blocking collectives  14.6 us (49%)
  starting transfers between devices  5.77 us (19%)
  waiting for transfers between devices  4.67 us (16%)
  Pallas kernels  3.62 us (12%)
  between operations  0.71 us (2%)
    all_to_all x1, blocking collectives, body(): received = lax.all_to_all(message, ('col', 'row'), 0, 0, tiled=True)  14.6 us
    ppermute x3, starting transfers between devices, exchange_rows(): lax.ppermute(x, ('row', 'col'), [(r * cols + c, (r ^ turn) * cols + (c ^...  3.04 us
    ppermute x1, waiting for transfers between devices, reduce_chips(): lax.ppermute(x, 'col', [(i, i ^ (2 * bit if i % 2 else bit)) for i in ran...  1.71 us
    pallas_call x1, Pallas kernels, body(): pl.pallas_call(functools.partial(image_kernel, hist, local, row_count, mi...  1.46 us
    ppermute x1, starting transfers between devices, reduce_chips(): lax.ppermute(x, 'col', [(i, i ^ (3 * bit if i % 2 else bit)) for i in ran...  1.42 us
    ppermute x3, waiting for transfers between devices, exchange_rows(): lax.ppermute(x, ('row', 'col'), [(r * cols + c, (r ^ turn) * cols + (c ^...  1.37 us
    ppermute x2, waiting for transfers between devices, exchange(): lax.ppermute(x, axis, [(i, i ^ turn) for i in range(count)])  0.96 us
    ppermute x1, starting transfers between devices, reduce_chips(): lax.ppermute(x, 'col', [(i, i ^ (2 * bit if i % 2 else bit)) for i in ran...  0.67 us
  transfers between devices with their start and end apart: 7, of which 5 were waited for; matrix products, arithmetic and copies ran while one was open for 0% of the time, Pallas kernels for 3%

profile of v8, /device:TPU:0, one launch (start us, length us, event | category | flops | bytes accessed | tf_op | source)
XLA Modules:
  0.0 29.5 jit_solution(2199902887376541333)
XLA Ops:
  0.6 0.0 copy-start.4
  0.6 0.0 copy-start.3
  0.6 0.6 %collective-permute-start = (f32[4096,128]{1,0:T(8,128)}, f32[4096,128]{1,0:T(8,128)S(1)}, u32[]{:S(2)}, u32[]{:S(2)}) collective-permute-start(f32[4096,128]{1,0:T(8,128)} %refs_0_.1), channel_id=1, source_target_pairs={{0,1},{1,0},{2,3},{3,2},{4,5},{5,4},{6,7},{7,6},{8,9},{9,8},{10,11... | collective-permute-start | bytes 6291464 | tf_op jit(solution)/shard_map/ppermute | solution.py:321
  1.2 0.1 copy-done.4
  1.3 0.0 copy-done.3
  1.3 0.0 copy-start
  1.3 0.3 %pack.1 = f32[128,128]{1,0:T(8,128)S(1)} custom-call(f32[8,128]{1,0:T(8,128)S(1)} %token_.1.token_ref, f32[11,32]{1,0:T(8,128)S(1)} %copy-done.3, f32[11,32]{1,0:T(8,128)S(1)} %copy-done.4), custom_call_target="tpu_custom_call" | custom-call | flops 10000000000 | bytes 40000000 | tf_op jit(solution)/shard_map/pack/pallas_call | solution.py:378
  1.7 14.6 %all_to_all.11 = f32[32,4,128]{2,1,0:T(4,128)S(1)} all-to-all(f32[32,4,128]{2,1,0:T(4,128)S(1)} %bitcast.7), channel_id=1, replica_groups=mesh['row'=4,'col'=8] {'col','row'}, dimensions={0} | all-to-all | bytes 131072 | tf_op jit(solution)/shard_map/all_to_all | solution.py:391
  16.3 0.0 collective-permute-done.refs_1_
  16.3 0.0 copy-done
  16.3 0.0 copy-start.1
  16.3 0.0 copy-start.2
  16.3 1.5 %image.1 = (bf16[4096,128]{1,0:T(8,128)(2,1)S(1)}, bf16[4096,128]{1,0:T(8,128)(2,1)S(1)}, bf16[4096,128]{1,0:T(8,128)(2,1)S(1)}, bf16[4096,128]{1,0:T(8,128)(2,1...) custom-call(f32[128,128]{1,0:T(8,128)S(1)} %bitcast.6, f32[4096,128]{1,0:T(8,128)S(1)} %copy-done, ...), custom_call_target="tpu_custom_call" | custom-call | tf_op jit(solution)/shard_map/image/pallas_call | solution.py:393
  17.8 0.7 %collective-permute-start.2 = (f32[32,128]{1,0:T(8,128)S(1)}, f32[32,128]{1,0:T(8,128)S(1)}, u32[]{:S(2)}, u32[]{:S(2)}) collective-permute-start(f32[32,128]{1,0:T(8,128)S(1)} %get-tuple-element.15.own_ref), channel_id=1, source_target_pairs={{0,2},{1,5},{2,0},{3,7},{4,6},{5,1},{6,4},{7,3},{8,10},{9,13},{10,... | collective-permute-start | bytes 49160 | tf_op jit(solution)/shard_map/ppermute | solution.py:343
  18.5 1.4 %collective-permute-start.1 = (f32[32,128]{1,0:T(8,128)S(1)}, f32[32,128]{1,0:T(8,128)S(1)}, u32[]{:S(2)}, u32[]{:S(2)}) collective-permute-start(f32[32,128]{1,0:T(8,128)S(1)} %get-tuple-element.15.own_ref), channel_id=1, source_target_pairs={{0,2},{1,7},{2,0},{3,5},{4,6},{5,3},{6,4},{7,1},{8,10},{9,15},{10,... | collective-permute-start | bytes 49160 | tf_op jit(solution)/shard_map/ppermute | solution.py:342
  19.9 1.7 %collective-permute-done.2.near_ref = f32[32,128]{1,0:T(8,128)S(1)} collective-permute-done((f32[32,128]{1,0:T(8,128)S(1)}, f32[32,128]{1,0:T(8,128)S(1)}, u32[]{:S(2)}, u32[]{:S(2)}) %collective-permute-start.2) | collective-permute-done | bytes 16416 | tf_op jit(solution)/shard_map/ppermute | solution.py:343
  21.6 0.6 %collective-permute-done.1.far_ref = f32[32,128]{1,0:T(8,128)S(1)} collective-permute-done((f32[32,128]{1,0:T(8,128)S(1)}, f32[32,128]{1,0:T(8,128)S(1)}, u32[]{:S(2)}, u32[]{:S(2)}) %collective-permute-start.1) | collective-permute-done | bytes 16416 | tf_op jit(solution)/shard_map/ppermute | solution.py:342
  22.2 0.1 collective-permute-start.3
  22.3 0.0 copy-done.1
  22.3 0.0 copy-done.2
  22.3 0.1 masks.1.refs_2_.refs_6_
  22.4 1.0 %collective-permute-done.3.refs_1_ = f32[32,128]{1,0:T(8,128)S(1)} collective-permute-done((f32[32,128]{1,0:T(8,128)S(1)}, f32[32,128]{1,0:T(8,128)S(1)}, u32[]{:S(2)}, u32[]{:S(2)}) %collective-permute-start.3) | collective-permute-done | bytes 16416 | tf_op jit(solution)/shard_map/ppermute | solution.py:321
  23.4 0.6 %cones.1 = (f32[32,128]{1,0:T(8,128)S(1)}, f32[8,128]{1,0:T(8,128)S(1)}, bf16[32,4096]{1,0:T(8,128)(2,1)S(1)}, f32[8,128]{1,0:T(8,128)S(1)}, f32[8,128]{1,0:T(8,128)S(1)}) custom-call(f32[32,128]{1,0:T(8,128)S(1)} %merge.1.refs_0_, f32[32,128]{1,0:T(8,128)S(1)} %collective-permute-done.3.refs_1_, f32[16,32,128]{2,1,0:T(8,128)S(1)} %masks.1.refs_2_.refs_6_, ...), custom_call_target="tpu_custom_call" | custom-call | tf_op jit(solution)/shard_map/cones/pallas_call | solution.py:421
  24.0 0.4 %collective-permute-start.6 = (f32[8,128]{1,0:T(8,128)S(1)}, f32[8,128]{1,0:T(8,128)S(1)}, u32[]{:S(2)}, u32[]{:S(2)}) collective-permute-start(f32[8,128]{1,0:T(8,128)S(1)} %get-tuple-element.23), channel_id=1, source_target_pairs={{0,17},{1,16},{2,19},{3,18},{4,21},{5,20},{6,23},{7,22},{8,25},{9,... | collective-permute-start | bytes 12296 | tf_op jit(solution)/shard_map/ppermute | solution.py:327
  24.4 1.5 %collective-permute-start.5 = (f32[8,128]{1,0:T(8,128)S(1)}, f32[8,128]{1,0:T(8,128)S(1)}, u32[]{:S(2)}, u32[]{:S(2)}) collective-permute-start(f32[8,128]{1,0:T(8,128)S(1)} %get-tuple-element.23), channel_id=1, source_target_pairs={{0,25},{1,24},{2,27},{3,26},{4,29},{5,28},{6,31},{7,30},{8,17},{9,... | collective-permute-start | bytes 12296 | tf_op jit(solution)/shard_map/ppermute | solution.py:327
  25.9 1.2 %collective-permute-start.4 = (f32[8,128]{1,0:T(8,128)S(1)}, f32[8,128]{1,0:T(8,128)S(1)}, u32[]{:S(2)}, u32[]{:S(2)}) collective-permute-start(f32[8,128]{1,0:T(8,128)S(1)} %get-tuple-element.23), channel_id=1, source_target_pairs={{0,9},{1,8},{2,11},{3,10},{4,13},{5,12},{6,15},{7,14},{8,1},{9,0},... | collective-permute-start | bytes 12296 | tf_op jit(solution)/shard_map/ppermute | solution.py:327
  27.0 0.5 %own.1.refs_0_ = f32[8,128]{1,0:T(8,128)S(1)} custom-call(bf16[32,4096]{1,0:T(8,128)(2,1)S(1)} %get-tuple-element.19.left_ref, bf16[4096,128]{1,0:T(8,128)(2,1)S(1)} %get-tuple-element.20.high_ref, bf16[4096,128]{1,0:T(8,128)(2,1)S(1)} %get-tuple-element.21.low_ref, f32[8,128]{1,0:T(8,128)S(1)} %get-tuple-element.22.scalar_ref), custom_call_target="tpu_custom_call" | custom-call | tf_op jit(solution)/shard_map/own/pallas_call | solution.py:435
  27.5 0.0 collective-permute-done.6.refs_3_
  27.5 0.8 %collective-permute-done.5.refs_2_ = f32[8,128]{1,0:T(8,128)S(1)} collective-permute-done((f32[8,128]{1,0:T(8,128)S(1)}, f32[8,128]{1,0:T(8,128)S(1)}, u32[]{:S(2)}, u32[]{:S(2)}) %collective-permute-start.5) | collective-permute-done | bytes 4128 | tf_op jit(solution)/shard_map/ppermute | solution.py:327
  28.3 0.6 %collective-permute-done.4.refs_1_ = f32[8,128]{1,0:T(8,128)S(1)} collective-permute-done((f32[8,128]{1,0:T(8,128)S(1)}, f32[8,128]{1,0:T(8,128)S(1)}, u32[]{:S(2)}, u32[]{:S(2)}) %collective-permute-start.4) | collective-permute-done | bytes 4128 | tf_op jit(solution)/shard_map/ppermute | solution.py:327
  28.9 0.6 %finish.1 = (f32[1,32]{1,0:T(1,128)}, f32[32,128]{1,0:T(8,128)}) custom-call(f32[8,128]{1,0:T(8,128)S(1)} %own.1.refs_0_, f32[8,128]{1,0:T(8,128)S(1)} %collective-permute-done.4.refs_1_, f32[8,128]{1,0:T(8,128)S(1)} %collective-permute-done.5.refs_2_, f32[8,128]{1,0:T(8,128)S(1)} %collective-permute-done.6.refs_3_, ...), custom_call_target="tpu_custom_call" | custom-call | tf_op jit(solution)/shard_map/finish/pallas_call | solution.py:446
  (2 shorter events, 0.0 us)
Async XLA Ops:
  0.6 0.7 %copy-start.4 = (f32[11,32]{1,0:T(8,128)S(1)}, f32[11,32]{1,0:T(8,128)}, u32[]{:S(2)}) copy-start(f32[11,32]{1,0:T(8,128)} %f_ref.1) | copy-start | bytes 4228
  0.6 0.7 %copy-start.3 = (f32[11,32]{1,0:T(8,128)S(1)}, f32[11,32]{1,0:T(8,128)}, u32[]{:S(2)}) copy-start(f32[11,32]{1,0:T(8,128)} %x_ref.1) | copy-start | bytes 4228
  0.6 15.7 %collective-permute-start = (f32[4096,128]{1,0:T(8,128)}, f32[4096,128]{1,0:T(8,128)S(1)}, u32[]{:S(2)}, u32[]{:S(2)}) collective-permute-start(f32[4096,128]{1,0:T(8,128)} %refs_0_.1), channel_id=1, source_target_pairs={{0,1},{1,0},{2,3},{3,2},{4,5},{5,4},{6,7},{7,6},{8,9},{9,8},{10,11... | collective-permute-start | bytes 6291464 | tf_op jit(solution)/shard_map/ppermute | solution.py:321
  1.3 15.0 %copy-start = (f32[4096,128]{1,0:T(8,128)S(1)}, f32[4096,128]{1,0:T(8,128)}, u32[]{:S(2)}) copy-start(f32[4096,128]{1,0:T(8,128)} %refs_0_.1) | copy-start | bytes 6291460
  16.3 6.0 %copy-start.1 = (s32[16384]{0:T(1024)S(1)}, s32[16384]{0:T(1024)}, u32[]{:S(2)}) copy-start(s32[16384]{0:T(1024)} %param.9) | copy-start | bytes 196612
  16.3 6.0 %copy-start.2 = (f32[16384]{0:T(1024)S(1)}, f32[16384]{0:T(1024)}, u32[]{:S(2)}) copy-start(f32[16384]{0:T(1024)} %param.8) | copy-start | bytes 196612
  17.8 3.8 %collective-permute-start.2 = (f32[32,128]{1,0:T(8,128)S(1)}, f32[32,128]{1,0:T(8,128)S(1)}, u32[]{:S(2)}, u32[]{:S(2)}) collective-permute-start(f32[32,128]{1,0:T(8,128)S(1)} %get-tuple-element.15.own_ref), channel_id=1, source_target_pairs={{0,2},{1,5},{2,0},{3,7},{4,6},{5,1},{6,4},{7,3},{8,10},{9,13},{10,... | collective-permute-start | bytes 49160 | tf_op jit(solution)/shard_map/ppermute | solution.py:343
  18.5 3.8 %collective-permute-start.1 = (f32[32,128]{1,0:T(8,128)S(1)}, f32[32,128]{1,0:T(8,128)S(1)}, u32[]{:S(2)}, u32[]{:S(2)}) collective-permute-start(f32[32,128]{1,0:T(8,128)S(1)} %get-tuple-element.15.own_ref), channel_id=1, source_target_pairs={{0,2},{1,7},{2,0},{3,5},{4,6},{5,3},{6,4},{7,1},{8,10},{9,15},{10,... | collective-permute-start | bytes 49160 | tf_op jit(solution)/shard_map/ppermute | solution.py:342
  22.2 1.2 %collective-permute-start.3 = (f32[32,128]{1,0:T(8,128)S(1)}, f32[32,128]{1,0:T(8,128)S(1)}, u32[]{:S(2)}, u32[]{:S(2)}) collective-permute-start(f32[32,128]{1,0:T(8,128)S(1)} %merge.1.refs_0_), channel_id=1, source_target_pairs={{0,1},{1,0},{2,3},{3,2},{4,5},{5,4},{6,7},{7,6},{8,9},{9,8},{10,11... | collective-permute-start | bytes 49160 | tf_op jit(solution)/shard_map/ppermute | solution.py:321
  24.0 3.5 %collective-permute-start.6 = (f32[8,128]{1,0:T(8,128)S(1)}, f32[8,128]{1,0:T(8,128)S(1)}, u32[]{:S(2)}, u32[]{:S(2)}) collective-permute-start(f32[8,128]{1,0:T(8,128)S(1)} %get-tuple-element.23), channel_id=1, source_target_pairs={{0,17},{1,16},{2,19},{3,18},{4,21},{5,20},{6,23},{7,22},{8,25},{9,... | collective-permute-start | bytes 12296 | tf_op jit(solution)/shard_map/ppermute | solution.py:327
  24.4 3.9 %collective-permute-start.5 = (f32[8,128]{1,0:T(8,128)S(1)}, f32[8,128]{1,0:T(8,128)S(1)}, u32[]{:S(2)}, u32[]{:S(2)}) collective-permute-start(f32[8,128]{1,0:T(8,128)S(1)} %get-tuple-element.23), channel_id=1, source_target_pairs={{0,25},{1,24},{2,27},{3,26},{4,29},{5,28},{6,31},{7,30},{8,17},{9,... | collective-permute-start | bytes 12296 | tf_op jit(solution)/shard_map/ppermute | solution.py:327
  25.9 3.0 %collective-permute-start.4 = (f32[8,128]{1,0:T(8,128)S(1)}, f32[8,128]{1,0:T(8,128)S(1)}, u32[]{:S(2)}, u32[]{:S(2)}) collective-permute-start(f32[8,128]{1,0:T(8,128)S(1)} %get-tuple-element.23), channel_id=1, source_target_pairs={{0,9},{1,8},{2,11},{3,10},{4,13},{5,12},{6,15},{7,14},{8,1},{9,0},... | collective-permute-start | bytes 12296 | tf_op jit(solution)/shard_map/ppermute | solution.py:327

commit v9 on v8

--- a/solution.py
+++ b/solution.py
@@ -391,7 +391,7 @@
     received = lax.all_to_all(message, ("col", "row"), 0, 0, tiled=True)
 
     *halves, part, blended = pl.pallas_call(
-        functools.partial(image_kernel, hist, local, row_count, min(512, row_block)),
+        functools.partial(image_kernel, hist, local, row_count, min(256, row_block)),
         name="image",
         in_specs=[vmem()] * 3,
         out_specs=[vmem()] * 6,

time: 29.8 us -> 29.8 us (level)
  no operation moved by 1% of the time
where the time goes in v9:
time: 29.8 us; the launch traced here: 29.5 us
  blocking collectives  14.6 us (49%)
  starting transfers between devices  5.77 us (19%)
  waiting for transfers between devices  4.67 us (16%)
  Pallas kernels  3.62 us (12%)
  between operations  0.71 us (2%)
    all_to_all x1, blocking collectives, body(): received = lax.all_to_all(message, ('col', 'row'), 0, 0, tiled=True)  14.6 us
    ppermute x3, starting transfers between devices, exchange_rows(): lax.ppermute(x, ('row', 'col'), [(r * cols + c, (r ^ turn) * cols + (c ^...  3.04 us
    ppermute x1, waiting for transfers between devices, reduce_chips(): lax.ppermute(x, 'col', [(i, i ^ (2 * bit if i % 2 else bit)) for i in ran...  1.71 us
    pallas_call x1, Pallas kernels, body(): pl.pallas_call(functools.partial(image_kernel, hist, local, row_count, mi...  1.46 us
    ppermute x1, starting transfers between devices, reduce_chips(): lax.ppermute(x, 'col', [(i, i ^ (3 * bit if i % 2 else bit)) for i in ran...  1.42 us
    ppermute x3, waiting for transfers between devices, exchange_rows(): lax.ppermute(x, ('row', 'col'), [(r * cols + c, (r ^ turn) * cols + (c ^...  1.37 us
    ppermute x2, waiting for transfers between devices, exchange(): lax.ppermute(x, axis, [(i, i ^ turn) for i in range(count)])  0.96 us
    ppermute x1, starting transfers between devices, reduce_chips(): lax.ppermute(x, 'col', [(i, i ^ (2 * bit if i % 2 else bit)) for i in ran...  0.67 us
  transfers between devices with their start and end apart: 7, of which 5 were waited for; matrix products, arithmetic and copies ran while one was open for 0% of the time, Pallas kernels for 3%

profile of v9, /device:TPU:0, one launch (start us, length us, event | category | flops | bytes accessed | tf_op | source)
XLA Modules:
  0.0 29.5 jit_solution(2199902887376541333)
XLA Ops:
  0.6 0.0 copy-start.4
  0.6 0.0 copy-start.3
  0.6 0.6 %collective-permute-start = (f32[4096,128]{1,0:T(8,128)}, f32[4096,128]{1,0:T(8,128)S(1)}, u32[]{:S(2)}, u32[]{:S(2)}) collective-permute-start(f32[4096,128]{1,0:T(8,128)} %refs_0_.1), channel_id=1, source_target_pairs={{0,1},{1,0},{2,3},{3,2},{4,5},{5,4},{6,7},{7,6},{8,9},{9,8},{10,11... | collective-permute-start | bytes 6291464 | tf_op jit(solution)/shard_map/ppermute | solution.py:321
  1.2 0.1 copy-done.4
  1.3 0.0 copy-done.3
  1.3 0.0 copy-start
  1.3 0.3 %pack.1 = f32[128,128]{1,0:T(8,128)S(1)} custom-call(f32[8,128]{1,0:T(8,128)S(1)} %token_.1.token_ref, f32[11,32]{1,0:T(8,128)S(1)} %copy-done.3, f32[11,32]{1,0:T(8,128)S(1)} %copy-done.4), custom_call_target="tpu_custom_call" | custom-call | flops 10000000000 | bytes 40000000 | tf_op jit(solution)/shard_map/pack/pallas_call | solution.py:378
  1.7 14.6 %all_to_all.11 = f32[32,4,128]{2,1,0:T(4,128)S(1)} all-to-all(f32[32,4,128]{2,1,0:T(4,128)S(1)} %bitcast.7), channel_id=1, replica_groups=mesh['row'=4,'col'=8] {'col','row'}, dimensions={0} | all-to-all | bytes 131072 | tf_op jit(solution)/shard_map/all_to_all | solution.py:391
  16.3 0.0 collective-permute-done.refs_1_
  16.3 0.0 copy-done
  16.3 0.0 copy-start.1
  16.3 0.0 copy-start.2
  16.3 1.5 %image.1 = (bf16[4096,128]{1,0:T(8,128)(2,1)S(1)}, bf16[4096,128]{1,0:T(8,128)(2,1)S(1)}, bf16[4096,128]{1,0:T(8,128)(2,1)S(1)}, bf16[4096,128]{1,0:T(8,128)(2,1...) custom-call(f32[128,128]{1,0:T(8,128)S(1)} %bitcast.6, f32[4096,128]{1,0:T(8,128)S(1)} %copy-done, ...), custom_call_target="tpu_custom_call" | custom-call | tf_op jit(solution)/shard_map/image/pallas_call | solution.py:393
  17.8 0.7 %collective-permute-start.2 = (f32[32,128]{1,0:T(8,128)S(1)}, f32[32,128]{1,0:T(8,128)S(1)}, u32[]{:S(2)}, u32[]{:S(2)}) collective-permute-start(f32[32,128]{1,0:T(8,128)S(1)} %get-tuple-element.15.own_ref), channel_id=1, source_target_pairs={{0,2},{1,5},{2,0},{3,7},{4,6},{5,1},{6,4},{7,3},{8,10},{9,13},{10,... | collective-permute-start | bytes 49160 | tf_op jit(solution)/shard_map/ppermute | solution.py:343
  18.5 1.4 %collective-permute-start.1 = (f32[32,128]{1,0:T(8,128)S(1)}, f32[32,128]{1,0:T(8,128)S(1)}, u32[]{:S(2)}, u32[]{:S(2)}) collective-permute-start(f32[32,128]{1,0:T(8,128)S(1)} %get-tuple-element.15.own_ref), channel_id=1, source_target_pairs={{0,2},{1,7},{2,0},{3,5},{4,6},{5,3},{6,4},{7,1},{8,10},{9,15},{10,... | collective-permute-start | bytes 49160 | tf_op jit(solution)/shard_map/ppermute | solution.py:342
  19.9 1.7 %collective-permute-done.2.near_ref = f32[32,128]{1,0:T(8,128)S(1)} collective-permute-done((f32[32,128]{1,0:T(8,128)S(1)}, f32[32,128]{1,0:T(8,128)S(1)}, u32[]{:S(2)}, u32[]{:S(2)}) %collective-permute-start.2) | collective-permute-done | bytes 16416 | tf_op jit(solution)/shard_map/ppermute | solution.py:343
  21.6 0.6 %collective-permute-done.1.far_ref = f32[32,128]{1,0:T(8,128)S(1)} collective-permute-done((f32[32,128]{1,0:T(8,128)S(1)}, f32[32,128]{1,0:T(8,128)S(1)}, u32[]{:S(2)}, u32[]{:S(2)}) %collective-permute-start.1) | collective-permute-done | bytes 16416 | tf_op jit(solution)/shard_map/ppermute | solution.py:342
  22.2 0.1 collective-permute-start.3
  22.3 0.0 copy-done.1
  22.3 0.0 copy-done.2
  22.3 0.1 masks.1.refs_2_.refs_6_
  22.4 1.0 %collective-permute-done.3.refs_1_ = f32[32,128]{1,0:T(8,128)S(1)} collective-permute-done((f32[32,128]{1,0:T(8,128)S(1)}, f32[32,128]{1,0:T(8,128)S(1)}, u32[]{:S(2)}, u32[]{:S(2)}) %collective-permute-start.3) | collective-permute-done | bytes 16416 | tf_op jit(solution)/shard_map/ppermute | solution.py:321
  23.4 0.6 %cones.1 = (f32[32,128]{1,0:T(8,128)S(1)}, f32[8,128]{1,0:T(8,128)S(1)}, bf16[32,4096]{1,0:T(8,128)(2,1)S(1)}, f32[8,128]{1,0:T(8,128)S(1)}, f32[8,128]{1,0:T(8,128)S(1)}) custom-call(f32[32,128]{1,0:T(8,128)S(1)} %merge.1.refs_0_, f32[32,128]{1,0:T(8,128)S(1)} %collective-permute-done.3.refs_1_, f32[16,32,128]{2,1,0:T(8,128)S(1)} %masks.1.refs_2_.refs_6_, ...), custom_call_target="tpu_custom_call" | custom-call | tf_op jit(solution)/shard_map/cones/pallas_call | solution.py:421
  24.0 0.4 %collective-permute-start.6 = (f32[8,128]{1,0:T(8,128)S(1)}, f32[8,128]{1,0:T(8,128)S(1)}, u32[]{:S(2)}, u32[]{:S(2)}) collective-permute-start(f32[8,128]{1,0:T(8,128)S(1)} %get-tuple-element.23), channel_id=1, source_target_pairs={{0,17},{1,16},{2,19},{3,18},{4,21},{5,20},{6,23},{7,22},{8,25},{9,... | collective-permute-start | bytes 12296 | tf_op jit(solution)/shard_map/ppermute | solution.py:327
  24.4 1.5 %collective-permute-start.5 = (f32[8,128]{1,0:T(8,128)S(1)}, f32[8,128]{1,0:T(8,128)S(1)}, u32[]{:S(2)}, u32[]{:S(2)}) collective-permute-start(f32[8,128]{1,0:T(8,128)S(1)} %get-tuple-element.23), channel_id=1, source_target_pairs={{0,25},{1,24},{2,27},{3,26},{4,29},{5,28},{6,31},{7,30},{8,17},{9,... | collective-permute-start | bytes 12296 | tf_op jit(solution)/shard_map/ppermute | solution.py:327
  25.9 1.2 %collective-permute-start.4 = (f32[8,128]{1,0:T(8,128)S(1)}, f32[8,128]{1,0:T(8,128)S(1)}, u32[]{:S(2)}, u32[]{:S(2)}) collective-permute-start(f32[8,128]{1,0:T(8,128)S(1)} %get-tuple-element.23), channel_id=1, source_target_pairs={{0,9},{1,8},{2,11},{3,10},{4,13},{5,12},{6,15},{7,14},{8,1},{9,0},... | collective-permute-start | bytes 12296 | tf_op jit(solution)/shard_map/ppermute | solution.py:327
  27.0 0.5 %own.1.refs_0_ = f32[8,128]{1,0:T(8,128)S(1)} custom-call(bf16[32,4096]{1,0:T(8,128)(2,1)S(1)} %get-tuple-element.19.left_ref, bf16[4096,128]{1,0:T(8,128)(2,1)S(1)} %get-tuple-element.20.high_ref, bf16[4096,128]{1,0:T(8,128)(2,1)S(1)} %get-tuple-element.21.low_ref, f32[8,128]{1,0:T(8,128)S(1)} %get-tuple-element.22.scalar_ref), custom_call_target="tpu_custom_call" | custom-call | tf_op jit(solution)/shard_map/own/pallas_call | solution.py:435
  27.5 0.0 collective-permute-done.6.refs_3_
  27.5 0.8 %collective-permute-done.5.refs_2_ = f32[8,128]{1,0:T(8,128)S(1)} collective-permute-done((f32[8,128]{1,0:T(8,128)S(1)}, f32[8,128]{1,0:T(8,128)S(1)}, u32[]{:S(2)}, u32[]{:S(2)}) %collective-permute-start.5) | collective-permute-done | bytes 4128 | tf_op jit(solution)/shard_map/ppermute | solution.py:327
  28.3 0.6 %collective-permute-done.4.refs_1_ = f32[8,128]{1,0:T(8,128)S(1)} collective-permute-done((f32[8,128]{1,0:T(8,128)S(1)}, f32[8,128]{1,0:T(8,128)S(1)}, u32[]{:S(2)}, u32[]{:S(2)}) %collective-permute-start.4) | collective-permute-done | bytes 4128 | tf_op jit(solution)/shard_map/ppermute | solution.py:327
  28.9 0.6 %finish.1 = (f32[1,32]{1,0:T(1,128)}, f32[32,128]{1,0:T(8,128)}) custom-call(f32[8,128]{1,0:T(8,128)S(1)} %own.1.refs_0_, f32[8,128]{1,0:T(8,128)S(1)} %collective-permute-done.4.refs_1_, f32[8,128]{1,0:T(8,128)S(1)} %collective-permute-done.5.refs_2_, f32[8,128]{1,0:T(8,128)S(1)} %collective-permute-done.6.refs_3_, ...), custom_call_target="tpu_custom_call" | custom-call | tf_op jit(solution)/shard_map/finish/pallas_call | solution.py:446
  (2 shorter events, 0.0 us)
Async XLA Ops:
  0.6 0.7 %copy-start.4 = (f32[11,32]{1,0:T(8,128)S(1)}, f32[11,32]{1,0:T(8,128)}, u32[]{:S(2)}) copy-start(f32[11,32]{1,0:T(8,128)} %f_ref.1) | copy-start | bytes 4228
  0.6 0.7 %copy-start.3 = (f32[11,32]{1,0:T(8,128)S(1)}, f32[11,32]{1,0:T(8,128)}, u32[]{:S(2)}) copy-start(f32[11,32]{1,0:T(8,128)} %x_ref.1) | copy-start | bytes 4228
  0.6 15.7 %collective-permute-start = (f32[4096,128]{1,0:T(8,128)}, f32[4096,128]{1,0:T(8,128)S(1)}, u32[]{:S(2)}, u32[]{:S(2)}) collective-permute-start(f32[4096,128]{1,0:T(8,128)} %refs_0_.1), channel_id=1, source_target_pairs={{0,1},{1,0},{2,3},{3,2},{4,5},{5,4},{6,7},{7,6},{8,9},{9,8},{10,11... | collective-permute-start | bytes 6291464 | tf_op jit(solution)/shard_map/ppermute | solution.py:321
  1.3 15.0 %copy-start = (f32[4096,128]{1,0:T(8,128)S(1)}, f32[4096,128]{1,0:T(8,128)}, u32[]{:S(2)}) copy-start(f32[4096,128]{1,0:T(8,128)} %refs_0_.1) | copy-start | bytes 6291460
  16.3 6.0 %copy-start.1 = (s32[16384]{0:T(1024)S(1)}, s32[16384]{0:T(1024)}, u32[]{:S(2)}) copy-start(s32[16384]{0:T(1024)} %param.9) | copy-start | bytes 196612
  16.3 6.0 %copy-start.2 = (f32[16384]{0:T(1024)S(1)}, f32[16384]{0:T(1024)}, u32[]{:S(2)}) copy-start(f32[16384]{0:T(1024)} %param.8) | copy-start | bytes 196612
  17.8 3.8 %collective-permute-start.2 = (f32[32,128]{1,0:T(8,128)S(1)}, f32[32,128]{1,0:T(8,128)S(1)}, u32[]{:S(2)}, u32[]{:S(2)}) collective-permute-start(f32[32,128]{1,0:T(8,128)S(1)} %get-tuple-element.15.own_ref), channel_id=1, source_target_pairs={{0,2},{1,5},{2,0},{3,7},{4,6},{5,1},{6,4},{7,3},{8,10},{9,13},{10,... | collective-permute-start | bytes 49160 | tf_op jit(solution)/shard_map/ppermute | solution.py:343
  18.5 3.8 %collective-permute-start.1 = (f32[32,128]{1,0:T(8,128)S(1)}, f32[32,128]{1,0:T(8,128)S(1)}, u32[]{:S(2)}, u32[]{:S(2)}) collective-permute-start(f32[32,128]{1,0:T(8,128)S(1)} %get-tuple-element.15.own_ref), channel_id=1, source_target_pairs={{0,2},{1,7},{2,0},{3,5},{4,6},{5,3},{6,4},{7,1},{8,10},{9,15},{10,... | collective-permute-start | bytes 49160 | tf_op jit(solution)/shard_map/ppermute | solution.py:342
  22.2 1.2 %collective-permute-start.3 = (f32[32,128]{1,0:T(8,128)S(1)}, f32[32,128]{1,0:T(8,128)S(1)}, u32[]{:S(2)}, u32[]{:S(2)}) collective-permute-start(f32[32,128]{1,0:T(8,128)S(1)} %merge.1.refs_0_), channel_id=1, source_target_pairs={{0,1},{1,0},{2,3},{3,2},{4,5},{5,4},{6,7},{7,6},{8,9},{9,8},{10,11... | collective-permute-start | bytes 49160 | tf_op jit(solution)/shard_map/ppermute | solution.py:321
  24.0 3.5 %collective-permute-start.6 = (f32[8,128]{1,0:T(8,128)S(1)}, f32[8,128]{1,0:T(8,128)S(1)}, u32[]{:S(2)}, u32[]{:S(2)}) collective-permute-start(f32[8,128]{1,0:T(8,128)S(1)} %get-tuple-element.23), channel_id=1, source_target_pairs={{0,17},{1,16},{2,19},{3,18},{4,21},{5,20},{6,23},{7,22},{8,25},{9,... | collective-permute-start | bytes 12296 | tf_op jit(solution)/shard_map/ppermute | solution.py:327
  24.4 3.9 %collective-permute-start.5 = (f32[8,128]{1,0:T(8,128)S(1)}, f32[8,128]{1,0:T(8,128)S(1)}, u32[]{:S(2)}, u32[]{:S(2)}) collective-permute-start(f32[8,128]{1,0:T(8,128)S(1)} %get-tuple-element.23), channel_id=1, source_target_pairs={{0,25},{1,24},{2,27},{3,26},{4,29},{5,28},{6,31},{7,30},{8,17},{9,... | collective-permute-start | bytes 12296 | tf_op jit(solution)/shard_map/ppermute | solution.py:327
  25.9 3.0 %collective-permute-start.4 = (f32[8,128]{1,0:T(8,128)S(1)}, f32[8,128]{1,0:T(8,128)S(1)}, u32[]{:S(2)}, u32[]{:S(2)}) collective-permute-start(f32[8,128]{1,0:T(8,128)S(1)} %get-tuple-element.23), channel_id=1, source_target_pairs={{0,9},{1,8},{2,11},{3,10},{4,13},{5,12},{6,15},{7,14},{8,1},{9,0},... | collective-permute-start | bytes 12296 | tf_op jit(solution)/shard_map/ppermute | solution.py:327
